TPU v7x, 256 devices: a whole 4x4x8 slice. The times are simulated.
256 devices in a mesh: gx: 8 (over z), gy: 32 (over x, y, core).
Axes of the slice: x: 4, y: 4, z: 8, core: 2. Of those that a mesh axis runs over, the one named last changes fastest.
Arguments:
- blocks: bfloat16 [2048, 8, 256, 256], P(('gx', 'gy')), may hold values from -0.1875 to 0.1875
- block_cols: int32 [2048, 8], P(('gx', 'gy')), may hold values from 0 to 23, as said below
- live_blocks: int32 [2048], P(('gx', 'gy')), may hold values from 1 to 8
- send_rows: int32 [256, 4, 4], P(('gx', 'gy')), may hold values from 0 to 7, as said below
- start: float32 [2048, 64, 256], P(('gx', 'gy')), may hold values from -6 to 6
- sketch: float32 [64, 2048, 256], P(None, ('gx', 'gy')), may hold values from -0.0009765625 to 0.0009765625
Outputs:
- basis: float32 [4, 2048, 64, 256], P(None, ('gx', 'gy'))
- factor: float32 [4, 4, 64], replicated
Inputs may be any that keep to these rules, and one draw needn't show every extreme that they name: block_cols[i, 0] is block row i itself (i % 8 in the owner's numbering); only the first live_blocks[i] entries of a row are used. `send_rows`: the 4 entries of one device and direction are distinct.
All inputs are finite; a program needn't handle non-finite values.
Results may differ from a plain program's by a relative error of at most 0.0036.
Values may be sent and summed in bfloat16 or wider, within the bound.
No kernel may reach another device: no remote copies, remote signals or barrier semaphores. Data moves between devices by JAX's collectives and lax.ppermute only.
A program may use at most 64 MiB of HBM per device.

v0:
```python
import jax
import jax.numpy as jnp
from jax import lax
from jax.sharding import Mesh
from jax.sharding import PartitionSpec as P

STEPS = 3
GY = ("gy_0", "gy_1", "gy_2")
GX_GY = ("gx", "gy_0", "gy_1", "gy_2")


def with_halo(block, sides, width):
    for axis, dim in sides:
        count = lax.axis_size(axis)
        forward = [(i, i + 1) for i in range(count - 1)]
        forward.append((count - 1, 0))
        backward = [(target, source) for source, target in forward]
        low = lax.ppermute(
            lax.slice_in_dim(block, block.shape[dim] - width, None, axis=dim), axis, forward
        )
        high = lax.ppermute(lax.slice_in_dim(block, 0, width, axis=dim), axis, backward)
        block = jnp.concatenate([low, block, high], axis=dim)
    return block


def in_blocks(x, dim, devices):
    lengths = x.shape
    pieces = x.reshape(*lengths[:dim], devices, lengths[dim] // devices, *lengths[dim + 1 :])
    return jnp.moveaxis(pieces, dim, 0)


def sent_and_summed(x, axis, dim):
    devices = lax.axis_size(axis)
    pieces = lax.all_to_all(in_blocks(x, dim, devices), axis, 0, 0, tiled=True)
    return jnp.sum(pieces, axis=0)


def sum_by_axis(x, axes, dim):
    far, near = axes
    own = sent_and_summed(in_blocks(x, dim, lax.axis_size(far)), near, dim + 1)
    return jnp.sum(lax.all_to_all(own, far, 0, 0, tiled=True), axis=0)


def rows_for(lines, devices):
    spare = -lines.shape[0] % devices
    if not spare:
        return lines
    return jnp.concatenate([lines, jnp.zeros((spare, *lines.shape[1:]), lines.dtype)])


def copy_for_each(x, axis):
    devices = lax.axis_size(axis)
    return lax.all_to_all(jnp.broadcast_to(x[None], (devices, *x.shape)), axis, 0, 0, tiled=True)


def joined_along(pieces, dim):
    pieces = jnp.moveaxis(pieces, 0, dim)
    lengths = pieces.shape
    return pieces.reshape(*lengths[:dim], lengths[dim] * lengths[dim + 1], *lengths[dim + 2 :])


def gathered_by_axis(x, axes, dim):
    far, near = axes
    first = copy_for_each(x, far)
    pieces = jnp.swapaxes(copy_for_each(first, near), 0, 1)
    return joined_along(pieces.reshape(-1, *x.shape), dim)


def sum_by_parts(x, axes):
    lines = x.reshape(-1, x.shape[-1])
    own = sum_by_axis(rows_for(lines, lax.axis_size(axes[0]) * lax.axis_size(axes[1])), axes, 0)
    whole = gathered_by_axis(own, axes, 0)
    return whole[: len(lines)].reshape(x.shape)


def orthogonalize(sketched):
    count = sketched.shape[0]
    columns = []
    factor = jnp.zeros((count, count, sketched.shape[2]), jnp.float32)
    for column in range(count):
        residue = sketched[column]
        for earlier in range(column):
            coefficient = jnp.sum(columns[earlier] * sketched[column], axis=0)
            factor = factor.at[earlier, column].set(coefficient)
            residue = residue - coefficient[None, :] * columns[earlier]
        length = jnp.sqrt(jnp.sum(residue * residue, axis=0) + 1e-06)
        factor = factor.at[column, column].set(length)
        columns.append(residue / length[None, :])
    return factor


def sketch_local(sketch, vectors):
    return jnp.einsum("sib,irb->sr", sketch, vectors, precision=lax.Precision.HIGHEST)


def on_device(blocks, block_cols, live_blocks, send_rows, start, sketch):
    lists = send_rows[0]
    send_count = lists.shape[1]
    slot_count = block_cols.shape[1]
    weights = (jnp.arange(slot_count, dtype=jnp.int32)[None, :] < live_blocks[:, None]).astype(
        jnp.bfloat16
    )
    vectors = [start]
    for section in range(STEPS):
        rounded = vectors[-1].astype(jnp.bfloat16)
        outgoing_y = jnp.concatenate([rounded[lists[1]], rounded[lists[0]]], axis=0)
        outgoing_x = jnp.concatenate([rounded[lists[3]], rounded[lists[2]]], axis=0)
        around_y = with_halo(outgoing_y, ((GY, 0),), send_count)
        around_x = with_halo(outgoing_x, (("gx", 0),), send_count)
        from_left_y = around_y[:send_count]
        from_right_y = around_y[3 * send_count :]
        from_left_x = around_x[:send_count]
        from_right_x = around_x[3 * send_count :]
        extended = jnp.concatenate(
            [rounded, from_left_y, from_right_y, from_left_x, from_right_x], axis=0
        )
        picked = extended[block_cols] * weights[:, :, None, None]
        product = jnp.einsum("ikrb,ikbc->irc", picked, blocks, preferred_element_type=jnp.float32)
        vectors.append(product)
    partial_sketch = jnp.stack([sketch_local(sketch, vector) for vector in vectors])
    sketched = sum_by_parts(partial_sketch, (("gx", "gy_0"), ("gy_1", "gy_2")))
    factor = orthogonalize(sketched)
    result = []
    for column in range(STEPS + 1):
        accum = vectors[column]
        for earlier in range(column):
            accum = accum - factor[earlier, column][None, :, None] * result[earlier]
        result.append(accum / factor[column, column][None, :, None])
    return (jnp.stack(result), factor)


def solution(mesh):
    split = Mesh(mesh.devices.reshape(mesh.shape["gx"], 4, 4, 2), ("gx", "gy_0", "gy_1", "gy_2"))
    return jax.shard_map(
        on_device,
        mesh=split,
        in_specs=(
            P(GX_GY, None, None, None),
            P(GX_GY, None),
            P(GX_GY),
            P(GX_GY, None, None),
            P(GX_GY, None, None),
            P(None, GX_GY, None),
        ),
        out_specs=(P(None, GX_GY, None, None), P()),
        check_vma=False,
    )
```

profile of v0, /device:TPU:8, one launch (start us, length us, event | category | flops | bytes accessed | tf_op | source)
XLA Modules:
  0.0 136.8 jit_solution(11208237600458600972)
XLA Ops:
  3.8 1.8 %collective-permute-start.1 = (bf16[4,64,256]{2,1,0:T(8,128)(2,1)S(1)}, bf16[4,64,256]{2,1,0:T(8,128)(2,1)S(1)}, u32[]{:S(2)}, u32[]{:S(2)}) collective-permute-start(bf16[4,64,256]{2,1,0:T(8,128)(2,1)S(1)} %gather_fusion.1), channel_id=1, source_target_pairs={{1,0},{2,1},{3,2},{4,3},{5,4},{6,5},{7,6},{8,7},{9,8},{10,9},{11,1... | collective-permute-start | bytes 393224 | tf_op jit(solution)/shard_map/ppermute | solution.py:21
  6.2 2.0 %collective-permute-start.2 = (bf16[4,64,256]{2,1,0:T(8,128)(2,1)S(1)}, bf16[4,64,256]{2,1,0:T(8,128)(2,1)S(1)}, u32[]{:S(2)}, u32[]{:S(2)}) collective-permute-start(bf16[4,64,256]{2,1,0:T(8,128)(2,1)S(1)} %gather_fusion.2), channel_id=1, source_target_pairs={{0,32},{32,64},{64,96},{96,128},{128,160},{160,192},{192,224},{224... | collective-permute-start | bytes 393224 | tf_op jit(solution)/shard_map/ppermute | solution.py:18
  8.8 4.0 %collective-permute-start.3 = (bf16[4,64,256]{2,1,0:T(8,128)(2,1)S(1)}, bf16[4,64,256]{2,1,0:T(8,128)(2,1)S(1)}, u32[]{:S(2)}, u32[]{:S(2)}) collective-permute-start(bf16[4,64,256]{2,1,0:T(8,128)(2,1)S(1)} %gather_fusion.3), channel_id=1, source_target_pairs={{32,0},{64,32},{96,64},{128,96},{160,128},{192,160},{224,192},{0,2... | collective-permute-start | bytes 393224 | tf_op jit(solution)/shard_map/ppermute | solution.py:21
  13.7 2.0 %collective-permute-done.2 = bf16[4,64,256]{2,1,0:T(8,128)(2,1)S(1)} collective-permute-done((bf16[4,64,256]{2,1,0:T(8,128)(2,1)S(1)}, bf16[4,64,256]{2,1,0:T(8,128)(2,1)S(1)}, u32[]{:S(2)}, u32[]{:S(2)}) %collective-permute-start.2) | collective-permute-done | bytes 131104 | tf_op jit(solution)/shard_map/ppermute | solution.py:18
  16.5 5.9 %constant_dynamic-update-slice_fusion.9 = (bf16[24,64,256]{2,1,0:T(8,128)(2,1)S(1)}, bf16[8,64,256]{2,1,0:T(8,128)(2,1)}, f32[8,64,256]{2,1,0:T(8,128)}) fusion(bf16[8,8,256,256]{3,2,1,0:T(8,128)(2,1)} %param.26, bf16[8,8,64,256]{3,2,1,0:T(8,128)(2,1)S(1)} %bitcast.121, bf16[8,8]{1,0:T(8,128)(2,1)S(1)} %fusion.22), kind=kOutput, calls=%fused_computation.65 | convolution fusion | flops 538050560 | bytes 11534464 | tf_op jit(solution)/shard_map/ikrb,ikbc->irc/dot_general | solution.py:118
  22.4 1.5 %gather_fusion.5 = bf16[4,64,256]{2,1,0:T(8,128)(2,1)S(1)} fusion(bf16[8,64,256]{2,1,0:T(8,128)(2,1)} %get-tuple-element.133, s32[1024]{0:T(1024)S(1)} %pad_clamp_fusion.4), kind=kCustom, calls=%fused_computation.5 | custom fusion | bytes 262160 | tf_op jit(solution)/shard_map/gather | solution.py:106
  23.9 1.5 %gather_fusion.6 = bf16[4,64,256]{2,1,0:T(8,128)(2,1)S(1)} fusion(bf16[8,64,256]{2,1,0:T(8,128)(2,1)} %get-tuple-element.133, s32[1024]{0:T(1024)S(1)} %pad_clamp_fusion.3), kind=kCustom, calls=%fused_computation.6 | custom fusion | bytes 262160 | tf_op jit(solution)/shard_map/gather | solution.py:106
  25.4 1.5 %gather_fusion.7 = bf16[4,64,256]{2,1,0:T(8,128)(2,1)S(1)} fusion(bf16[8,64,256]{2,1,0:T(8,128)(2,1)} %get-tuple-element.133, s32[1024]{0:T(1024)S(1)} %pad_clamp_fusion.2), kind=kCustom, calls=%fused_computation.7 | custom fusion | bytes 262160 | tf_op jit(solution)/shard_map/gather | solution.py:107
  26.9 1.5 %gather_fusion.8 = bf16[4,64,256]{2,1,0:T(8,128)(2,1)S(1)} fusion(bf16[8,64,256]{2,1,0:T(8,128)(2,1)} %get-tuple-element.133, s32[1024]{0:T(1024)S(1)} %pad_clamp_fusion.1), kind=kCustom, calls=%fused_computation.8 | custom fusion | bytes 262160 | tf_op jit(solution)/shard_map/gather | solution.py:107
  28.5 1.7 %collective-permute-start.5 = (bf16[4,64,256]{2,1,0:T(8,128)(2,1)S(1)}, bf16[4,64,256]{2,1,0:T(8,128)(2,1)S(1)}, u32[]{:S(2)}, u32[]{:S(2)}) collective-permute-start(bf16[4,64,256]{2,1,0:T(8,128)(2,1)S(1)} %gather_fusion.6), channel_id=1, source_target_pairs={{1,0},{2,1},{3,2},{4,3},{5,4},{6,5},{7,6},{8,7},{9,8},{10,9},{11,1... | collective-permute-start | bytes 393224 | tf_op jit(solution)/shard_map/ppermute | solution.py:21
  30.5 3.4 %collective-permute-start.7 = (bf16[4,64,256]{2,1,0:T(8,128)(2,1)S(1)}, bf16[4,64,256]{2,1,0:T(8,128)(2,1)S(1)}, u32[]{:S(2)}, u32[]{:S(2)}) collective-permute-start(bf16[4,64,256]{2,1,0:T(8,128)(2,1)S(1)} %gather_fusion.8), channel_id=1, source_target_pairs={{32,0},{64,32},{96,64},{128,96},{160,128},{192,160},{224,192},{0,2... | collective-permute-start | bytes 393224 | tf_op jit(solution)/shard_map/ppermute | solution.py:21
  33.8 1.7 %convolution_bitcast_fusion.2 = f32[1,64,64]{2,1,0:T(8,128)S(1)} fusion(f32[8,64,256]{2,1,0:T(8,128)} %get-tuple-element.167, f32[64,8,256]{2,1,0:T(8,128)S(1)} %copy-done), kind=kOutput, calls=%fused_computation.27 | convolution fusion | flops 100663296 | bytes 1064960 | tf_op jit(solution)/shard_map/sib,irb->sr/dot_general | solution.py:93
  35.6 1.5 %collective-permute-done.6 = bf16[4,64,256]{2,1,0:T(8,128)(2,1)S(1)} collective-permute-done((bf16[4,64,256]{2,1,0:T(8,128)(2,1)S(1)}, bf16[4,64,256]{2,1,0:T(8,128)(2,1)S(1)}, u32[]{:S(2)}, u32[]{:S(2)}) %collective-permute-start.6) | collective-permute-done | bytes 131104 | tf_op jit(solution)/shard_map/ppermute | solution.py:18
  37.9 5.9 %constant_dynamic-update-slice_fusion.14 = (bf16[24,64,256]{2,1,0:T(8,128)(2,1)S(1)}, bf16[8,64,256]{2,1,0:T(8,128)(2,1)}, f32[8,64,256]{2,1,0:T(8,128)}) fusion(bf16[8,8,256,256]{3,2,1,0:T(8,128)(2,1)} %param.26, bf16[8,8,64,256]{3,2,1,0:T(8,128)(2,1)S(1)} %bitcast.122, bf16[8,8]{1,0:T(8,128)(2,1)S(1)} %fusion.22), kind=kOutput, calls=%fused_computation.70 | convolution fusion | flops 538050560 | bytes 11534464 | tf_op jit(solution)/shard_map/ikrb,ikbc->irc/dot_general | solution.py:118
  43.8 1.5 %gather_fusion.10 = bf16[4,64,256]{2,1,0:T(8,128)(2,1)S(1)} fusion(bf16[8,64,256]{2,1,0:T(8,128)(2,1)} %get-tuple-element.131, s32[1024]{0:T(1024)S(1)} %pad_clamp_fusion.4), kind=kCustom, calls=%fused_computation.10 | custom fusion | bytes 262160 | tf_op jit(solution)/shard_map/gather | solution.py:106
  45.3 1.5 %gather_fusion.11 = bf16[4,64,256]{2,1,0:T(8,128)(2,1)S(1)} fusion(bf16[8,64,256]{2,1,0:T(8,128)(2,1)} %get-tuple-element.131, s32[1024]{0:T(1024)S(1)} %pad_clamp_fusion.3), kind=kCustom, calls=%fused_computation.11 | custom fusion | bytes 262160 | tf_op jit(solution)/shard_map/gather | solution.py:106
  46.8 1.5 %gather_fusion.12 = bf16[4,64,256]{2,1,0:T(8,128)(2,1)S(1)} fusion(bf16[8,64,256]{2,1,0:T(8,128)(2,1)} %get-tuple-element.131, s32[1024]{0:T(1024)S(1)} %pad_clamp_fusion.2), kind=kCustom, calls=%fused_computation.12 | custom fusion | bytes 262160 | tf_op jit(solution)/shard_map/gather | solution.py:107
  48.3 1.5 %gather_fusion.13 = bf16[4,64,256]{2,1,0:T(8,128)(2,1)S(1)} fusion(bf16[8,64,256]{2,1,0:T(8,128)(2,1)} %get-tuple-element.131, s32[1024]{0:T(1024)S(1)} %pad_clamp_fusion.1), kind=kCustom, calls=%fused_computation.13 | custom fusion | bytes 262160 | tf_op jit(solution)/shard_map/gather | solution.py:107
  49.9 1.7 %collective-permute-start.9 = (bf16[4,64,256]{2,1,0:T(8,128)(2,1)S(1)}, bf16[4,64,256]{2,1,0:T(8,128)(2,1)S(1)}, u32[]{:S(2)}, u32[]{:S(2)}) collective-permute-start(bf16[4,64,256]{2,1,0:T(8,128)(2,1)S(1)} %gather_fusion.11), channel_id=1, source_target_pairs={{1,0},{2,1},{3,2},{4,3},{5,4},{6,5},{7,6},{8,7},{9,8},{10,9},{11,1... | collective-permute-start | bytes 393224 | tf_op jit(solution)/shard_map/ppermute | solution.py:21
  51.6 2.6 %collective-permute-start.10 = (bf16[4,64,256]{2,1,0:T(8,128)(2,1)S(1)}, bf16[4,64,256]{2,1,0:T(8,128)(2,1)S(1)}, u32[]{:S(2)}, u32[]{:S(2)}) collective-permute-start(bf16[4,64,256]{2,1,0:T(8,128)(2,1)S(1)} %gather_fusion.12), channel_id=1, source_target_pairs={{0,32},{32,64},{64,96},{96,128},{128,160},{160,192},{192,224},{224... | collective-permute-start | bytes 393224 | tf_op jit(solution)/shard_map/ppermute | solution.py:18
  54.9 1.7 %convolution_bitcast_fusion.1 = f32[1,64,64]{2,1,0:T(8,128)S(1)} fusion(f32[8,64,256]{2,1,0:T(8,128)} %get-tuple-element.168, f32[64,8,256]{2,1,0:T(8,128)S(1)} %copy-done), kind=kOutput, calls=%fused_computation.26 | convolution fusion | flops 100663296 | bytes 1064960 | tf_op jit(solution)/shard_map/sib,irb->sr/dot_general | solution.py:93
  59.9 5.0 %fusion.12 = f32[8,64,256]{2,1,0:T(8,128)S(1)} fusion(bf16[8,8,256,256]{3,2,1,0:T(8,128)(2,1)} %param.26, bf16[8,8,64,256]{3,2,1,0:T(8,128)(2,1)S(1)} %bitcast.120, bf16[8,8]{1,0:T(8,128)(2,1)S(1)} %fusion.22), kind=kOutput, calls=%fused_computation.24 | convolution fusion | flops 537919488 | bytes 11010176 | tf_op jit(solution)/shard_map/ikrb,ikbc->irc/dot_general | solution.py:118
  66.4 13.3 %all-to-all-start = ((f32[8,1,2048]{2,1,0:T(1,128)}), f32[8,1,2048]{2,1,0:T(1,128)S(1)}, u32[]{:S(2)}, u32[]{:S(2)}) async-start(f32[8,1,2048]{2,1,0:T(1,128)} %reshape.854), calls=%async_computation | async-start | bytes 131072 | tf_op jit(solution)/shard_map/all_to_all | solution.py:34
  80.5 3.4 %all-to-all-done = f32[8,1,2048]{2,1,0:T(1,128)S(1)} async-done(((f32[8,1,2048]{2,1,0:T(1,128)}), f32[8,1,2048]{2,1,0:T(1,128)S(1)}, u32[]{:S(2)}, u32[]{:S(2)}) %all-to-all-start) | async-done | bytes 65568 | tf_op jit(solution)/shard_map/all_to_all | solution.py:34
  85.9 5.0 %all-to-all-start.1 = ((f32[32,1,64]{2,1,0:T(1,128)}), f32[32,1,64]{2,1,0:T(1,128)S(1)}, u32[]{:S(2)}, u32[]{:S(2)}) async-start(f32[32,1,64]{2,1,0:T(1,128)} %bitcast.30), calls=%async_computation.1 | async-start | bytes 32768 | tf_op jit(solution)/shard_map/all_to_all | solution.py:41
  91.6 9.1 %all-to-all-done.1 = f32[32,1,64]{2,1,0:T(1,128)S(1)} async-done(((f32[32,1,64]{2,1,0:T(1,128)}), f32[32,1,64]{2,1,0:T(1,128)S(1)}, u32[]{:S(2)}, u32[]{:S(2)}) %all-to-all-start.1) | async-done | bytes 8224 | tf_op jit(solution)/shard_map/all_to_all | solution.py:41
  101.3 3.9 %all-to-all-start.2 = ((f32[32,1,64]{2,1,0:T(1,128)}), f32[32,1,64]{2,1,0:T(1,128)S(1)}, u32[]{:S(2)}, u32[]{:S(2)}) async-start(f32[32,1,64]{2,1,0:T(1,128)} %broadcast_in_dim.9), calls=%async_computation.2 | async-start | bytes 32768 | tf_op jit(solution)/shard_map/all_to_all | solution.py:53
  105.8 9.2 %all-to-all-done.2 = f32[32,1,64]{2,1,0:T(1,128)S(1)} async-done(((f32[32,1,64]{2,1,0:T(1,128)}), f32[32,1,64]{2,1,0:T(1,128)S(1)}, u32[]{:S(2)}, u32[]{:S(2)}) %all-to-all-start.2) | async-done | bytes 8224 | tf_op jit(solution)/shard_map/all_to_all | solution.py:53
  116.7 4.7 %all-to-all-start.3 = ((f32[8,1,2048]{2,1,0:T(1,128)}), f32[8,1,2048]{2,1,0:T(1,128)S(1)}, u32[]{:S(2)}, u32[]{:S(2)}) async-start(f32[8,1,2048]{2,1,0:T(1,128)} %reshape.856), calls=%async_computation.3 | async-start | bytes 131072 | tf_op jit(solution)/shard_map/all_to_all | solution.py:53
  122.1 3.6 %all-to-all-done.3 = f32[8,1,2048]{2,1,0:T(1,128)S(1)} async-done(((f32[8,1,2048]{2,1,0:T(1,128)}), f32[8,1,2048]{2,1,0:T(1,128)S(1)}, u32[]{:S(2)}, u32[]{:S(2)}) %all-to-all-start.3) | async-done | bytes 65568 | tf_op jit(solution)/shard_map/all_to_all | solution.py:53
  128.3 1.9 %broadcast_select_fusion.1 = f32[1,1,64]{2,1,0:T(1,128)S(1)} fusion(pred[]{:T(512)} %get-tuple-element.127, f32[64]{0:T(128)S(1)} %get-tuple-element.125, f32[4,4,64]{2,1,0:T(4,128)S(1)} %scatter.36, s32[]{:T(128)} %bitcast.39, s32[]{:T(128)} %bitcast.40), kind=kLoop, calls=%fused_computation.88 | loop fusion | flops 64 | bytes 777 | tf_op jit(solution)/shard_map/select.13
  131.6 1.8 %broadcast_select_fusion = f32[1,1,64]{2,1,0:T(1,128)S(1)} fusion(pred[]{:T(512)} %get-tuple-element.126, f32[64]{0:T(128)S(1)} %get-tuple-element.124, f32[4,4,64]{2,1,0:T(4,128)S(1)} %scatter.41, s32[]{:T(128)} %bitcast.44, s32[]{:T(128)} %bitcast.45), kind=kLoop, calls=%fused_computation.87 | loop fusion | flops 64 | bytes 777 | tf_op jit(solution)/shard_map/select.16
  (109 shorter events, 26.8 us)
Async XLA Ops:
  0.6 12.3 %copy-start.1 = (f32[8,64,256]{2,1,0:T(8,128)S(1)}, f32[8,64,256]{2,1,0:T(8,128)}, u32[]{:S(2)}) copy-start(f32[8,64,256]{2,1,0:T(8,128)} %param.30) | copy-start | bytes 1572868
  0.6 12.2 %copy-start.6 = (s32[8,8]{1,0:T(8,128)S(1)}, s32[8,8]{1,0:T(8,128)}, u32[]{:S(2)}) copy-start(s32[8,8]{1,0:T(8,128)} %param.27) | copy-start | bytes 772
  0.7 12.3 %copy-start.7 = (s32[8]{0:T(128)S(1)}, s32[8]{0:T(128)}, u32[]{:S(2)}) copy-start(s32[8]{0:T(128)} %param.28) | copy-start | bytes 100
  0.7 12.3 %copy-start = (f32[64,8,256]{2,1,0:T(8,128)S(1)}, f32[64,8,256]{2,1,0:T(8,128)}, u32[]{:S(2)}) copy-start(f32[64,8,256]{2,1,0:T(8,128)} %param.31) | copy-start | bytes 1572868
  3.2 10.5 %collective-permute-start = (bf16[4,64,256]{2,1,0:T(8,128)(2,1)S(1)}, bf16[4,64,256]{2,1,0:T(8,128)(2,1)S(1)}, u32[]{:S(2)}, u32[]{:S(2)}) collective-permute-start(bf16[4,64,256]{2,1,0:T(8,128)(2,1)S(1)} %gather_fusion), channel_id=1, source_target_pairs={{0,1},{1,2},{2,3},{3,4},{4,5},{5,6},{6,7},{7,8},{8,9},{9,10},{10,1... | collective-permute-start | bytes 393224 | tf_op jit(solution)/shard_map/ppermute | solution.py:18
  3.8 9.9 %collective-permute-start.1 = (bf16[4,64,256]{2,1,0:T(8,128)(2,1)S(1)}, bf16[4,64,256]{2,1,0:T(8,128)(2,1)S(1)}, u32[]{:S(2)}, u32[]{:S(2)}) collective-permute-start(bf16[4,64,256]{2,1,0:T(8,128)(2,1)S(1)} %gather_fusion.1), channel_id=1, source_target_pairs={{1,0},{2,1},{3,2},{4,3},{5,4},{6,5},{7,6},{8,7},{9,8},{10,9},{11,1... | collective-permute-start | bytes 393224 | tf_op jit(solution)/shard_map/ppermute | solution.py:21
  6.2 9.6 %collective-permute-start.2 = (bf16[4,64,256]{2,1,0:T(8,128)(2,1)S(1)}, bf16[4,64,256]{2,1,0:T(8,128)(2,1)S(1)}, u32[]{:S(2)}, u32[]{:S(2)}) collective-permute-start(bf16[4,64,256]{2,1,0:T(8,128)(2,1)S(1)} %gather_fusion.2), channel_id=1, source_target_pairs={{0,32},{32,64},{64,96},{96,128},{128,160},{160,192},{192,224},{224... | collective-permute-start | bytes 393224 | tf_op jit(solution)/shard_map/ppermute | solution.py:18
  8.8 7.0 %collective-permute-start.3 = (bf16[4,64,256]{2,1,0:T(8,128)(2,1)S(1)}, bf16[4,64,256]{2,1,0:T(8,128)(2,1)S(1)}, u32[]{:S(2)}, u32[]{:S(2)}) collective-permute-start(bf16[4,64,256]{2,1,0:T(8,128)(2,1)S(1)} %gather_fusion.3), channel_id=1, source_target_pairs={{32,0},{64,32},{96,64},{128,96},{160,128},{192,160},{224,192},{0,2... | collective-permute-start | bytes 393224 | tf_op jit(solution)/shard_map/ppermute | solution.py:21
  28.4 7.1 %collective-permute-start.4 = (bf16[4,64,256]{2,1,0:T(8,128)(2,1)S(1)}, bf16[4,64,256]{2,1,0:T(8,128)(2,1)S(1)}, u32[]{:S(2)}, u32[]{:S(2)}) collective-permute-start(bf16[4,64,256]{2,1,0:T(8,128)(2,1)S(1)} %gather_fusion.5), channel_id=1, source_target_pairs={{0,1},{1,2},{2,3},{3,4},{4,5},{5,6},{6,7},{7,8},{8,9},{9,10},{10,1... | collective-permute-start | bytes 393224 | tf_op jit(solution)/shard_map/ppermute | solution.py:18
  28.5 7.1 %collective-permute-start.5 = (bf16[4,64,256]{2,1,0:T(8,128)(2,1)S(1)}, bf16[4,64,256]{2,1,0:T(8,128)(2,1)S(1)}, u32[]{:S(2)}, u32[]{:S(2)}) collective-permute-start(bf16[4,64,256]{2,1,0:T(8,128)(2,1)S(1)} %gather_fusion.6), channel_id=1, source_target_pairs={{1,0},{2,1},{3,2},{4,3},{5,4},{6,5},{7,6},{8,7},{9,8},{10,9},{11,1... | collective-permute-start | bytes 393224 | tf_op jit(solution)/shard_map/ppermute | solution.py:21
  30.3 6.9 %collective-permute-start.6 = (bf16[4,64,256]{2,1,0:T(8,128)(2,1)S(1)}, bf16[4,64,256]{2,1,0:T(8,128)(2,1)S(1)}, u32[]{:S(2)}, u32[]{:S(2)}) collective-permute-start(bf16[4,64,256]{2,1,0:T(8,128)(2,1)S(1)} %gather_fusion.7), channel_id=1, source_target_pairs={{0,32},{32,64},{64,96},{96,128},{128,160},{160,192},{192,224},{224... | collective-permute-start | bytes 393224 | tf_op jit(solution)/shard_map/ppermute | solution.py:18
  30.5 6.7 %collective-permute-start.7 = (bf16[4,64,256]{2,1,0:T(8,128)(2,1)S(1)}, bf16[4,64,256]{2,1,0:T(8,128)(2,1)S(1)}, u32[]{:S(2)}, u32[]{:S(2)}) collective-permute-start(bf16[4,64,256]{2,1,0:T(8,128)(2,1)S(1)} %gather_fusion.8), channel_id=1, source_target_pairs={{32,0},{64,32},{96,64},{128,96},{160,128},{192,160},{224,192},{0,2... | collective-permute-start | bytes 393224 | tf_op jit(solution)/shard_map/ppermute | solution.py:21
  49.8 6.8 %collective-permute-start.8 = (bf16[4,64,256]{2,1,0:T(8,128)(2,1)S(1)}, bf16[4,64,256]{2,1,0:T(8,128)(2,1)S(1)}, u32[]{:S(2)}, u32[]{:S(2)}) collective-permute-start(bf16[4,64,256]{2,1,0:T(8,128)(2,1)S(1)} %gather_fusion.10), channel_id=1, source_target_pairs={{0,1},{1,2},{2,3},{3,4},{4,5},{5,6},{6,7},{7,8},{8,9},{9,10},{10,1... | collective-permute-start | bytes 393224 | tf_op jit(solution)/shard_map/ppermute | solution.py:18
  49.9 6.7 %collective-permute-start.9 = (bf16[4,64,256]{2,1,0:T(8,128)(2,1)S(1)}, bf16[4,64,256]{2,1,0:T(8,128)(2,1)S(1)}, u32[]{:S(2)}, u32[]{:S(2)}) collective-permute-start(bf16[4,64,256]{2,1,0:T(8,128)(2,1)S(1)} %gather_fusion.11), channel_id=1, source_target_pairs={{1,0},{2,1},{3,2},{4,3},{5,4},{6,5},{7,6},{8,7},{9,8},{10,9},{11,1... | collective-permute-start | bytes 393224 | tf_op jit(solution)/shard_map/ppermute | solution.py:21
  51.6 6.2 %collective-permute-start.10 = (bf16[4,64,256]{2,1,0:T(8,128)(2,1)S(1)}, bf16[4,64,256]{2,1,0:T(8,128)(2,1)S(1)}, u32[]{:S(2)}, u32[]{:S(2)}) collective-permute-start(bf16[4,64,256]{2,1,0:T(8,128)(2,1)S(1)} %gather_fusion.12), channel_id=1, source_target_pairs={{0,32},{32,64},{64,96},{96,128},{128,160},{160,192},{192,224},{224... | collective-permute-start | bytes 393224 | tf_op jit(solution)/shard_map/ppermute | solution.py:18
  54.2 5.0 %collective-permute-start.11 = (bf16[4,64,256]{2,1,0:T(8,128)(2,1)S(1)}, bf16[4,64,256]{2,1,0:T(8,128)(2,1)S(1)}, u32[]{:S(2)}, u32[]{:S(2)}) collective-permute-start(bf16[4,64,256]{2,1,0:T(8,128)(2,1)S(1)} %gather_fusion.13), channel_id=1, source_target_pairs={{32,0},{64,32},{96,64},{128,96},{160,128},{192,160},{224,192},{0,2... | collective-permute-start | bytes 393224 | tf_op jit(solution)/shard_map/ppermute | solution.py:21
  59.9 19.8 %copy-start.8 = (s32[3]{0:T(128)S(1)}, s32[3]{0:T(128)}, u32[]{:S(2)}) copy-start(s32[3]{0:T(128)} %constant.296.clone.1) | copy-start | bytes 40
  64.9 69.9 %copy-start.2 = (f32[8,64,256]{2,1,0:T(8,128)S(1)}, f32[8,64,256]{2,1,0:T(8,128)}, u32[]{:S(2)}) copy-start(f32[8,64,256]{2,1,0:T(8,128)} %param.30) | copy-start | bytes 1572868
  64.9 69.9 %copy-start.3 = (f32[8,64,256]{2,1,0:T(8,128)S(1)}, f32[8,64,256]{2,1,0:T(8,128)}, u32[]{:S(2)}) copy-start(f32[8,64,256]{2,1,0:T(8,128)} %get-tuple-element.167) | copy-start | bytes 1572868
  64.9 69.9 %copy-start.4 = (f32[8,64,256]{2,1,0:T(8,128)S(1)}, f32[8,64,256]{2,1,0:T(8,128)}, u32[]{:S(2)}) copy-start(f32[8,64,256]{2,1,0:T(8,128)} %get-tuple-element.168) | copy-start | bytes 1572868
  66.4 17.5 %all-to-all-start = ((f32[8,1,2048]{2,1,0:T(1,128)}), f32[8,1,2048]{2,1,0:T(1,128)S(1)}, u32[]{:S(2)}, u32[]{:S(2)}) async-start(f32[8,1,2048]{2,1,0:T(1,128)} %reshape.854), calls=%async_computation | async-start | bytes 131072 | tf_op jit(solution)/shard_map/all_to_all | solution.py:34
  85.9 14.8 %all-to-all-start.1 = ((f32[32,1,64]{2,1,0:T(1,128)}), f32[32,1,64]{2,1,0:T(1,128)S(1)}, u32[]{:S(2)}, u32[]{:S(2)}) async-start(f32[32,1,64]{2,1,0:T(1,128)} %bitcast.30), calls=%async_computation.1 | async-start | bytes 32768 | tf_op jit(solution)/shard_map/all_to_all | solution.py:41
  101.3 13.6 %all-to-all-start.2 = ((f32[32,1,64]{2,1,0:T(1,128)}), f32[32,1,64]{2,1,0:T(1,128)S(1)}, u32[]{:S(2)}, u32[]{:S(2)}) async-start(f32[32,1,64]{2,1,0:T(1,128)} %broadcast_in_dim.9), calls=%async_computation.2 | async-start | bytes 32768 | tf_op jit(solution)/shard_map/all_to_all | solution.py:53
  116.7 8.9 %all-to-all-start.3 = ((f32[8,1,2048]{2,1,0:T(1,128)}), f32[8,1,2048]{2,1,0:T(1,128)S(1)}, u32[]{:S(2)}, u32[]{:S(2)}) async-start(f32[8,1,2048]{2,1,0:T(1,128)} %reshape.856), calls=%async_computation.3 | async-start | bytes 131072 | tf_op jit(solution)/shard_map/all_to_all | solution.py:53
  134.8 0.6 copy-start.5
where the time goes:
time: 139 us; the launch traced here: 137 us
  starting transfers between devices  45.2 us (33%)
  waiting for transfers between devices  31.4 us (23%)
  local copies, waits for them, and re-layouts  25.5 us (18%)
  matrix products  21.4 us (15%)
  other arithmetic  12.1 us (9%)
    dot_general x3, matrix products, on_device(): jnp.einsum('ikrb,ikbc->irc', picked, blocks, preferred_element_type=jnp.f...  16.7 us
    ppermute x6, starting transfers between devices, with_halo(): lax.ppermute(lax.slice_in_dim(block, 0, width, axis=dim), axis, backward)  13.3 us
    all_to_all x1, starting transfers between devices, sent_and_summed(): pieces = lax.all_to_all(in_blocks(x, dim, devices), axis, 0, 0, tiled=True)  13.3 us
    all_to_all x2, waiting for transfers between devices, copy_for_each(): lax.all_to_all(jnp.broadcast_to(x[None], (devices, *x.shape)), axis, 0, 0...  12.7 us
    all_to_all x1, waiting for transfers between devices, sum_by_axis(): return jnp.sum(lax.all_to_all(own, far, 0, 0, tiled=True), axis=0)  9.11 us
    all_to_all x2, starting transfers between devices, copy_for_each(): lax.all_to_all(jnp.broadcast_to(x[None], (devices, *x.shape)), axis, 0, 0...  8.56 us
    gather x6, local copies, waits for them, and re-layouts, on_device(): outgoing_x = jnp.concatenate([rounded[lists[3]], rounded[lists[2]]], axis=0)  7.13 us
    gather x6, local copies, waits for them, and re-layouts, on_device(): outgoing_y = jnp.concatenate([rounded[lists[1]], rounded[lists[0]]], axis=0)  7.13 us
  transfers between devices with their start and end apart: 16, of which 8 were waited for; matrix products, arithmetic and copies ran while one was open for 6% of the time, Pallas kernels for 0%

commit v1 on v0

v1 whole, which is shorter than its diff:
```python
import jax
import jax.numpy as jnp
from jax import lax
from jax.experimental import pallas as pl
from jax.experimental.pallas import tpu as pltpu
from jax.sharding import Mesh
from jax.sharding import PartitionSpec as P

STEPS = 3
GY = ("y0", "y1", "core")
GX_GY = ("gx", "y0", "y1", "core")
F32, BF16 = jnp.float32, jnp.bfloat16
VMEM = pl.BlockSpec(memory_space=pltpu.VMEM)
SMEM = pl.BlockSpec(memory_space=pltpu.SMEM)


def call(kernel, name, ins, outs, scratch=(), flops=0, nbytes=0, out_specs=None):
    return pl.pallas_call(
        kernel,
        name=name,
        in_specs=ins,
        out_specs=out_specs or [VMEM] * len(outs),
        out_shape=outs,
        scratch_shapes=scratch,
        cost_estimate=pl.CostEstimate(flops=flops, bytes_accessed=nbytes, transcendentals=0),
        compiler_params=pltpu.CompilerParams(vmem_limit_bytes=24 << 20),
    )


def parities():
    return lax.axis_index("core"), lax.rem(lax.axis_index("gx"), 2)


def directions(side, layer):
    received = (1 - side, side, 3 - layer, 2 + layer)
    sent = (side, 1 - side, 2 + layer, 3 - layer)
    return received, sent


def fill_messages(send, rows, outs, side, layer):
    _, sent = directions(side, layer)
    for out, direction in zip(outs, sent, strict=True):
        for j in range(out.shape[0]):
            out[j] = rows[send[0, direction, j]]


def first_kernel(send, start, x_out, *outs):
    side, layer = parities()
    x_out[...] = start[...].astype(BF16)
    fill_messages(send, x_out, outs, side, layer)


def place_rows(x, received, src, side, layer):
    count = x.shape[0]
    width = received[0].shape[0]
    src[:count] = x[...]
    numbers, _ = directions(side, layer)
    for ref, direction in zip(received, numbers, strict=True):
        src[pl.ds(count + direction * width, width)] = ref[...]
    src[count + 4 * width] = jnp.zeros(src.shape[1:], src.dtype)


def product_of_row(i, cols, live, src, blocks):
    slots, dead = cols.shape[1], src.shape[0] - 1
    picked = [src[jnp.where(k < live[i], cols[i, k], dead)] for k in range(slots)]
    tall = blocks[i].reshape(slots * blocks.shape[2], blocks.shape[3])
    return jnp.dot(jnp.concatenate(picked, axis=1), tall, preferred_element_type=F32)


def step_kernel(cols, live, send, x, ra, rb, rc, rd, blocks, v_out, x_out, oa, ob, oc, od, src):
    side, layer = parities()
    place_rows(x, (ra, rb, rc, rd), src, side, layer)
    for i in range(x.shape[0]):
        v = product_of_row(i, cols, live, src, blocks)
        v_out[i] = v
        x_out[i] = v.astype(BF16)
    fill_messages(send, x_out, (oa, ob, oc, od), side, layer)


def halves(v):
    high = v.astype(BF16)
    return high, (v - high.astype(F32)).astype(BF16)


def sketched(v, high, low):
    left, right = [], []
    for i in range(v.shape[0]):
        v_high, v_low = halves(v[i])
        left += [v_high, v_low, v_high]
        right += [high[i], high[i], low[i]]
    return lax.dot_general(
        jnp.concatenate(left, axis=1),
        jnp.concatenate(right, axis=1),
        (((1,), (1,)), ((), ())),
        preferred_element_type=F32,
    )


def prepare_kernel(sketch, start, high, low, w_out):
    for i in range(start.shape[0]):
        high[i], low[i] = halves(sketch[:, i, :])
    w_out[...] = sketched(start, high, low)


def sketch_kernel(v, high, low, w_out):
    w_out[...] = sketched(v, high, low)


def last_kernel(cols, live, x, ra, rb, rc, rd, blocks, high, low, w0, w1, w2, v_out, w_out, src):
    side, layer = parities()
    place_rows(x, (ra, rb, rc, rd), src, side, layer)
    for i in range(x.shape[0]):
        v_out[i] = product_of_row(i, cols, live, src, blocks)
    w3 = sketched(v_out, high, low)
    w_out[0] = jnp.concatenate([w0[...], w1[...]], axis=1)
    w_out[1] = jnp.concatenate([w2[...], w3], axis=1)


def final_kernel(v0, v1, v2, v3, w, basis, factor_out, out, sems):
    count = 4
    size = w.shape[2] // 2
    sums = [w[s // 2][:, (s % 2) * size : (s % 2 + 1) * size] for s in range(count)]
    columns, factor, inverse = [], {}, []
    for s in range(count):
        residue = sums[s]
        for m in range(s):
            factor[m, s] = jnp.sum(columns[m] * sums[s], axis=1, keepdims=True)
            residue = residue - factor[m, s] * columns[m]
        factor[s, s] = jnp.sqrt(jnp.sum(residue * residue, axis=1, keepdims=True) + 1e-06)
        inverse.append(1.0 / factor[s, s])
        columns.append(residue * inverse[s])
    copies = []
    for s, v in enumerate((v0, v1, v2, v3)):
        for i in range(v.shape[0]):
            total = v[i]
            for m in range(s):
                total = total - factor[m, s] * out[m, i]
            out[s, i] = total * inverse[s]
        copies.append(pltpu.make_async_copy(out.at[s], basis.at[s], sems.at[s]))
        copies[-1].start()
    lane = lax.broadcasted_iota(jnp.int32, (w.shape[1], 128), 1)
    table = jnp.zeros((w.shape[1], 128), F32)
    for (m, s), value in factor.items():
        table = table + jnp.where(lane == m * count + s, value, 0.0)
    table = table.T
    for m in range(count):
        factor_out[m] = table[m * count : (m + 1) * count]
    for copy in copies:
        copy.wait()


def swaps(count, offset):
    pairs = []
    for i in range(offset, count + offset, 2):
        a, b = i % count, (i + 1) % count
        pairs += [(a, b), (b, a)]
    return pairs


def exchange(messages):
    oa, ob, oc, od = messages
    gy, gx = lax.axis_size(GY), lax.axis_size("gx")
    rd = lax.ppermute(od, "gx", swaps(gx, 1))
    rc = lax.ppermute(oc, "gx", swaps(gx, 0))
    rb = lax.ppermute(ob, GY, swaps(gy, 1))
    ra = lax.ppermute(oa, GY, swaps(gy, 0))
    return ra, rb, rc, rd


def shifted_sum(x, axis):
    count = lax.axis_size(axis)
    parts = [lax.ppermute(x, axis, [(i, (i + k) % count) for i in range(count)]) for k in range(1, count)]
    return sum(parts, x)


def doubled_sum(x, axis):
    count = lax.axis_size(axis)
    k = 1
    while k < count:
        x = x + lax.ppermute(x, axis, [(i, i ^ k) for i in range(count)])
        k *= 2
    return x


def summed(x):
    x = doubled_sum(x, "core")
    x = shifted_sum(x, "y1")
    x = shifted_sum(x, "y0")
    return doubled_sum(x, "gx")


def on_device(blocks, block_cols, live_blocks, send_rows, start, sketch):
    rows, slots, size, _ = blocks.shape
    rhs = start.shape[1]
    width = send_rows.shape[2]
    count = sketch.shape[0]
    vector = jax.ShapeDtypeStruct(start.shape, F32)
    rounded = jax.ShapeDtypeStruct(start.shape, BF16)
    message = jax.ShapeDtypeStruct((width, rhs, size), BF16)
    part = jax.ShapeDtypeStruct((rhs, count), F32)
    src = pltpu.VMEM((rows + 4 * width + 1, rhs, size), BF16)
    flops = 2 * rows * slots * rhs * size * size
    sketch_flops = 6 * rows * rhs * size * count

    x, *messages = call(
        first_kernel, "first", [SMEM, VMEM], [rounded] + [message] * 4, flops=1 << 20, nbytes=1 << 20
    )(send_rows, start)
    received = exchange(messages)
    high, low, w0 = call(
        prepare_kernel, "prepare", [VMEM] * 2, [rounded] * 2 + [part], flops=sketch_flops, nbytes=1 << 20
    )(sketch, start)
    step = call(
        step_kernel,
        "step",
        [SMEM] * 3 + [VMEM] * 6,
        [vector, rounded] + [message] * 4,
        [src],
        flops=flops,
        nbytes=blocks.size * 2,
    )
    sketch_of = call(sketch_kernel, "sketch", [VMEM] * 3, [part], flops=sketch_flops, nbytes=1 << 20)
    v1, x, *messages = step(block_cols, live_blocks, send_rows, x, *received, blocks)
    received = exchange(messages)
    (w1,) = sketch_of(v1, high, low)
    v2, x, *messages = step(block_cols, live_blocks, send_rows, x, *received, blocks)
    received = exchange(messages)
    (w2,) = sketch_of(v2, high, low)
    v3, w = call(
        last_kernel,
        "last",
        [SMEM] * 2 + [VMEM] * 11,
        [vector, jax.ShapeDtypeStruct((2, rhs, 2 * count), F32)],
        [src],
        flops=flops + sketch_flops,
        nbytes=blocks.size * 2,
    )(block_cols, live_blocks, x, *received, blocks, high, low, w0, w1, w2)
    w = summed(w)
    basis, factor = call(
        final_kernel,
        "final",
        [VMEM] * 5,
        [
            jax.ShapeDtypeStruct((STEPS + 1, *start.shape), F32),
            jax.ShapeDtypeStruct((STEPS + 1, STEPS + 1, rhs), F32),
        ],
        [pltpu.VMEM((STEPS + 1, *start.shape), F32), pltpu.SemaphoreType.DMA((STEPS + 1,))],
        flops=1 << 22,
        nbytes=1 << 22,
        out_specs=[pl.BlockSpec(memory_space=pl.ANY), VMEM],
    )(start, v1, v2, v3, w)
    return basis, factor


def solution(mesh):
    split = Mesh(mesh.devices.reshape(mesh.shape["gx"], 4, 4, 2), GX_GY)
    return jax.shard_map(
        on_device,
        mesh=split,
        in_specs=(
            P(GX_GY, None, None, None),
            P(GX_GY, None),
            P(GX_GY),
            P(GX_GY, None, None),
            P(GX_GY, None, None),
            P(None, GX_GY, None),
        ),
        out_specs=(P(None, GX_GY, None, None), P()),
        check_vma=False,
    )
```

time: 139 us -> 84.3 us (0.61); the launches traced: 137 us -> 84 us
  matrix products: 21.4 us -> 0 us
  local copies, waits for them, and re-layouts: 25.5 us -> 6.46 us
  Pallas kernels: 0 us -> 13.2 us
  other arithmetic: 12.1 us -> 0.07 us
  starting transfers between devices: 45.2 us -> 33.2 us
    all_to_all x4 -> x0, starting transfers between devices: 26.9 us -> none  [the longest x1 13.3 us: sent_and_summed(): pieces = lax.all_to_all(in_blocks(x, dim, devices), axis, 0, 0, tiled=True)]
    all_to_all x4 -> x0, waiting for transfers between devices: 25.3 us -> none  [the longest x2 12.7 us: copy_for_each(): lax.all_to_all(jnp.broadcast_to(x[None], (devices, *x.shape)), axis, 0, 0...]
    ppermute x12 -> x22, waiting for transfers between devices: 6.16 us -> 30.2 us  [the longest x4 13.5 us: doubled_sum(): x = x + lax.ppermute(x, axis, [(i, i ^ k) for i in range(count)])]
    dot_general x7 -> x0, matrix products: 21.4 us -> none  [the longest x3 16.7 us: on_device(): jnp.einsum('ikrb,ikbc->irc', picked, blocks, preferred_element_type=jnp.f...]
    gather x15 -> x0, local copies, waits for them, and re-layouts: 16.3 us -> none  [the longest x6 7.13 us: on_device(): outgoing_x = jnp.concatenate([rounded[lists[3]], rounded[lists[2]]], axis=0)]
    ppermute x12 -> x22, starting transfers between devices: 18.4 us -> 33.2 us  [the longest x3 11.3 us: exchange(): rd = lax.ppermute(od, 'gx', swaps(gx, 1))]
    pallas_call x0 -> x8, Pallas kernels: none -> 13.2 us  [the longest x2 4.59 us: on_device(): step(block_cols, live_blocks, send_rows, x, *received, blocks)]
    another operation x7 -> x0, other arithmetic: 6.51 us -> none
  transfers between devices with their start and end apart: 16 -> 22, of which waited for: 8 -> 13; matrix products, arithmetic and copies ran while one was open for 6% -> 0% of each run, Pallas kernels for 0% -> 3%
where the time goes in v1:
time: 84.3 us; the launch traced here: 84 us
  starting transfers between devices  33.2 us (39%)
  waiting for transfers between devices  30.2 us (36%)
  Pallas kernels  13.2 us (16%)
  local copies, waits for them, and re-layouts  6.46 us (8%)
  between operations  0.96 us (1%)
    ppermute x4, waiting for transfers between devices, doubled_sum(): x = x + lax.ppermute(x, axis, [(i, i ^ k) for i in range(count)])  13.5 us
    ppermute x3, starting transfers between devices, exchange(): rd = lax.ppermute(od, 'gx', swaps(gx, 1))  11.3 us
    ppermute x6, waiting for transfers between devices, shifted_sum(): lax.ppermute(x, axis, [(i, (i + k) % count) for i in range(count)])  9.28 us
    ppermute x3, starting transfers between devices, exchange(): rb = lax.ppermute(ob, GY, swaps(gy, 1))  7.96 us
    ppermute x6, starting transfers between devices, shifted_sum(): lax.ppermute(x, axis, [(i, (i + k) % count) for i in range(count)])  6.64 us
    ppermute x4, starting transfers between devices, doubled_sum(): x = x + lax.ppermute(x, axis, [(i, i ^ k) for i in range(count)])  6.59 us
    unnamed x20, local copies, waits for them, and re-layouts  6.46 us
    ppermute x3, waiting for transfers between devices, exchange(): rd = lax.ppermute(od, 'gx', swaps(gx, 1))  5.62 us
  transfers between devices with their start and end apart: 22, of which 13 were waited for; matrix products, arithmetic and copies ran while one was open for 0% of the time, Pallas kernels for 3%

profile of v1, /device:TPU:8, one launch (start us, length us, event | category | flops | bytes accessed | tf_op | source)
XLA Modules:
  0.0 84.0 jit_solution(15231809669476840886)
XLA Ops:
  0.6 1.0 %copy-done.2 = f32[8,64,256]{2,1,0:T(8,128)S(1)} copy-done((f32[8,64,256]{2,1,0:T(8,128)S(1)}, f32[8,64,256]{2,1,0:T(8,128)}, u32[]{:S(2)}) %copy-start.2) | copy-done | bytes 524312
  1.7 0.7 copy-done.7
  3.1 2.3 %collective-permute-start.1 = (bf16[4,64,256]{2,1,0:T(8,128)(2,1)S(1)}, bf16[4,64,256]{2,1,0:T(8,128)(2,1)S(1)}, u32[]{:S(2)}, u32[]{:S(2)}) collective-permute-start(bf16[4,64,256]{2,1,0:T(8,128)(2,1)S(1)} %get-tuple-element.26), channel_id=1, source_target_pairs={{1,2},{2,1},{3,4},{4,3},{5,6},{6,5},{7,8},{8,7},{9,10},{10,9},{11,... | collective-permute-start | bytes 393224 | tf_op jit(solution)/shard_map/ppermute | solution.py:165
  5.6 4.9 %collective-permute-start.3 = (bf16[4,64,256]{2,1,0:T(8,128)(2,1)S(1)}, bf16[4,64,256]{2,1,0:T(8,128)(2,1)S(1)}, u32[]{:S(2)}, u32[]{:S(2)}) collective-permute-start(bf16[4,64,256]{2,1,0:T(8,128)(2,1)S(1)} %get-tuple-element.28), channel_id=1, source_target_pairs={{32,64},{64,32},{96,128},{128,96},{160,192},{192,160},{224,0},{0,2... | collective-permute-start | bytes 393224 | tf_op jit(solution)/shard_map/ppermute | solution.py:163
  10.5 4.1 %collective-permute-done.3.rd = bf16[4,64,256]{2,1,0:T(8,128)(2,1)S(1)} collective-permute-done((bf16[4,64,256]{2,1,0:T(8,128)(2,1)S(1)}, bf16[4,64,256]{2,1,0:T(8,128)(2,1)S(1)}, u32[]{:S(2)}, u32[]{:S(2)}) %collective-permute-start.3) | collective-permute-done | bytes 131104 | tf_op jit(solution)/shard_map/ppermute | solution.py:163
  14.6 3.4 %copy-done = bf16[8,8,256,256]{3,2,1,0:T(8,128)(2,1)S(1)} copy-done((bf16[8,8,256,256]{3,2,1,0:T(8,128)(2,1)S(1)}, bf16[8,8,256,256]{3,2,1,0:T(8,128)(2,1)}, u32[]{:S(2)}) %copy-start) | copy-done | bytes 8388632
  18.0 0.7 copy-done.5
  19.3 2.3 %step.2 = (f32[8,64,256]{2,1,0:T(8,128)S(1)}, bf16[8,64,256]{2,1,0:T(8,128)(2,1)S(1)}, bf16[4,64,256]{2,1,0:T(8,128)(2,1)S(1)}, bf16[4,64,256]{2,1,0:T(8,128)(2,...) custom-call(s32[8,8]{1,0:T(8,128)S(1)} %copy-done.5, s32[8]{0:T(128)S(1)} %copy-done.8, ...), custom_call_target="tpu_custom_call" | custom-call | flops 536870912 | bytes 8388608 | tf_op jit(solution)/shard_map/step/pallas_call | solution.py:222
  21.8 4.1 %collective-permute-start.5 = (bf16[4,64,256]{2,1,0:T(8,128)(2,1)S(1)}, bf16[4,64,256]{2,1,0:T(8,128)(2,1)S(1)}, u32[]{:S(2)}, u32[]{:S(2)}) collective-permute-start(bf16[4,64,256]{2,1,0:T(8,128)(2,1)S(1)} %get-tuple-element.32), channel_id=1, source_target_pairs={{1,2},{2,1},{3,4},{4,3},{5,6},{6,5},{7,8},{8,7},{9,10},{10,9},{11,... | collective-permute-start | bytes 393224 | tf_op jit(solution)/shard_map/ppermute | solution.py:165
  25.9 3.2 %collective-permute-start.7 = (bf16[4,64,256]{2,1,0:T(8,128)(2,1)S(1)}, bf16[4,64,256]{2,1,0:T(8,128)(2,1)S(1)}, u32[]{:S(2)}, u32[]{:S(2)}) collective-permute-start(bf16[4,64,256]{2,1,0:T(8,128)(2,1)S(1)} %get-tuple-element.34), channel_id=1, source_target_pairs={{32,64},{64,32},{96,128},{128,96},{160,192},{192,160},{224,0},{0,2... | collective-permute-start | bytes 393224 | tf_op jit(solution)/shard_map/ppermute | solution.py:163
  29.1 1.7 %collective-permute-done.6.rc = bf16[4,64,256]{2,1,0:T(8,128)(2,1)S(1)} collective-permute-done((bf16[4,64,256]{2,1,0:T(8,128)(2,1)S(1)}, bf16[4,64,256]{2,1,0:T(8,128)(2,1)S(1)}, u32[]{:S(2)}, u32[]{:S(2)}) %collective-permute-start.6) | collective-permute-done | bytes 131104 | tf_op jit(solution)/shard_map/ppermute | solution.py:164
  30.9 1.2 %collective-permute-done.7.rd = bf16[4,64,256]{2,1,0:T(8,128)(2,1)S(1)} collective-permute-done((bf16[4,64,256]{2,1,0:T(8,128)(2,1)S(1)}, bf16[4,64,256]{2,1,0:T(8,128)(2,1)S(1)}, u32[]{:S(2)}, u32[]{:S(2)}) %collective-permute-start.7) | collective-permute-done | bytes 131104 | tf_op jit(solution)/shard_map/ppermute | solution.py:163
  32.1 2.3 %step.3 = (f32[8,64,256]{2,1,0:T(8,128)S(1)}, bf16[8,64,256]{2,1,0:T(8,128)(2,1)S(1)}, bf16[4,64,256]{2,1,0:T(8,128)(2,1)S(1)}, bf16[4,64,256]{2,1,0:T(8,128)(2,...) custom-call(s32[8,8]{1,0:T(8,128)S(1)} %copy-done.6, s32[8]{0:T(128)S(1)} %copy-done.9, ...), custom_call_target="tpu_custom_call" | custom-call | flops 536870912 | bytes 8388608 | tf_op jit(solution)/shard_map/step/pallas_call | solution.py:225
  34.5 1.6 %collective-permute-start.9 = (bf16[4,64,256]{2,1,0:T(8,128)(2,1)S(1)}, bf16[4,64,256]{2,1,0:T(8,128)(2,1)S(1)}, u32[]{:S(2)}, u32[]{:S(2)}) collective-permute-start(bf16[4,64,256]{2,1,0:T(8,128)(2,1)S(1)} %get-tuple-element.38), channel_id=1, source_target_pairs={{1,2},{2,1},{3,4},{4,3},{5,6},{6,5},{7,8},{8,7},{9,10},{10,9},{11,... | collective-permute-start | bytes 393224 | tf_op jit(solution)/shard_map/ppermute | solution.py:165
  36.3 3.1 %collective-permute-start.11 = (bf16[4,64,256]{2,1,0:T(8,128)(2,1)S(1)}, bf16[4,64,256]{2,1,0:T(8,128)(2,1)S(1)}, u32[]{:S(2)}, u32[]{:S(2)}) collective-permute-start(bf16[4,64,256]{2,1,0:T(8,128)(2,1)S(1)} %get-tuple-element.40), channel_id=1, source_target_pairs={{32,64},{64,32},{96,128},{128,96},{160,192},{192,160},{224,0},{0,2... | collective-permute-start | bytes 393224 | tf_op jit(solution)/shard_map/ppermute | solution.py:163
  39.4 1.9 %prepare.1 = (bf16[8,64,256]{2,1,0:T(8,128)(2,1)S(1)}, bf16[8,64,256]{2,1,0:T(8,128)(2,1)S(1)}, f32[64,64]{1,0:T(8,128)S(1)}) custom-call(f32[64,8,256]{2,1,0:T(8,128)S(1)} %copy-done.4, f32[8,64,256]{2,1,0:T(8,128)S(1)} %copy-done.3), custom_call_target="tpu_custom_call" | custom-call | flops 50331648 | bytes 1048576 | tf_op jit(solution)/shard_map/prepare/pallas_call | solution.py:209
  42.4 2.6 %last.1 = (f32[8,64,256]{2,1,0:T(8,128)S(1)}, f32[2,64,128]{2,1,0:T(8,128)S(1)}) custom-call(s32[8,8]{1,0:T(8,128)S(1)} %copy-done.6, s32[8]{0:T(128)S(1)} %copy-done.9, bf16[8,64,256]{2,1,0:T(8,128)(2,1)S(1)} %get-tuple-element.36.x, bf16[4,64,256]{2,1,0:T(8,128)(2,1)S(1)} %collective-permute-done.8.ra, bf16[4,64,256]{2,1,0:T(8,128)(2,1)S(1)} %collective-permute-done.9.rb, ...), custom_call_target="tpu_custom_call" | custom-call | flops 587202560 | bytes 8388608 | tf_op jit(solution)/shard_map/last/pallas_call | solution.py:228
  45.2 1.2 %collective-permute-done.12 = f32[2,64,128]{2,1,0:T(8,128)S(1)} collective-permute-done((f32[2,64,128]{2,1,0:T(8,128)S(1)}, f32[2,64,128]{2,1,0:T(8,128)S(1)}, u32[]{:S(2)}, u32[]{:S(2)}) %collective-permute-start.12) | collective-permute-done | bytes 65568 | tf_op jit(solution)/shard_map/ppermute | solution.py:180
  46.4 2.8 %collective-permute-start.15 = (f32[2,64,128]{2,1,0:T(8,128)S(1)}, f32[2,64,128]{2,1,0:T(8,128)S(1)}, u32[]{:S(2)}, u32[]{:S(2)}) collective-permute-start(f32[2,64,128]{2,1,0:T(8,128)S(1)} %add.30), channel_id=1, source_target_pairs={{0,6},{2,0},{4,2},{6,4},{1,7},{3,1},{5,3},{7,5},{8,14},{10,8},{12,... | collective-permute-start | bytes 196616 | tf_op jit(solution)/shard_map/ppermute | solution.py:172
  49.3 1.6 %collective-permute-start.13 = (f32[2,64,128]{2,1,0:T(8,128)S(1)}, f32[2,64,128]{2,1,0:T(8,128)S(1)}, u32[]{:S(2)}, u32[]{:S(2)}) collective-permute-start(f32[2,64,128]{2,1,0:T(8,128)S(1)} %add.30), channel_id=1, source_target_pairs={{0,2},{2,4},{4,6},{6,0},{1,3},{3,5},{5,7},{7,1},{8,10},{10,12},{12... | collective-permute-start | bytes 196616 | tf_op jit(solution)/shard_map/ppermute | solution.py:172
  50.8 0.8 collective-permute-done.15
  51.7 3.4 %collective-permute-done.14 = f32[2,64,128]{2,1,0:T(8,128)S(1)} collective-permute-done((f32[2,64,128]{2,1,0:T(8,128)S(1)}, f32[2,64,128]{2,1,0:T(8,128)S(1)}, u32[]{:S(2)}, u32[]{:S(2)}) %collective-permute-start.14) | collective-permute-done | bytes 65568 | tf_op jit(solution)/shard_map/ppermute | solution.py:172
  55.1 0.8 %collective-permute-start.18 = (f32[2,64,128]{2,1,0:T(8,128)S(1)}, f32[2,64,128]{2,1,0:T(8,128)S(1)}, u32[]{:S(2)}, u32[]{:S(2)}) collective-permute-start(f32[2,64,128]{2,1,0:T(8,128)S(1)} %add_add_fusion.1), channel_id=1, source_target_pairs={{0,24},{8,0},{16,8},{24,16},{1,25},{9,1},{17,9},{25,17},{2,26},{10... | collective-permute-start | bytes 196616 | tf_op jit(solution)/shard_map/ppermute | solution.py:172
  56.4 0.9 %collective-permute-start.16 = (f32[2,64,128]{2,1,0:T(8,128)S(1)}, f32[2,64,128]{2,1,0:T(8,128)S(1)}, u32[]{:S(2)}, u32[]{:S(2)}) collective-permute-start(f32[2,64,128]{2,1,0:T(8,128)S(1)} %add_add_fusion.1), channel_id=1, source_target_pairs={{0,8},{8,16},{16,24},{24,0},{1,9},{9,17},{17,25},{25,1},{2,10},{10... | collective-permute-start | bytes 196616 | tf_op jit(solution)/shard_map/ppermute | solution.py:172
  57.3 2.1 %collective-permute-done.18 = f32[2,64,128]{2,1,0:T(8,128)S(1)} collective-permute-done((f32[2,64,128]{2,1,0:T(8,128)S(1)}, f32[2,64,128]{2,1,0:T(8,128)S(1)}, u32[]{:S(2)}, u32[]{:S(2)}) %collective-permute-start.18) | collective-permute-done | bytes 65568 | tf_op jit(solution)/shard_map/ppermute | solution.py:172
  59.4 2.3 %collective-permute-done.17 = f32[2,64,128]{2,1,0:T(8,128)S(1)} collective-permute-done((f32[2,64,128]{2,1,0:T(8,128)S(1)}, f32[2,64,128]{2,1,0:T(8,128)S(1)}, u32[]{:S(2)}, u32[]{:S(2)}) %collective-permute-start.17) | collective-permute-done | bytes 65568 | tf_op jit(solution)/shard_map/ppermute | solution.py:172
  62.8 4.2 %collective-permute-done.19 = f32[2,64,128]{2,1,0:T(8,128)S(1)} collective-permute-done((f32[2,64,128]{2,1,0:T(8,128)S(1)}, f32[2,64,128]{2,1,0:T(8,128)S(1)}, u32[]{:S(2)}, u32[]{:S(2)}) %collective-permute-start.19) | collective-permute-done | bytes 65568 | tf_op jit(solution)/shard_map/ppermute | solution.py:180
  67.0 1.3 %collective-permute-start.20 = (f32[2,64,128]{2,1,0:T(8,128)S(1)}, f32[2,64,128]{2,1,0:T(8,128)S(1)}, u32[]{:S(2)}, u32[]{:S(2)}) collective-permute-start(f32[2,64,128]{2,1,0:T(8,128)S(1)} %add.37), channel_id=1, source_target_pairs={{0,64},{32,96},{64,0},{96,32},{128,192},{160,224},{192,128},{224,1... | collective-permute-start | bytes 196616 | tf_op jit(solution)/shard_map/ppermute | solution.py:180
  68.3 4.6 %collective-permute-done.20 = f32[2,64,128]{2,1,0:T(8,128)S(1)} collective-permute-done((f32[2,64,128]{2,1,0:T(8,128)S(1)}, f32[2,64,128]{2,1,0:T(8,128)S(1)}, u32[]{:S(2)}, u32[]{:S(2)}) %collective-permute-start.20) | collective-permute-done | bytes 65568 | tf_op jit(solution)/shard_map/ppermute | solution.py:180
  73.0 4.7 %collective-permute-start.21 = (f32[2,64,128]{2,1,0:T(8,128)S(1)}, f32[2,64,128]{2,1,0:T(8,128)S(1)}, u32[]{:S(2)}, u32[]{:S(2)}) collective-permute-start(f32[2,64,128]{2,1,0:T(8,128)S(1)} %add.38), channel_id=1, source_target_pairs={{0,128},{32,160},{64,192},{96,224},{128,0},{160,32},{192,64},{224,... | collective-permute-start | bytes 196616 | tf_op jit(solution)/shard_map/ppermute | solution.py:180
  77.7 3.5 %collective-permute-done.21 = f32[2,64,128]{2,1,0:T(8,128)S(1)} collective-permute-done((f32[2,64,128]{2,1,0:T(8,128)S(1)}, f32[2,64,128]{2,1,0:T(8,128)S(1)}, u32[]{:S(2)}, u32[]{:S(2)}) %collective-permute-start.21) | collective-permute-done | bytes 65568 | tf_op jit(solution)/shard_map/ppermute | solution.py:180
  81.2 2.6 %final.1 = (f32[4,8,64,256]{3,2,1,0:T(8,128)}, f32[4,4,64]{2,1,0:T(4,128)}) custom-call(f32[8,64,256]{2,1,0:T(8,128)S(1)} %copy-done.3, f32[8,64,256]{2,1,0:T(8,128)S(1)} %get-tuple-element.29.v.v1, f32[8,64,256]{2,1,0:T(8,128)S(1)} %get-tuple-element.35.v.v2, f32[8,64,256]{2,1,0:T(8,128)S(1)} %get-tuple-element.44.v3, f32[2,64,128]{2,1,0:T(8,128)S(1)} %add.39.w), custom_call_target="tpu_custom_call" | custom-call | flops 4194304 | bytes 4194304 | tf_op jit(solution)/shard_map/final/pallas_call | solution.py:238
  (46 shorter events, 4.8 us)
Async XLA Ops:
  0.6 1.0 %copy-start.2 = (f32[8,64,256]{2,1,0:T(8,128)S(1)}, f32[8,64,256]{2,1,0:T(8,128)}, u32[]{:S(2)}) copy-start(f32[8,64,256]{2,1,0:T(8,128)} %v0.1) | copy-start | bytes 1572868
  1.7 0.7 copy-start.7
  2.4 29.7 %copy-start.6 = (s32[8,8]{1,0:T(8,128)S(1)}, s32[8,8]{1,0:T(8,128)}, u32[]{:S(2)}) copy-start(s32[8,8]{1,0:T(8,128)} %cols.5) | copy-start | bytes 772
  2.4 29.7 %copy-start.9 = (s32[8]{0:T(128)S(1)}, s32[8]{0:T(128)}, u32[]{:S(2)}) copy-start(s32[8]{0:T(128)} %live.5) | copy-start | bytes 100
  3.0 7.5 %collective-permute-start = (bf16[4,64,256]{2,1,0:T(8,128)(2,1)S(1)}, bf16[4,64,256]{2,1,0:T(8,128)(2,1)S(1)}, u32[]{:S(2)}, u32[]{:S(2)}) collective-permute-start(bf16[4,64,256]{2,1,0:T(8,128)(2,1)S(1)} %get-tuple-element.25), channel_id=1, source_target_pairs={{0,1},{1,0},{2,3},{3,2},{4,5},{5,4},{6,7},{7,6},{8,9},{9,8},{10,11... | collective-permute-start | bytes 393224 | tf_op jit(solution)/shard_map/ppermute | solution.py:166
  3.1 7.4 %collective-permute-start.1 = (bf16[4,64,256]{2,1,0:T(8,128)(2,1)S(1)}, bf16[4,64,256]{2,1,0:T(8,128)(2,1)S(1)}, u32[]{:S(2)}, u32[]{:S(2)}) collective-permute-start(bf16[4,64,256]{2,1,0:T(8,128)(2,1)S(1)} %get-tuple-element.26), channel_id=1, source_target_pairs={{1,2},{2,1},{3,4},{4,3},{5,6},{6,5},{7,8},{8,7},{9,10},{10,9},{11,... | collective-permute-start | bytes 393224 | tf_op jit(solution)/shard_map/ppermute | solution.py:165
  5.4 5.2 %collective-permute-start.2 = (bf16[4,64,256]{2,1,0:T(8,128)(2,1)S(1)}, bf16[4,64,256]{2,1,0:T(8,128)(2,1)S(1)}, u32[]{:S(2)}, u32[]{:S(2)}) collective-permute-start(bf16[4,64,256]{2,1,0:T(8,128)(2,1)S(1)} %get-tuple-element.27), channel_id=1, source_target_pairs={{0,32},{32,0},{64,96},{96,64},{128,160},{160,128},{192,224},{224,1... | collective-permute-start | bytes 393224 | tf_op jit(solution)/shard_map/ppermute | solution.py:164
  5.6 9.0 %collective-permute-start.3 = (bf16[4,64,256]{2,1,0:T(8,128)(2,1)S(1)}, bf16[4,64,256]{2,1,0:T(8,128)(2,1)S(1)}, u32[]{:S(2)}, u32[]{:S(2)}) collective-permute-start(bf16[4,64,256]{2,1,0:T(8,128)(2,1)S(1)} %get-tuple-element.28), channel_id=1, source_target_pairs={{32,64},{64,32},{96,128},{128,96},{160,192},{192,160},{224,0},{0,2... | collective-permute-start | bytes 393224 | tf_op jit(solution)/shard_map/ppermute | solution.py:163
  14.6 3.4 %copy-start = (bf16[8,8,256,256]{3,2,1,0:T(8,128)(2,1)S(1)}, bf16[8,8,256,256]{3,2,1,0:T(8,128)(2,1)}, u32[]{:S(2)}) copy-start(bf16[8,8,256,256]{3,2,1,0:T(8,128)(2,1)} %blocks.5) | copy-start | bytes 25165828
  18.0 0.7 copy-start.5
  18.7 0.7 copy-start.8
  19.3 12.8 %copy-start.1 = (bf16[8,8,256,256]{3,2,1,0:T(8,128)(2,1)S(1)}, bf16[8,8,256,256]{3,2,1,0:T(8,128)(2,1)}, u32[]{:S(2)}) copy-start(bf16[8,8,256,256]{3,2,1,0:T(8,128)(2,1)} %blocks.5) | copy-start | bytes 25165828
  19.3 20.1 %copy-start.3 = (f32[8,64,256]{2,1,0:T(8,128)S(1)}, f32[8,64,256]{2,1,0:T(8,128)}, u32[]{:S(2)}) copy-start(f32[8,64,256]{2,1,0:T(8,128)} %v0.1) | copy-start | bytes 1572868
  19.3 20.1 %copy-start.4 = (f32[64,8,256]{2,1,0:T(8,128)S(1)}, f32[64,8,256]{2,1,0:T(8,128)}, u32[]{:S(2)}) copy-start(f32[64,8,256]{2,1,0:T(8,128)} %sketch.3) | copy-start | bytes 1572868
  21.6 7.5 %collective-permute-start.4 = (bf16[4,64,256]{2,1,0:T(8,128)(2,1)S(1)}, bf16[4,64,256]{2,1,0:T(8,128)(2,1)S(1)}, u32[]{:S(2)}, u32[]{:S(2)}) collective-permute-start(bf16[4,64,256]{2,1,0:T(8,128)(2,1)S(1)} %get-tuple-element.31), channel_id=1, source_target_pairs={{0,1},{1,0},{2,3},{3,2},{4,5},{5,4},{6,7},{7,6},{8,9},{9,8},{10,11... | collective-permute-start | bytes 393224 | tf_op jit(solution)/shard_map/ppermute | solution.py:166
  21.8 7.3 %collective-permute-start.5 = (bf16[4,64,256]{2,1,0:T(8,128)(2,1)S(1)}, bf16[4,64,256]{2,1,0:T(8,128)(2,1)S(1)}, u32[]{:S(2)}, u32[]{:S(2)}) collective-permute-start(bf16[4,64,256]{2,1,0:T(8,128)(2,1)S(1)} %get-tuple-element.32), channel_id=1, source_target_pairs={{1,2},{2,1},{3,4},{4,3},{5,6},{6,5},{7,8},{8,7},{9,10},{10,9},{11,... | collective-permute-start | bytes 393224 | tf_op jit(solution)/shard_map/ppermute | solution.py:165
  25.9 5.0 %collective-permute-start.6 = (bf16[4,64,256]{2,1,0:T(8,128)(2,1)S(1)}, bf16[4,64,256]{2,1,0:T(8,128)(2,1)S(1)}, u32[]{:S(2)}, u32[]{:S(2)}) collective-permute-start(bf16[4,64,256]{2,1,0:T(8,128)(2,1)S(1)} %get-tuple-element.33), channel_id=1, source_target_pairs={{0,32},{32,0},{64,96},{96,64},{128,160},{160,128},{192,224},{224,1... | collective-permute-start | bytes 393224 | tf_op jit(solution)/shard_map/ppermute | solution.py:164
  25.9 6.2 %collective-permute-start.7 = (bf16[4,64,256]{2,1,0:T(8,128)(2,1)S(1)}, bf16[4,64,256]{2,1,0:T(8,128)(2,1)S(1)}, u32[]{:S(2)}, u32[]{:S(2)}) collective-permute-start(bf16[4,64,256]{2,1,0:T(8,128)(2,1)S(1)} %get-tuple-element.34), channel_id=1, source_target_pairs={{32,64},{64,32},{96,128},{128,96},{160,192},{192,160},{224,0},{0,2... | collective-permute-start | bytes 393224 | tf_op jit(solution)/shard_map/ppermute | solution.py:163
  34.4 7.7 %collective-permute-start.8 = (bf16[4,64,256]{2,1,0:T(8,128)(2,1)S(1)}, bf16[4,64,256]{2,1,0:T(8,128)(2,1)S(1)}, u32[]{:S(2)}, u32[]{:S(2)}) collective-permute-start(bf16[4,64,256]{2,1,0:T(8,128)(2,1)S(1)} %get-tuple-element.37), channel_id=1, source_target_pairs={{0,1},{1,0},{2,3},{3,2},{4,5},{5,4},{6,7},{7,6},{8,9},{9,8},{10,11... | collective-permute-start | bytes 393224 | tf_op jit(solution)/shard_map/ppermute | solution.py:166
  34.5 7.6 %collective-permute-start.9 = (bf16[4,64,256]{2,1,0:T(8,128)(2,1)S(1)}, bf16[4,64,256]{2,1,0:T(8,128)(2,1)S(1)}, u32[]{:S(2)}, u32[]{:S(2)}) collective-permute-start(bf16[4,64,256]{2,1,0:T(8,128)(2,1)S(1)} %get-tuple-element.38), channel_id=1, source_target_pairs={{1,2},{2,1},{3,4},{4,3},{5,6},{6,5},{7,8},{8,7},{9,10},{10,9},{11,... | collective-permute-start | bytes 393224 | tf_op jit(solution)/shard_map/ppermute | solution.py:165
  36.1 6.0 %collective-permute-start.10 = (bf16[4,64,256]{2,1,0:T(8,128)(2,1)S(1)}, bf16[4,64,256]{2,1,0:T(8,128)(2,1)S(1)}, u32[]{:S(2)}, u32[]{:S(2)}) collective-permute-start(bf16[4,64,256]{2,1,0:T(8,128)(2,1)S(1)} %get-tuple-element.39), channel_id=1, source_target_pairs={{0,32},{32,0},{64,96},{96,64},{128,160},{160,128},{192,224},{224,1... | collective-permute-start | bytes 393224 | tf_op jit(solution)/shard_map/ppermute | solution.py:164
  36.3 6.2 %collective-permute-start.11 = (bf16[4,64,256]{2,1,0:T(8,128)(2,1)S(1)}, bf16[4,64,256]{2,1,0:T(8,128)(2,1)S(1)}, u32[]{:S(2)}, u32[]{:S(2)}) collective-permute-start(bf16[4,64,256]{2,1,0:T(8,128)(2,1)S(1)} %get-tuple-element.40), channel_id=1, source_target_pairs={{32,64},{64,32},{96,128},{128,96},{160,192},{192,160},{224,0},{0,2... | collective-permute-start | bytes 393224 | tf_op jit(solution)/shard_map/ppermute | solution.py:163
  45.1 1.3 %collective-permute-start.12 = (f32[2,64,128]{2,1,0:T(8,128)S(1)}, f32[2,64,128]{2,1,0:T(8,128)S(1)}, u32[]{:S(2)}, u32[]{:S(2)}) collective-permute-start(f32[2,64,128]{2,1,0:T(8,128)S(1)} %get-tuple-element.45), channel_id=1, source_target_pairs={{0,1},{1,0},{2,3},{3,2},{4,5},{5,4},{6,7},{7,6},{8,9},{9,8},{10,11... | collective-permute-start | bytes 196616 | tf_op jit(solution)/shard_map/ppermute | solution.py:180
  46.4 5.2 %collective-permute-start.15 = (f32[2,64,128]{2,1,0:T(8,128)S(1)}, f32[2,64,128]{2,1,0:T(8,128)S(1)}, u32[]{:S(2)}, u32[]{:S(2)}) collective-permute-start(f32[2,64,128]{2,1,0:T(8,128)S(1)} %add.30), channel_id=1, source_target_pairs={{0,6},{2,0},{4,2},{6,4},{1,7},{3,1},{5,3},{7,5},{8,14},{10,8},{12,... | collective-permute-start | bytes 196616 | tf_op jit(solution)/shard_map/ppermute | solution.py:172
  49.3 5.8 %collective-permute-start.14 = (f32[2,64,128]{2,1,0:T(8,128)S(1)}, f32[2,64,128]{2,1,0:T(8,128)S(1)}, u32[]{:S(2)}, u32[]{:S(2)}) collective-permute-start(f32[2,64,128]{2,1,0:T(8,128)S(1)} %add.30), channel_id=1, source_target_pairs={{0,4},{2,6},{4,0},{6,2},{1,5},{3,7},{5,1},{7,3},{8,12},{10,14},{12... | collective-permute-start | bytes 196616 | tf_op jit(solution)/shard_map/ppermute | solution.py:172
  49.3 5.8 %collective-permute-start.13 = (f32[2,64,128]{2,1,0:T(8,128)S(1)}, f32[2,64,128]{2,1,0:T(8,128)S(1)}, u32[]{:S(2)}, u32[]{:S(2)}) collective-permute-start(f32[2,64,128]{2,1,0:T(8,128)S(1)} %add.30), channel_id=1, source_target_pairs={{0,2},{2,4},{4,6},{6,0},{1,3},{3,5},{5,7},{7,1},{8,10},{10,12},{12... | collective-permute-start | bytes 196616 | tf_op jit(solution)/shard_map/ppermute | solution.py:172
  55.1 4.3 %collective-permute-start.18 = (f32[2,64,128]{2,1,0:T(8,128)S(1)}, f32[2,64,128]{2,1,0:T(8,128)S(1)}, u32[]{:S(2)}, u32[]{:S(2)}) collective-permute-start(f32[2,64,128]{2,1,0:T(8,128)S(1)} %add_add_fusion.1), channel_id=1, source_target_pairs={{0,24},{8,0},{16,8},{24,16},{1,25},{9,1},{17,9},{25,17},{2,26},{10... | collective-permute-start | bytes 196616 | tf_op jit(solution)/shard_map/ppermute | solution.py:172
  55.9 5.8 %collective-permute-start.17 = (f32[2,64,128]{2,1,0:T(8,128)S(1)}, f32[2,64,128]{2,1,0:T(8,128)S(1)}, u32[]{:S(2)}, u32[]{:S(2)}) collective-permute-start(f32[2,64,128]{2,1,0:T(8,128)S(1)} %add_add_fusion.1), channel_id=1, source_target_pairs={{0,16},{8,24},{16,0},{24,8},{1,17},{9,25},{17,1},{25,9},{2,18},{10... | collective-permute-start | bytes 196616 | tf_op jit(solution)/shard_map/ppermute | solution.py:172
  56.4 6.0 %collective-permute-start.16 = (f32[2,64,128]{2,1,0:T(8,128)S(1)}, f32[2,64,128]{2,1,0:T(8,128)S(1)}, u32[]{:S(2)}, u32[]{:S(2)}) collective-permute-start(f32[2,64,128]{2,1,0:T(8,128)S(1)} %add_add_fusion.1), channel_id=1, source_target_pairs={{0,8},{8,16},{16,24},{24,0},{1,9},{9,17},{17,25},{25,1},{2,10},{10... | collective-permute-start | bytes 196616 | tf_op jit(solution)/shard_map/ppermute | solution.py:172
  62.4 4.6 %collective-permute-start.19 = (f32[2,64,128]{2,1,0:T(8,128)S(1)}, f32[2,64,128]{2,1,0:T(8,128)S(1)}, u32[]{:S(2)}, u32[]{:S(2)}) collective-permute-start(f32[2,64,128]{2,1,0:T(8,128)S(1)} %add_add_fusion), channel_id=1, source_target_pairs={{0,32},{32,0},{64,96},{96,64},{128,160},{160,128},{192,224},{224,1... | collective-permute-start | bytes 196616 | tf_op jit(solution)/shard_map/ppermute | solution.py:180
  67.0 6.0 %collective-permute-start.20 = (f32[2,64,128]{2,1,0:T(8,128)S(1)}, f32[2,64,128]{2,1,0:T(8,128)S(1)}, u32[]{:S(2)}, u32[]{:S(2)}) collective-permute-start(f32[2,64,128]{2,1,0:T(8,128)S(1)} %add.37), channel_id=1, source_target_pairs={{0,64},{32,96},{64,0},{96,32},{128,192},{160,224},{192,128},{224,1... | collective-permute-start | bytes 196616 | tf_op jit(solution)/shard_map/ppermute | solution.py:180
  73.0 8.3 %collective-permute-start.21 = (f32[2,64,128]{2,1,0:T(8,128)S(1)}, f32[2,64,128]{2,1,0:T(8,128)S(1)}, u32[]{:S(2)}, u32[]{:S(2)}) collective-permute-start(f32[2,64,128]{2,1,0:T(8,128)S(1)} %add.38), channel_id=1, source_target_pairs={{0,128},{32,160},{64,192},{96,224},{128,0},{160,32},{192,64},{224,... | collective-permute-start | bytes 196616 | tf_op jit(solution)/shard_map/ppermute | solution.py:180

commit v2 on v1

--- a/solution.py
+++ b/solution.py
@@ -12,6 +12,7 @@
 F32, BF16 = jnp.float32, jnp.bfloat16
 VMEM = pl.BlockSpec(memory_space=pltpu.VMEM)
 SMEM = pl.BlockSpec(memory_space=pltpu.SMEM)
+HBM = pl.BlockSpec(memory_space=pltpu.HBM)
 
 
 def call(kernel, name, ins, outs, scratch=(), flops=0, nbytes=0, out_specs=None):
@@ -27,6 +28,10 @@
     )
 
 
+def in_hbm(x):
+    return pltpu.with_memory_space_constraint(x, pltpu.HBM)
+
+
 def parities():
     return lax.axis_index("core"), lax.rem(lax.axis_index("gx"), 2)
 
@@ -44,10 +49,20 @@
             out[j] = rows[send[0, direction, j]]
 
 
-def first_kernel(send, start, x_out, *outs):
+def copy_all(pairs, sems):
+    copies = [pltpu.make_async_copy(source, target, sems.at[n]) for n, (source, target) in enumerate(pairs)]
+    for copy in copies:
+        copy.start()
+    return copies
+
+
+def first_kernel(send_hbm, start_hbm, v_out, send_out, x_out, oa, ob, oc, od, send, sems):
+    copies = copy_all(((send_hbm, send), (start_hbm, v_out), (send_hbm, send_out)), sems)
     side, layer = parities()
-    x_out[...] = start[...].astype(BF16)
-    fill_messages(send, x_out, outs, side, layer)
+    for copy in copies:
+        copy.wait()
+    x_out[...] = v_out[...].astype(BF16)
+    fill_messages(send, x_out, (oa, ob, oc, od), side, layer)
 
 
 def place_rows(x, received, src, side, layer):
@@ -67,7 +82,7 @@
     return jnp.dot(jnp.concatenate(picked, axis=1), tall, preferred_element_type=F32)
 
 
-def step_kernel(cols, live, send, x, ra, rb, rc, rd, blocks, v_out, x_out, oa, ob, oc, od, src):
+def step_kernel(cols, live, send, x, rd, rc, ra, rb, blocks, v_out, x_out, oa, ob, oc, od, src):
     side, layer = parities()
     place_rows(x, (ra, rb, rc, rd), src, side, layer)
     for i in range(x.shape[0]):
@@ -96,32 +111,87 @@
     )
 
 
-def prepare_kernel(sketch, start, high, low, w_out):
-    for i in range(start.shape[0]):
+def prepare_kernel(
+    blocks_hbm, sketch_hbm, cols_hbm, live_hbm, start, blocks, cols, live, high, low, w_out, sketch, sems
+):
+    rows = start.shape[0]
+    pairs = [(sketch_hbm, sketch)]
+    pairs += [(blocks_hbm.at[i], blocks.at[i]) for i in range(rows)]
+    pairs += [(cols_hbm, cols), (live_hbm, live)]
+    copies = copy_all(pairs, sems)
+    copies[0].wait()
+    for i in range(rows):
         high[i], low[i] = halves(sketch[:, i, :])
     w_out[...] = sketched(start, high, low)
+    for copy in copies[1:]:
+        copy.wait()
 
 
 def sketch_kernel(v, high, low, w_out):
     w_out[...] = sketched(v, high, low)
 
 
-def last_kernel(cols, live, x, ra, rb, rc, rd, blocks, high, low, w0, w1, w2, v_out, w_out, src):
+def spread_kernel(low_row, high_row, cols, live, high, blocks, *refs):
+    z = refs[-1]
+    dead = z.shape[0] - 1
+    if low_row == 0:
+        z[...] = jnp.zeros(z.shape, z.dtype)
+    else:
+        z[...] = refs[0][...]
+    for i in range(low_row, high_row):
+        for k in range(cols.shape[1]):
+            column = jnp.where(k < live[i], cols[i, k], dead)
+            z[column] += lax.dot_general(
+                high[i], blocks[i, k], (((1,), (1,)), ((), ())), preferred_element_type=F32
+            )
+
+
+def against(rows, z_rows):
+    left, right = [], []
+    for row, z_row in zip(rows, z_rows, strict=True):
+        left += [row, row]
+        right += list(halves(z_row))
+    return lax.dot_general(
+        jnp.concatenate(left, axis=1),
+        jnp.concatenate(right, axis=1),
+        (((1,), (1,)), ((), ())),
+        preferred_element_type=F32,
+    )
+
+
+def own_kernel(x, z, w_out):
+    own = range(x.shape[0])
+    w_out[...] = against([x[e] for e in own], [z[e] for e in own])
+
+
+def gather_kernel(rd, rc, ra, rb, z, w0, w1, w2, own, w_out):
+    side, layer = parities()
+    numbers, _ = directions(side, layer)
+    width = ra.shape[0]
+    count = z.shape[0] - 1 - 4 * width
+    rows, z_rows = [], []
+    for ref, direction in zip((ra, rb, rc, rd), numbers, strict=True):
+        rows += [ref[j] for j in range(width)]
+        z_rows += [z[count + direction * width + j] for j in range(width)]
+    w_out[0] = jnp.concatenate([w0[...], w1[...]], axis=1)
+    w_out[1] = jnp.concatenate([w2[...], own[...] + against(rows, z_rows)], axis=1)
+
+
+def last_kernel(cols, live, x, rd, rc, ra, rb, blocks, v_out, src):
     side, layer = parities()
     place_rows(x, (ra, rb, rc, rd), src, side, layer)
     for i in range(x.shape[0]):
         v_out[i] = product_of_row(i, cols, live, src, blocks)
-    w3 = sketched(v_out, high, low)
-    w_out[0] = jnp.concatenate([w0[...], w1[...]], axis=1)
-    w_out[1] = jnp.concatenate([w2[...], w3], axis=1)
 
 
 def final_kernel(v0, v1, v2, v3, w, basis, factor_out, out, sems):
     count = 4
     size = w.shape[2] // 2
     sums = [w[s // 2][:, (s % 2) * size : (s % 2 + 1) * size] for s in range(count)]
-    columns, factor, inverse = [], {}, []
-    for s in range(count):
+    columns, inverse, factor, copies = [], [], {}, []
+    vectors = (v0, v1, v2, v3)
+
+    def add_column(s):
         residue = sums[s]
         for m in range(s):
             factor[m, s] = jnp.sum(columns[m] * sums[s], axis=1, keepdims=True)
@@ -129,15 +199,21 @@
         factor[s, s] = jnp.sqrt(jnp.sum(residue * residue, axis=1, keepdims=True) + 1e-06)
         inverse.append(1.0 / factor[s, s])
         columns.append(residue * inverse[s])
-    copies = []
-    for s, v in enumerate((v0, v1, v2, v3)):
-        for i in range(v.shape[0]):
-            total = v[i]
+
+    def write_basis(s):
+        for i in range(v0.shape[0]):
+            total = vectors[s][i]
             for m in range(s):
                 total = total - factor[m, s] * out[m, i]
             out[s, i] = total * inverse[s]
         copies.append(pltpu.make_async_copy(out.at[s], basis.at[s], sems.at[s]))
         copies[-1].start()
+
+    add_column(0)
+    for s in range(1, count):
+        add_column(s)
+        write_basis(s - 1)
+    write_basis(count - 1)
     lane = lax.broadcasted_iota(jnp.int32, (w.shape[1], 128), 1)
     table = jnp.zeros((w.shape[1], 128), F32)
     for (m, s), value in factor.items():
@@ -162,30 +238,37 @@
     gy, gx = lax.axis_size(GY), lax.axis_size("gx")
     rd = lax.ppermute(od, "gx", swaps(gx, 1))
     rc = lax.ppermute(oc, "gx", swaps(gx, 0))
+    ra = lax.ppermute(oa, GY, swaps(gy, 0))
     rb = lax.ppermute(ob, GY, swaps(gy, 1))
-    ra = lax.ppermute(oa, GY, swaps(gy, 0))
-    return ra, rb, rc, rd
-
-
-def shifted_sum(x, axis):
+    return rd, rc, ra, rb
+
+
+def rounded_to(x):
+    return lax.reduce_precision(x, 8, 7)
+
+
+def ring_sum(x, axis):
     count = lax.axis_size(axis)
-    parts = [lax.ppermute(x, axis, [(i, (i + k) % count) for i in range(count)]) for k in range(1, count)]
-    return sum(parts, x)
+    x = rounded_to(x)
+    sent = x.astype(BF16)
+    parts = [lax.ppermute(sent, axis, [(i, i ^ k) for i in range(count)]).astype(F32) for k in range(1, count)]
+    return (parts[0] + parts[2]) + (x + parts[1])
 
 
 def doubled_sum(x, axis):
     count = lax.axis_size(axis)
     k = 1
     while k < count:
-        x = x + lax.ppermute(x, axis, [(i, i ^ k) for i in range(count)])
+        x = rounded_to(x)
+        x = x + lax.ppermute(x.astype(BF16), axis, [(i, i ^ k) for i in range(count)]).astype(F32)
         k *= 2
     return x
 
 
 def summed(x):
-    x = doubled_sum(x, "core")
-    x = shifted_sum(x, "y1")
-    x = shifted_sum(x, "y0")
+    x = x + lax.ppermute(x, "core", [(0, 1), (1, 0)])
+    x = ring_sum(x, "y1")
+    x = ring_sum(x, "y0")
     return doubled_sum(x, "gx")
 
 
@@ -202,38 +285,89 @@
     flops = 2 * rows * slots * rhs * size * size
     sketch_flops = 6 * rows * rhs * size * count
 
-    x, *messages = call(
-        first_kernel, "first", [SMEM, VMEM], [rounded] + [message] * 4, flops=1 << 20, nbytes=1 << 20
-    )(send_rows, start)
+    v0, send, x, *messages = call(
+        first_kernel,
+        "first",
+        [HBM] * 2,
+        [vector, jax.ShapeDtypeStruct(send_rows.shape, jnp.int32), rounded] + [message] * 4,
+        [pltpu.SMEM(send_rows.shape, jnp.int32), pltpu.SemaphoreType.DMA((3,))],
+        flops=1 << 20,
+        nbytes=1 << 20,
+    )(in_hbm(send_rows), in_hbm(start))
     received = exchange(messages)
-    high, low, w0 = call(
-        prepare_kernel, "prepare", [VMEM] * 2, [rounded] * 2 + [part], flops=sketch_flops, nbytes=1 << 20
-    )(sketch, start)
-    step = call(
-        step_kernel,
-        "step",
-        [SMEM] * 3 + [VMEM] * 6,
-        [vector, rounded] + [message] * 4,
+    here, cols, live, high, low, w0 = call(
+        prepare_kernel,
+        "prepare",
+        [HBM] * 4 + [VMEM],
+        [
+            jax.ShapeDtypeStruct(blocks.shape, BF16),
+            jax.ShapeDtypeStruct(block_cols.shape, jnp.int32),
+            jax.ShapeDtypeStruct(live_blocks.shape, jnp.int32),
+            rounded,
+            rounded,
+            part,
+        ],
+        [pltpu.VMEM(sketch.shape, F32), pltpu.SemaphoreType.DMA((rows + 3,))],
+        flops=sketch_flops,
+        nbytes=blocks.size * 2,
+    )(in_hbm(blocks), in_hbm(sketch), in_hbm(block_cols), in_hbm(live_blocks), v0)
+
+    def step(x, received, *earlier):
+        inputs = (cols, live, send, x, *received, here)
+
+        def kernel(*refs):
+            step_kernel(*refs[: len(inputs)], *refs[len(inputs) + len(earlier) :])
+
+        return call(
+            kernel,
+            "step",
+            [SMEM] * 3 + [VMEM] * (6 + len(earlier)),
+            [vector, rounded] + [message] * 4,
+            [src],
+            flops=flops,
+            nbytes=blocks.size * 2,
+        )(*inputs, *earlier)
+
+    sketch_of = call(sketch_kernel, "sketch", [VMEM] * 3, [part], flops=sketch_flops, nbytes=1 << 20)
+    v1, x, *messages = step(x, received)
+    received = exchange(messages)
+    (w1,) = sketch_of(v1, high, low)
+    half = rows // 2
+    table = jax.ShapeDtypeStruct((src.shape[0], count, size), F32)
+
+    def spread(name, low_row, high_row, extra):
+        return call(
+            lambda *refs: spread_kernel(low_row, high_row, *refs),
+            name,
+            [SMEM] * 2 + [VMEM] * (2 + extra),
+            [table],
+            flops=flops,
+            nbytes=blocks.size,
+        )
+
+    (z,) = spread("spread", 0, half, 0)(cols, live, high, here)
+    v2, x, *messages = step(x, received, z, w1)
+    received = exchange(messages)
+    (w2,) = sketch_of(v2, high, low)
+    (z,) = spread("respread", half, rows, 1)(cols, live, high, here, z)
+    (own,) = call(own_kernel, "own", [VMEM] * 2, [part], flops=sketch_flops, nbytes=1 << 20)(x, z)
+    (w,) = call(
+        gather_kernel,
+        "gather",
+        [VMEM] * 9,
+        [jax.ShapeDtypeStruct((2, rhs, 2 * count), F32)],
+        flops=sketch_flops,
+        nbytes=1 << 20,
+    )(*received, z, w0, w1, w2, own)
+    (v3,) = call(
+        last_kernel,
+        "last",
+        [SMEM] * 2 + [VMEM] * 6,
+        [vector],
         [src],
         flops=flops,
         nbytes=blocks.size * 2,
-    )
-    sketch_of = call(sketch_kernel, "sketch", [VMEM] * 3, [part], flops=sketch_flops, nbytes=1 << 20)
-    v1, x, *messages = step(block_cols, live_blocks, send_rows, x, *received, blocks)
-    received = exchange(messages)
-    (w1,) = sketch_of(v1, high, low)
-    v2, x, *messages = step(block_cols, live_blocks, send_rows, x, *received, blocks)
-    received = exchange(messages)
-    (w2,) = sketch_of(v2, high, low)
-    v3, w = call(
-        last_kernel,
-        "last",
-        [SMEM] * 2 + [VMEM] * 11,
-        [vector, jax.ShapeDtypeStruct((2, rhs, 2 * count), F32)],
-        [src],
-        flops=flops + sketch_flops,
-        nbytes=blocks.size * 2,
-    )(block_cols, live_blocks, x, *received, blocks, high, low, w0, w1, w2)
+    )(cols, live, x, *received, here)
     w = summed(w)
     basis, factor = call(
         final_kernel,
@@ -247,7 +381,7 @@
         flops=1 << 22,
         nbytes=1 << 22,
         out_specs=[pl.BlockSpec(memory_space=pl.ANY), VMEM],
-    )(start, v1, v2, v3, w)
+    )(v0, v1, v2, v3, w)
     return basis, factor
 
 

time: 84.3 us -> 76 us (0.902)
  waiting for transfers between devices: 30.2 us -> 20 us
  Pallas kernels: 13.2 us -> 19.8 us
  local copies, waits for them, and re-layouts: 6.46 us -> 0 us
  starting transfers between devices: 33.2 us -> 34.7 us
    pallas_call x5 -> x9, Pallas kernels: 9.81 us -> 16.4 us  [the longest x2 4.61 us: step(): call(kernel, 'step', [SMEM] * 3 + [VMEM] * (6 + len(earlier)), [vector, r...]
    unnamed x20 -> x0, local copies, waits for them, and re-layouts: 6.46 us -> none
    ppermute x3, waiting for transfers between devices: 5.62 us -> 0.01 us  [exchange(): rd = lax.ppermute(od, 'gx', swaps(gx, 1))]
    ppermute x10, waiting for transfers between devices: 22.8 us -> 19 us  [the longest x3 11.8 us: doubled_sum(): lax.ppermute(x.astype(BF16), axis, [(i, i ^ k) for i in range(count)])]
    ppermute x3, starting transfers between devices: 11.3 us -> 7.83 us  [exchange(): rd = lax.ppermute(od, 'gx', swaps(gx, 1))]
    ppermute x3, starting transfers between devices: 0.32 us -> 2.78 us  [exchange(): rc = lax.ppermute(oc, 'gx', swaps(gx, 0))]
    ppermute x3, starting transfers between devices: 7.96 us -> 10.4 us  [exchange(): rb = lax.ppermute(ob, GY, swaps(gy, 1))]
    ppermute x3, waiting for transfers between devices: 1.73 us -> 0.73 us  [exchange(): rc = lax.ppermute(oc, 'gx', swaps(gx, 0))]
  transfers between devices with their start and end apart: 22 -> 22, of which waited for: 13 -> 10; matrix products, arithmetic and copies ran while one was open for 0% -> 0% of each run, Pallas kernels for 3% -> 14%
where the time goes in v2:
time: 76 us; the launch traced here: 75.6 us
  starting transfers between devices  34.7 us (46%)
  waiting for transfers between devices  20 us (26%)
  Pallas kernels  19.8 us (26%)
  between operations  0.99 us (1%)
    ppermute x3, waiting for transfers between devices, doubled_sum(): lax.ppermute(x.astype(BF16), axis, [(i, i ^ k) for i in range(count)])  11.8 us
    ppermute x3, starting transfers between devices, exchange(): rb = lax.ppermute(ob, GY, swaps(gy, 1))  10.4 us
    ppermute x6, starting transfers between devices, ring_sum(): lax.ppermute(sent, axis, [(i, i ^ k) for i in range(count)]).astype(F32)  10 us
    ppermute x3, starting transfers between devices, exchange(): rd = lax.ppermute(od, 'gx', swaps(gx, 1))  7.83 us
    ppermute x6, waiting for transfers between devices, ring_sum(): lax.ppermute(sent, axis, [(i, i ^ k) for i in range(count)]).astype(F32)  6 us
    pallas_call x2, Pallas kernels, step(): call(kernel, 'step', [SMEM] * 3 + [VMEM] * (6 + len(earlier)), [vector, r...  4.61 us
    pallas_call x1, Pallas kernels, on_device(): call(prepare_kernel, 'prepare', [HBM] * 4 + [VMEM], [jax.ShapeDtypeStruct...  3.66 us
    ppermute x3, starting transfers between devices, doubled_sum(): lax.ppermute(x.astype(BF16), axis, [(i, i ^ k) for i in range(count)])  3.15 us
  transfers between devices with their start and end apart: 22, of which 10 were waited for; matrix products, arithmetic and copies ran while one was open for 0% of the time, Pallas kernels for 14%

profile of v2, /device:TPU:8, one launch (start us, length us, event | category | flops | bytes accessed | tf_op | source)
XLA Modules:
  0.0 75.6 jit_solution(2471734140969681788)
XLA Ops:
  0.6 1.1 %first.1 = (f32[8,64,256]{2,1,0:T(8,128)S(1)}, s32[1,4,4]{2,1,0:T(4,128)S(1)}, bf16[8,64,256]{2,1,0:T(8,128)(2,1)S(1)}, bf16[4,64,256]{2,1,0:T(8,128)(2,1)S(1)},...) custom-call(s32[1,4,4]{2,1,0:T(4,128)} %send_hbm.1, ...), custom_call_target="tpu_custom_call" | custom-call | flops 1048576 | bytes 1048576 | tf_op jit(solution)/shard_map/first/pallas_call | solution.py:288
  1.8 5.9 %collective-permute-start = (bf16[4,64,256]{2,1,0:T(8,128)(2,1)S(1)}, bf16[4,64,256]{2,1,0:T(8,128)(2,1)S(1)}, u32[]{:S(2)}, u32[]{:S(2)}) collective-permute-start(bf16[4,64,256]{2,1,0:T(8,128)(2,1)S(1)} %get-tuple-element.32), channel_id=1, source_target_pairs={{32,64},{64,32},{96,128},{128,96},{160,192},{192,160},{224,0},{0,2... | collective-permute-start | bytes 393224 | tf_op jit(solution)/shard_map/ppermute | solution.py:239
  7.7 0.6 collective-permute-start.3
  8.3 3.7 %prepare.1 = (bf16[8,8,256,256]{3,2,1,0:T(8,128)(2,1)S(1)}, s32[8,8]{1,0:T(8,128)S(1)}, s32[8]{0:T(128)S(1)}, bf16[8,64,256]{2,1,0:T(8,128)(2,1)S(1)}, bf16[8,64...) custom-call(bf16[8,8,256,256]{3,2,1,0:T(8,128)(2,1)} %blocks_hbm.1, f32[64,8,256]{2,1,0:T(8,128)} %sketch_hbm.1, ...), custom_call_target="tpu_custom_call" | custom-call | flops 50331648 | bytes 8388608 | tf_op jit(solution)/shard_map/prepare/pallas_call | solution.py:298
  12.0 0.7 collective-permute-done.1.refs_5_
  12.7 2.3 %step.2 = (f32[8,64,256]{2,1,0:T(8,128)S(1)}, bf16[8,64,256]{2,1,0:T(8,128)(2,1)S(1)}, bf16[4,64,256]{2,1,0:T(8,128)(2,1)S(1)}, bf16[4,64,256]{2,1,0:T(8,128)(2,...) custom-call(s32[8,8]{1,0:T(8,128)S(1)} %get-tuple-element.28.refs_0_.cols, ...), custom_call_target="tpu_custom_call" | custom-call | flops 536870912 | bytes 8388608 | tf_op jit(solution)/shard_map/step/pallas_call | solution.py:321
  15.0 1.6 %collective-permute-start.4 = (bf16[4,64,256]{2,1,0:T(8,128)(2,1)S(1)}, bf16[4,64,256]{2,1,0:T(8,128)(2,1)S(1)}, u32[]{:S(2)}, u32[]{:S(2)}) collective-permute-start(bf16[4,64,256]{2,1,0:T(8,128)(2,1)S(1)} %get-tuple-element.39), channel_id=1, source_target_pairs={{32,64},{64,32},{96,128},{128,96},{160,192},{192,160},{224,0},{0,2... | collective-permute-start | bytes 393224 | tf_op jit(solution)/shard_map/ppermute | solution.py:239
  16.6 1.0 %collective-permute-start.5 = (bf16[4,64,256]{2,1,0:T(8,128)(2,1)S(1)}, bf16[4,64,256]{2,1,0:T(8,128)(2,1)S(1)}, u32[]{:S(2)}, u32[]{:S(2)}) collective-permute-start(bf16[4,64,256]{2,1,0:T(8,128)(2,1)S(1)} %get-tuple-element.40), channel_id=1, source_target_pairs={{0,32},{32,0},{64,96},{96,64},{128,160},{160,128},{192,224},{224,1... | collective-permute-start | bytes 393224 | tf_op jit(solution)/shard_map/ppermute | solution.py:240
  17.5 0.4 collective-permute-start.6
  18.0 4.8 %collective-permute-start.7 = (bf16[4,64,256]{2,1,0:T(8,128)(2,1)S(1)}, bf16[4,64,256]{2,1,0:T(8,128)(2,1)S(1)}, u32[]{:S(2)}, u32[]{:S(2)}) collective-permute-start(bf16[4,64,256]{2,1,0:T(8,128)(2,1)S(1)} %get-tuple-element.42), channel_id=1, source_target_pairs={{1,2},{2,1},{3,4},{4,3},{5,6},{6,5},{7,8},{8,7},{9,10},{10,9},{11,... | collective-permute-start | bytes 393224 | tf_op jit(solution)/shard_map/ppermute | solution.py:242
  22.7 2.0 %spread.1.refs_9_.refs_4_ = f32[25,64,256]{2,1,0:T(8,128)S(1)} custom-call(s32[8,8]{1,0:T(8,128)S(1)} %get-tuple-element.28.refs_0_.cols, s32[8]{0:T(128)S(1)} %get-tuple-element.29.refs_1_.live, bf16[8,64,256]{2,1,0:T(8,128)(2,1)S(1)} %get-tuple-element.43.refs_2_.high, bf16[8,8,256,256]{3,2,1,0:T(8,128)(2,1)S(1)} %get-tuple-element.36.refs_8_.refs_3_.blocks), custom_call_target="tpu_custom_call" | custom-call | flops 536870912 | bytes 4194304 | tf_op jit(solution)/shard_map/spread/pallas_call | solution.py:348
  25.4 2.3 %step.3 = (f32[8,64,256]{2,1,0:T(8,128)S(1)}, bf16[8,64,256]{2,1,0:T(8,128)(2,1)S(1)}, bf16[4,64,256]{2,1,0:T(8,128)(2,1)S(1)}, bf16[4,64,256]{2,1,0:T(8,128)(2,...) custom-call(s32[8,8]{1,0:T(8,128)S(1)} %get-tuple-element.28.refs_0_.cols, ...), custom_call_target="tpu_custom_call" | custom-call | flops 536870912 | bytes 8388608 | tf_op jit(solution)/shard_map/step/pallas_call | solution.py:321
  28.0 1.8 %collective-permute-start.9 = (bf16[4,64,256]{2,1,0:T(8,128)(2,1)S(1)}, bf16[4,64,256]{2,1,0:T(8,128)(2,1)S(1)}, u32[]{:S(2)}, u32[]{:S(2)}) collective-permute-start(bf16[4,64,256]{2,1,0:T(8,128)(2,1)S(1)} %get-tuple-element.48), channel_id=1, source_target_pairs={{0,32},{32,0},{64,96},{96,64},{128,160},{160,128},{192,224},{224,1... | collective-permute-start | bytes 393224 | tf_op jit(solution)/shard_map/ppermute | solution.py:240
  29.8 5.1 %collective-permute-start.11 = (bf16[4,64,256]{2,1,0:T(8,128)(2,1)S(1)}, bf16[4,64,256]{2,1,0:T(8,128)(2,1)S(1)}, u32[]{:S(2)}, u32[]{:S(2)}) collective-permute-start(bf16[4,64,256]{2,1,0:T(8,128)(2,1)S(1)} %get-tuple-element.50), channel_id=1, source_target_pairs={{1,2},{2,1},{3,4},{4,3},{5,6},{6,5},{7,8},{8,7},{9,10},{10,9},{11,... | collective-permute-start | bytes 393224 | tf_op jit(solution)/shard_map/ppermute | solution.py:242
  34.9 2.0 %respread.1.z = f32[25,64,256]{2,1,0:T(8,128)S(1)} custom-call(s32[8,8]{1,0:T(8,128)S(1)} %get-tuple-element.28.refs_0_.cols, s32[8]{0:T(128)S(1)} %get-tuple-element.29.refs_1_.live, bf16[8,64,256]{2,1,0:T(8,128)(2,1)S(1)} %get-tuple-element.43.refs_2_.high, bf16[8,8,256,256]{3,2,1,0:T(8,128)(2,1)S(1)} %get-tuple-element.36.refs_8_.refs_3_.blocks, ...), custom_call_target="tpu_custom_call" | custom-call | flops 536870912 | bytes 4194304 | tf_op jit(solution)/shard_map/respread/pallas_call | solution.py:352
  36.9 0.3 sketch.3.w2
  37.6 0.5 gather.1
  38.2 1.2 %collective-permute-done.12 = f32[2,64,128]{2,1,0:T(8,128)S(1)} collective-permute-done((f32[2,64,128]{2,1,0:T(8,128)S(1)}, f32[2,64,128]{2,1,0:T(8,128)S(1)}, u32[]{:S(2)}, u32[]{:S(2)}) %collective-permute-start.12) | collective-permute-done | bytes 65568 | tf_op jit(solution)/shard_map/ppermute | solution.py:269
  39.5 0.9 %collective-permute-start.15 = (bf16[2,64,128]{2,1,0:T(8,128)(2,1)S(1)}, bf16[2,64,128]{2,1,0:T(8,128)(2,1)S(1)}, u32[]{:S(2)}, u32[]{:S(2)}) collective-permute-start(bf16[2,64,128]{2,1,0:T(8,128)(2,1)S(1)} %fusion.1), channel_id=1, source_target_pairs={{0,4},{2,6},{4,0},{6,2},{1,5},{3,7},{5,1},{7,3},{8,12},{10,14},{12... | collective-permute-start | bytes 98312 | tf_op jit(solution)/shard_map/ppermute | solution.py:254
  40.4 5.5 %collective-permute-start.14 = (bf16[2,64,128]{2,1,0:T(8,128)(2,1)S(1)}, bf16[2,64,128]{2,1,0:T(8,128)(2,1)S(1)}, u32[]{:S(2)}, u32[]{:S(2)}) collective-permute-start(bf16[2,64,128]{2,1,0:T(8,128)(2,1)S(1)} %fusion.1), channel_id=1, source_target_pairs={{0,6},{2,4},{4,2},{6,0},{1,7},{3,5},{5,3},{7,1},{8,14},{10,12},{12... | collective-permute-start | bytes 98312 | tf_op jit(solution)/shard_map/ppermute | solution.py:254
  45.9 1.9 %collective-permute-done.14 = bf16[2,64,128]{2,1,0:T(8,128)(2,1)S(1)} collective-permute-done((bf16[2,64,128]{2,1,0:T(8,128)(2,1)S(1)}, bf16[2,64,128]{2,1,0:T(8,128)(2,1)S(1)}, u32[]{:S(2)}, u32[]{:S(2)}) %collective-permute-start.14) | collective-permute-done | bytes 32800 | tf_op jit(solution)/shard_map/ppermute | solution.py:254
  47.8 2.0 %collective-permute-done.13 = bf16[2,64,128]{2,1,0:T(8,128)(2,1)S(1)} collective-permute-done((bf16[2,64,128]{2,1,0:T(8,128)(2,1)S(1)}, bf16[2,64,128]{2,1,0:T(8,128)(2,1)S(1)}, u32[]{:S(2)}, u32[]{:S(2)}) %collective-permute-start.13) | collective-permute-done | bytes 32800 | tf_op jit(solution)/shard_map/ppermute | solution.py:254
  50.0 0.9 %collective-permute-start.17 = (bf16[2,64,128]{2,1,0:T(8,128)(2,1)S(1)}, bf16[2,64,128]{2,1,0:T(8,128)(2,1)S(1)}, u32[]{:S(2)}, u32[]{:S(2)}) collective-permute-start(bf16[2,64,128]{2,1,0:T(8,128)(2,1)S(1)} %get-tuple-element.54), channel_id=1, source_target_pairs={{0,24},{8,16},{16,8},{24,0},{1,25},{9,17},{17,9},{25,1},{2,26},{10... | collective-permute-start | bytes 98312 | tf_op jit(solution)/shard_map/ppermute | solution.py:254
  50.9 2.5 %collective-permute-start.16 = (bf16[2,64,128]{2,1,0:T(8,128)(2,1)S(1)}, bf16[2,64,128]{2,1,0:T(8,128)(2,1)S(1)}, u32[]{:S(2)}, u32[]{:S(2)}) collective-permute-start(bf16[2,64,128]{2,1,0:T(8,128)(2,1)S(1)} %get-tuple-element.54), channel_id=1, source_target_pairs={{0,8},{8,0},{16,24},{24,16},{1,9},{9,1},{17,25},{25,17},{2,10},{10... | collective-permute-start | bytes 98312 | tf_op jit(solution)/shard_map/ppermute | solution.py:254
  53.4 2.0 %collective-permute-done.18 = bf16[2,64,128]{2,1,0:T(8,128)(2,1)S(1)} collective-permute-done((bf16[2,64,128]{2,1,0:T(8,128)(2,1)S(1)}, bf16[2,64,128]{2,1,0:T(8,128)(2,1)S(1)}, u32[]{:S(2)}, u32[]{:S(2)}) %collective-permute-start.18) | collective-permute-done | bytes 32800 | tf_op jit(solution)/shard_map/ppermute | solution.py:254
  55.9 4.1 %collective-permute-done.19 = bf16[2,64,128]{2,1,0:T(8,128)(2,1)S(1)} collective-permute-done((bf16[2,64,128]{2,1,0:T(8,128)(2,1)S(1)}, bf16[2,64,128]{2,1,0:T(8,128)(2,1)S(1)}, u32[]{:S(2)}, u32[]{:S(2)}) %collective-permute-start.19) | collective-permute-done | bytes 32800 | tf_op jit(solution)/shard_map/ppermute | solution.py:263
  59.9 0.5 collective-permute-start.20
  60.4 4.4 %collective-permute-done.20 = bf16[2,64,128]{2,1,0:T(8,128)(2,1)S(1)} collective-permute-done((bf16[2,64,128]{2,1,0:T(8,128)(2,1)S(1)}, bf16[2,64,128]{2,1,0:T(8,128)(2,1)S(1)}, u32[]{:S(2)}, u32[]{:S(2)}) %collective-permute-start.20) | collective-permute-done | bytes 32800 | tf_op jit(solution)/shard_map/ppermute | solution.py:263
  64.9 2.4 %collective-permute-start.21 = (bf16[2,64,128]{2,1,0:T(8,128)(2,1)S(1)}, bf16[2,64,128]{2,1,0:T(8,128)(2,1)S(1)}, u32[]{:S(2)}, u32[]{:S(2)}) collective-permute-start(bf16[2,64,128]{2,1,0:T(8,128)(2,1)S(1)} %fusion.2), channel_id=1, source_target_pairs={{0,128},{32,160},{64,192},{96,224},{128,0},{160,32},{192,64},{224,... | collective-permute-start | bytes 98312 | tf_op jit(solution)/shard_map/ppermute | solution.py:263
  67.3 2.2 %last.1.v3 = f32[8,64,256]{2,1,0:T(8,128)S(1)} custom-call(s32[8,8]{1,0:T(8,128)S(1)} %get-tuple-element.28.refs_0_.cols, s32[8]{0:T(128)S(1)} %get-tuple-element.29.refs_1_.live, bf16[8,64,256]{2,1,0:T(8,128)(2,1)S(1)} %get-tuple-element.46.x, bf16[4,64,256]{2,1,0:T(8,128)(2,1)S(1)} %collective-permute-done.8.rd, ...), custom_call_target="tpu_custom_call" | custom-call | flops 536870912 | bytes 8388608 | tf_op jit(solution)/shard_map/last/pallas_call | solution.py:362
  69.5 3.3 %collective-permute-done.21 = bf16[2,64,128]{2,1,0:T(8,128)(2,1)S(1)} collective-permute-done((bf16[2,64,128]{2,1,0:T(8,128)(2,1)S(1)}, bf16[2,64,128]{2,1,0:T(8,128)(2,1)S(1)}, u32[]{:S(2)}, u32[]{:S(2)}) %collective-permute-start.21) | collective-permute-done | bytes 32800 | tf_op jit(solution)/shard_map/ppermute | solution.py:263
  72.8 2.6 %final.1 = (f32[4,8,64,256]{3,2,1,0:T(8,128)}, f32[4,4,64]{2,1,0:T(4,128)}) custom-call(f32[8,64,256]{2,1,0:T(8,128)S(1)} %get-tuple-element.27.start.v0, f32[8,64,256]{2,1,0:T(8,128)S(1)} %get-tuple-element.37.v.v1, f32[8,64,256]{2,1,0:T(8,128)S(1)} %get-tuple-element.45.v.v2, f32[8,64,256]{2,1,0:T(8,128)S(1)} %last.1.v3, f32[2,64,128]{2,1,0:T(8,128)S(1)} %convert_add_fusion.w), custom_call_target="tpu_custom_call" | custom-call | flops 4194304 | bytes 4194304 | tf_op jit(solution)/shard_map/final/pallas_call | solution.py:372
  (30 shorter events, 1.9 us)
Async XLA Ops:
  1.8 10.2 %collective-permute-start = (bf16[4,64,256]{2,1,0:T(8,128)(2,1)S(1)}, bf16[4,64,256]{2,1,0:T(8,128)(2,1)S(1)}, u32[]{:S(2)}, u32[]{:S(2)}) collective-permute-start(bf16[4,64,256]{2,1,0:T(8,128)(2,1)S(1)} %get-tuple-element.32), channel_id=1, source_target_pairs={{32,64},{64,32},{96,128},{128,96},{160,192},{192,160},{224,0},{0,2... | collective-permute-start | bytes 393224 | tf_op jit(solution)/shard_map/ppermute | solution.py:239
  7.7 5.0 %collective-permute-start.1 = (bf16[4,64,256]{2,1,0:T(8,128)(2,1)S(1)}, bf16[4,64,256]{2,1,0:T(8,128)(2,1)S(1)}, u32[]{:S(2)}, u32[]{:S(2)}) collective-permute-start(bf16[4,64,256]{2,1,0:T(8,128)(2,1)S(1)} %get-tuple-element.33), channel_id=1, source_target_pairs={{0,32},{32,0},{64,96},{96,64},{128,160},{160,128},{192,224},{224,1... | collective-permute-start | bytes 393224 | tf_op jit(solution)/shard_map/ppermute | solution.py:240
  7.7 5.0 %collective-permute-start.2 = (bf16[4,64,256]{2,1,0:T(8,128)(2,1)S(1)}, bf16[4,64,256]{2,1,0:T(8,128)(2,1)S(1)}, u32[]{:S(2)}, u32[]{:S(2)}) collective-permute-start(bf16[4,64,256]{2,1,0:T(8,128)(2,1)S(1)} %get-tuple-element.34), channel_id=1, source_target_pairs={{0,1},{1,0},{2,3},{3,2},{4,5},{5,4},{6,7},{7,6},{8,9},{9,8},{10,11... | collective-permute-start | bytes 393224 | tf_op jit(solution)/shard_map/ppermute | solution.py:241
  7.7 5.0 %collective-permute-start.3 = (bf16[4,64,256]{2,1,0:T(8,128)(2,1)S(1)}, bf16[4,64,256]{2,1,0:T(8,128)(2,1)S(1)}, u32[]{:S(2)}, u32[]{:S(2)}) collective-permute-start(bf16[4,64,256]{2,1,0:T(8,128)(2,1)S(1)} %get-tuple-element.35), channel_id=1, source_target_pairs={{1,2},{2,1},{3,4},{4,3},{5,6},{6,5},{7,8},{8,7},{9,10},{10,9},{11,... | collective-permute-start | bytes 393224 | tf_op jit(solution)/shard_map/ppermute | solution.py:242
  15.0 10.1 %collective-permute-start.4 = (bf16[4,64,256]{2,1,0:T(8,128)(2,1)S(1)}, bf16[4,64,256]{2,1,0:T(8,128)(2,1)S(1)}, u32[]{:S(2)}, u32[]{:S(2)}) collective-permute-start(bf16[4,64,256]{2,1,0:T(8,128)(2,1)S(1)} %get-tuple-element.39), channel_id=1, source_target_pairs={{32,64},{64,32},{96,128},{128,96},{160,192},{192,160},{224,0},{0,2... | collective-permute-start | bytes 393224 | tf_op jit(solution)/shard_map/ppermute | solution.py:239
  16.6 8.5 %collective-permute-start.5 = (bf16[4,64,256]{2,1,0:T(8,128)(2,1)S(1)}, bf16[4,64,256]{2,1,0:T(8,128)(2,1)S(1)}, u32[]{:S(2)}, u32[]{:S(2)}) collective-permute-start(bf16[4,64,256]{2,1,0:T(8,128)(2,1)S(1)} %get-tuple-element.40), channel_id=1, source_target_pairs={{0,32},{32,0},{64,96},{96,64},{128,160},{160,128},{192,224},{224,1... | collective-permute-start | bytes 393224 | tf_op jit(solution)/shard_map/ppermute | solution.py:240
  17.5 7.6 %collective-permute-start.6 = (bf16[4,64,256]{2,1,0:T(8,128)(2,1)S(1)}, bf16[4,64,256]{2,1,0:T(8,128)(2,1)S(1)}, u32[]{:S(2)}, u32[]{:S(2)}) collective-permute-start(bf16[4,64,256]{2,1,0:T(8,128)(2,1)S(1)} %get-tuple-element.41), channel_id=1, source_target_pairs={{0,1},{1,0},{2,3},{3,2},{4,5},{5,4},{6,7},{7,6},{8,9},{9,8},{10,11... | collective-permute-start | bytes 393224 | tf_op jit(solution)/shard_map/ppermute | solution.py:241
  18.0 7.4 %collective-permute-start.7 = (bf16[4,64,256]{2,1,0:T(8,128)(2,1)S(1)}, bf16[4,64,256]{2,1,0:T(8,128)(2,1)S(1)}, u32[]{:S(2)}, u32[]{:S(2)}) collective-permute-start(bf16[4,64,256]{2,1,0:T(8,128)(2,1)S(1)} %get-tuple-element.42), channel_id=1, source_target_pairs={{1,2},{2,1},{3,4},{4,3},{5,6},{6,5},{7,8},{8,7},{9,10},{10,9},{11,... | collective-permute-start | bytes 393224 | tf_op jit(solution)/shard_map/ppermute | solution.py:242
  27.7 9.9 %collective-permute-start.8 = (bf16[4,64,256]{2,1,0:T(8,128)(2,1)S(1)}, bf16[4,64,256]{2,1,0:T(8,128)(2,1)S(1)}, u32[]{:S(2)}, u32[]{:S(2)}) collective-permute-start(bf16[4,64,256]{2,1,0:T(8,128)(2,1)S(1)} %get-tuple-element.47), channel_id=1, source_target_pairs={{32,64},{64,32},{96,128},{128,96},{160,192},{192,160},{224,0},{0,2... | collective-permute-start | bytes 393224 | tf_op jit(solution)/shard_map/ppermute | solution.py:239
  28.0 9.6 %collective-permute-start.9 = (bf16[4,64,256]{2,1,0:T(8,128)(2,1)S(1)}, bf16[4,64,256]{2,1,0:T(8,128)(2,1)S(1)}, u32[]{:S(2)}, u32[]{:S(2)}) collective-permute-start(bf16[4,64,256]{2,1,0:T(8,128)(2,1)S(1)} %get-tuple-element.48), channel_id=1, source_target_pairs={{0,32},{32,0},{64,96},{96,64},{128,160},{160,128},{192,224},{224,1... | collective-permute-start | bytes 393224 | tf_op jit(solution)/shard_map/ppermute | solution.py:240
  29.8 7.8 %collective-permute-start.10 = (bf16[4,64,256]{2,1,0:T(8,128)(2,1)S(1)}, bf16[4,64,256]{2,1,0:T(8,128)(2,1)S(1)}, u32[]{:S(2)}, u32[]{:S(2)}) collective-permute-start(bf16[4,64,256]{2,1,0:T(8,128)(2,1)S(1)} %get-tuple-element.49), channel_id=1, source_target_pairs={{0,1},{1,0},{2,3},{3,2},{4,5},{5,4},{6,7},{7,6},{8,9},{9,8},{10,11... | collective-permute-start | bytes 393224 | tf_op jit(solution)/shard_map/ppermute | solution.py:241
  29.8 7.8 %collective-permute-start.11 = (bf16[4,64,256]{2,1,0:T(8,128)(2,1)S(1)}, bf16[4,64,256]{2,1,0:T(8,128)(2,1)S(1)}, u32[]{:S(2)}, u32[]{:S(2)}) collective-permute-start(bf16[4,64,256]{2,1,0:T(8,128)(2,1)S(1)} %get-tuple-element.50), channel_id=1, source_target_pairs={{1,2},{2,1},{3,4},{4,3},{5,6},{6,5},{7,8},{8,7},{9,10},{10,9},{11,... | collective-permute-start | bytes 393224 | tf_op jit(solution)/shard_map/ppermute | solution.py:242
  38.1 1.3 %collective-permute-start.12 = (f32[2,64,128]{2,1,0:T(8,128)S(1)}, f32[2,64,128]{2,1,0:T(8,128)S(1)}, u32[]{:S(2)}, u32[]{:S(2)}) collective-permute-start(f32[2,64,128]{2,1,0:T(8,128)S(1)} %gather.1), channel_id=1, source_target_pairs={{0,1},{1,0},{2,3},{3,2},{4,5},{5,4},{6,7},{7,6},{8,9},{9,8},{10,11... | collective-permute-start | bytes 196616 | tf_op jit(solution)/shard_map/ppermute | solution.py:269
  39.5 6.4 %collective-permute-start.15 = (bf16[2,64,128]{2,1,0:T(8,128)(2,1)S(1)}, bf16[2,64,128]{2,1,0:T(8,128)(2,1)S(1)}, u32[]{:S(2)}, u32[]{:S(2)}) collective-permute-start(bf16[2,64,128]{2,1,0:T(8,128)(2,1)S(1)} %fusion.1), channel_id=1, source_target_pairs={{0,4},{2,6},{4,0},{6,2},{1,5},{3,7},{5,1},{7,3},{8,12},{10,14},{12... | collective-permute-start | bytes 98312 | tf_op jit(solution)/shard_map/ppermute | solution.py:254
  40.4 7.4 %collective-permute-start.14 = (bf16[2,64,128]{2,1,0:T(8,128)(2,1)S(1)}, bf16[2,64,128]{2,1,0:T(8,128)(2,1)S(1)}, u32[]{:S(2)}, u32[]{:S(2)}) collective-permute-start(bf16[2,64,128]{2,1,0:T(8,128)(2,1)S(1)} %fusion.1), channel_id=1, source_target_pairs={{0,6},{2,4},{4,2},{6,0},{1,7},{3,5},{5,3},{7,1},{8,14},{10,12},{12... | collective-permute-start | bytes 98312 | tf_op jit(solution)/shard_map/ppermute | solution.py:254
  45.9 3.9 %collective-permute-start.13 = (bf16[2,64,128]{2,1,0:T(8,128)(2,1)S(1)}, bf16[2,64,128]{2,1,0:T(8,128)(2,1)S(1)}, u32[]{:S(2)}, u32[]{:S(2)}) collective-permute-start(bf16[2,64,128]{2,1,0:T(8,128)(2,1)S(1)} %fusion.1), channel_id=1, source_target_pairs={{0,2},{2,0},{4,6},{6,4},{1,3},{3,1},{5,7},{7,5},{8,10},{10,8},{12,... | collective-permute-start | bytes 98312 | tf_op jit(solution)/shard_map/ppermute | solution.py:254
  49.9 5.6 %collective-permute-start.18 = (bf16[2,64,128]{2,1,0:T(8,128)(2,1)S(1)}, bf16[2,64,128]{2,1,0:T(8,128)(2,1)S(1)}, u32[]{:S(2)}, u32[]{:S(2)}) collective-permute-start(bf16[2,64,128]{2,1,0:T(8,128)(2,1)S(1)} %get-tuple-element.54), channel_id=1, source_target_pairs={{0,16},{8,24},{16,0},{24,8},{1,17},{9,25},{17,1},{25,9},{2,18},{10... | collective-permute-start | bytes 98312 | tf_op jit(solution)/shard_map/ppermute | solution.py:254
  50.0 5.6 %collective-permute-start.17 = (bf16[2,64,128]{2,1,0:T(8,128)(2,1)S(1)}, bf16[2,64,128]{2,1,0:T(8,128)(2,1)S(1)}, u32[]{:S(2)}, u32[]{:S(2)}) collective-permute-start(bf16[2,64,128]{2,1,0:T(8,128)(2,1)S(1)} %get-tuple-element.54), channel_id=1, source_target_pairs={{0,24},{8,16},{16,8},{24,0},{1,25},{9,17},{17,9},{25,1},{2,26},{10... | collective-permute-start | bytes 98312 | tf_op jit(solution)/shard_map/ppermute | solution.py:254
  50.9 4.6 %collective-permute-start.16 = (bf16[2,64,128]{2,1,0:T(8,128)(2,1)S(1)}, bf16[2,64,128]{2,1,0:T(8,128)(2,1)S(1)}, u32[]{:S(2)}, u32[]{:S(2)}) collective-permute-start(bf16[2,64,128]{2,1,0:T(8,128)(2,1)S(1)} %get-tuple-element.54), channel_id=1, source_target_pairs={{0,8},{8,0},{16,24},{24,16},{1,9},{9,1},{17,25},{25,17},{2,10},{10... | collective-permute-start | bytes 98312 | tf_op jit(solution)/shard_map/ppermute | solution.py:254
  55.6 4.4 %collective-permute-start.19 = (bf16[2,64,128]{2,1,0:T(8,128)(2,1)S(1)}, bf16[2,64,128]{2,1,0:T(8,128)(2,1)S(1)}, u32[]{:S(2)}, u32[]{:S(2)}) collective-permute-start(bf16[2,64,128]{2,1,0:T(8,128)(2,1)S(1)} %get-tuple-element.52), channel_id=1, source_target_pairs={{0,32},{32,0},{64,96},{96,64},{128,160},{160,128},{192,224},{224,1... | collective-permute-start | bytes 98312 | tf_op jit(solution)/shard_map/ppermute | solution.py:263
  59.9 4.9 %collective-permute-start.20 = (bf16[2,64,128]{2,1,0:T(8,128)(2,1)S(1)}, bf16[2,64,128]{2,1,0:T(8,128)(2,1)S(1)}, u32[]{:S(2)}, u32[]{:S(2)}) collective-permute-start(bf16[2,64,128]{2,1,0:T(8,128)(2,1)S(1)} %fusion), channel_id=1, source_target_pairs={{0,64},{32,96},{64,0},{96,32},{128,192},{160,224},{192,128},{224,1... | collective-permute-start | bytes 98312 | tf_op jit(solution)/shard_map/ppermute | solution.py:263
  64.9 7.9 %collective-permute-start.21 = (bf16[2,64,128]{2,1,0:T(8,128)(2,1)S(1)}, bf16[2,64,128]{2,1,0:T(8,128)(2,1)S(1)}, u32[]{:S(2)}, u32[]{:S(2)}) collective-permute-start(bf16[2,64,128]{2,1,0:T(8,128)(2,1)S(1)} %fusion.2), channel_id=1, source_target_pairs={{0,128},{32,160},{64,192},{96,224},{128,0},{160,32},{192,64},{224,... | collective-permute-start | bytes 98312 | tf_op jit(solution)/shard_map/ppermute | solution.py:263

commit v3 on v2

--- a/solution.py
+++ b/solution.py
@@ -82,7 +82,7 @@
     return jnp.dot(jnp.concatenate(picked, axis=1), tall, preferred_element_type=F32)
 
 
-def step_kernel(cols, live, send, x, rd, rc, ra, rb, blocks, v_out, x_out, oa, ob, oc, od, src):
+def step_kernel(cols, live, send, x, rb, rd, rc, ra, blocks, v_out, x_out, oa, ob, oc, od, src):
     side, layer = parities()
     place_rows(x, (ra, rb, rc, rd), src, side, layer)
     for i in range(x.shape[0]):
@@ -164,7 +164,7 @@
     w_out[...] = against([x[e] for e in own], [z[e] for e in own])
 
 
-def gather_kernel(rd, rc, ra, rb, z, w0, w1, w2, own, w_out):
+def gather_kernel(rb, rd, rc, ra, z, w0, w1, w2, own, w_out):
     side, layer = parities()
     numbers, _ = directions(side, layer)
     width = ra.shape[0]
@@ -177,7 +177,7 @@
     w_out[1] = jnp.concatenate([w2[...], own[...] + against(rows, z_rows)], axis=1)
 
 
-def last_kernel(cols, live, x, rd, rc, ra, rb, blocks, v_out, src):
+def last_kernel(cols, live, x, rb, rd, rc, ra, blocks, v_out, src):
     side, layer = parities()
     place_rows(x, (ra, rb, rc, rd), src, side, layer)
     for i in range(x.shape[0]):
@@ -240,36 +240,29 @@
     rc = lax.ppermute(oc, "gx", swaps(gx, 0))
     ra = lax.ppermute(oa, GY, swaps(gy, 0))
     rb = lax.ppermute(ob, GY, swaps(gy, 1))
-    return rd, rc, ra, rb
+    return rb, rd, rc, ra
 
 
 def rounded_to(x):
     return lax.reduce_precision(x, 8, 7)
 
 
-def ring_sum(x, axis):
-    count = lax.axis_size(axis)
+def four_sum(x, axes, low, high):
+    count = lax.axis_size(axes)
     x = rounded_to(x)
     sent = x.astype(BF16)
-    parts = [lax.ppermute(sent, axis, [(i, i ^ k) for i in range(count)]).astype(F32) for k in range(1, count)]
-    return (parts[0] + parts[2]) + (x + parts[1])
-
-
-def doubled_sum(x, axis):
-    count = lax.axis_size(axis)
-    k = 1
-    while k < count:
-        x = rounded_to(x)
-        x = x + lax.ppermute(x.astype(BF16), axis, [(i, i ^ k) for i in range(count)]).astype(F32)
-        k *= 2
-    return x
+    one, two, three = (
+        lax.ppermute(sent, axes, [(i, i ^ bits) for i in range(count)]).astype(F32)
+        for bits in (low, high, low + high)
+    )
+    return (one + three) + (x + two)
 
 
 def summed(x):
-    x = x + lax.ppermute(x, "core", [(0, 1), (1, 0)])
-    x = ring_sum(x, "y1")
-    x = ring_sum(x, "y0")
-    return doubled_sum(x, "gx")
+    x = four_sum(x, ("gx", "core"), 1, 2)
+    x = four_sum(x, "y1", 1, 2)
+    x = four_sum(x, "y0", 1, 2)
+    return four_sum(x, "gx", 2, 4)
 
 
 def on_device(blocks, block_cols, live_blocks, send_rows, start, sketch):

time: 76 us -> 69.2 us (0.911)
  waiting for transfers between devices: 20 us -> 14.5 us
  starting transfers between devices: 34.7 us -> 33.5 us
    ppermute x10 -> x12, waiting for transfers between devices: 19 us -> 10.1 us  [four_sum(): lax.ppermute(sent, axes, [(i, i ^ bits) for i in range(count)]).astype(F32)]
    ppermute x3, starting transfers between devices: 10.4 us -> 3.08 us  [exchange(): rb = lax.ppermute(ob, GY, swaps(gy, 1))]
    ppermute x10 -> x12, starting transfers between devices: 13.2 us -> 17.7 us  [four_sum(): lax.ppermute(sent, axes, [(i, i ^ bits) for i in range(count)]).astype(F32)]
    ppermute x3, waiting for transfers between devices: 0.01 us -> 1.89 us  [exchange(): rd = lax.ppermute(od, 'gx', swaps(gx, 1))]
    ppermute x3, waiting for transfers between devices: 0.73 us -> 2.57 us  [exchange(): rc = lax.ppermute(oc, 'gx', swaps(gx, 0))]
    ppermute x3, starting transfers between devices: 7.83 us -> 9.4 us  [exchange(): rd = lax.ppermute(od, 'gx', swaps(gx, 1))]
    ppermute x3, starting transfers between devices: 0.45 us -> 1.32 us  [exchange(): ra = lax.ppermute(oa, GY, swaps(gy, 0))]
  transfers between devices with their start and end apart: 22 -> 24, of which waited for: 10 -> 13; matrix products, arithmetic and copies ran while one was open for 0% -> 0% of each run, Pallas kernels for 14% -> 16%
where the time goes in v3:
time: 69.2 us; the launch traced here: 68.9 us
  starting transfers between devices  33.5 us (48%)
  Pallas kernels  19.7 us (28%)
  waiting for transfers between devices  14.5 us (21%)
  between operations  0.96 us (1%)
    ppermute x12, starting transfers between devices, four_sum(): lax.ppermute(sent, axes, [(i, i ^ bits) for i in range(count)]).astype(F32)  17.7 us
    ppermute x12, waiting for transfers between devices, four_sum(): lax.ppermute(sent, axes, [(i, i ^ bits) for i in range(count)]).astype(F32)  10.1 us
    ppermute x3, starting transfers between devices, exchange(): rd = lax.ppermute(od, 'gx', swaps(gx, 1))  9.4 us
    pallas_call x2, Pallas kernels, step(): call(kernel, 'step', [SMEM] * 3 + [VMEM] * (6 + len(earlier)), [vector, r...  4.6 us
    pallas_call x1, Pallas kernels, on_device(): call(prepare_kernel, 'prepare', [HBM] * 4 + [VMEM], [jax.ShapeDtypeStruct...  3.66 us
    ppermute x3, starting transfers between devices, exchange(): rb = lax.ppermute(ob, GY, swaps(gy, 1))  3.08 us
    pallas_call x1, Pallas kernels, on_device(): call(final_kernel, 'final', [VMEM] * 5, [jax.ShapeDtypeStruct((STEPS + 1,...  2.63 us
    ppermute x3, waiting for transfers between devices, exchange(): rc = lax.ppermute(oc, 'gx', swaps(gx, 0))  2.57 us
  transfers between devices with their start and end apart: 24, of which 13 were waited for; matrix products, arithmetic and copies ran while one was open for 0% of the time, Pallas kernels for 16%

profile of v3, /device:TPU:8, one launch (start us, length us, event | category | flops | bytes accessed | tf_op | source)
XLA Modules:
  0.0 68.9 jit_solution(5383737741579744886)
XLA Ops:
  0.6 1.1 %first.1 = (f32[8,64,256]{2,1,0:T(8,128)S(1)}, s32[1,4,4]{2,1,0:T(4,128)S(1)}, bf16[8,64,256]{2,1,0:T(8,128)(2,1)S(1)}, bf16[4,64,256]{2,1,0:T(8,128)(2,1)S(1)},...) custom-call(s32[1,4,4]{2,1,0:T(4,128)} %send_hbm.1, ...), custom_call_target="tpu_custom_call" | custom-call | flops 1048576 | bytes 1048576 | tf_op jit(solution)/shard_map/first/pallas_call | solution.py:281
  1.9 5.9 %collective-permute-start.1 = (bf16[4,64,256]{2,1,0:T(8,128)(2,1)S(1)}, bf16[4,64,256]{2,1,0:T(8,128)(2,1)S(1)}, u32[]{:S(2)}, u32[]{:S(2)}) collective-permute-start(bf16[4,64,256]{2,1,0:T(8,128)(2,1)S(1)} %get-tuple-element.33), channel_id=1, source_target_pairs={{32,64},{64,32},{96,128},{128,96},{160,192},{192,160},{224,0},{0,2... | collective-permute-start | bytes 393224 | tf_op jit(solution)/shard_map/ppermute | solution.py:239
  7.8 1.3 %collective-permute-start.3 = (bf16[4,64,256]{2,1,0:T(8,128)(2,1)S(1)}, bf16[4,64,256]{2,1,0:T(8,128)(2,1)S(1)}, u32[]{:S(2)}, u32[]{:S(2)}) collective-permute-start(bf16[4,64,256]{2,1,0:T(8,128)(2,1)S(1)} %get-tuple-element.35), channel_id=1, source_target_pairs={{0,1},{1,0},{2,3},{3,2},{4,5},{5,4},{6,7},{7,6},{8,9},{9,8},{10,11... | collective-permute-start | bytes 393224 | tf_op jit(solution)/shard_map/ppermute | solution.py:241
  9.1 3.7 %prepare.1 = (bf16[8,8,256,256]{3,2,1,0:T(8,128)(2,1)S(1)}, s32[8,8]{1,0:T(8,128)S(1)}, s32[8]{0:T(128)S(1)}, bf16[8,64,256]{2,1,0:T(8,128)(2,1)S(1)}, bf16[8,64...) custom-call(bf16[8,8,256,256]{3,2,1,0:T(8,128)(2,1)} %blocks_hbm.1, f32[64,8,256]{2,1,0:T(8,128)} %sketch_hbm.1, ...), custom_call_target="tpu_custom_call" | custom-call | flops 50331648 | bytes 8388608 | tf_op jit(solution)/shard_map/prepare/pallas_call | solution.py:291
  12.8 1.0 %collective-permute-done.2.refs_6_ = bf16[4,64,256]{2,1,0:T(8,128)(2,1)S(1)} collective-permute-done((bf16[4,64,256]{2,1,0:T(8,128)(2,1)S(1)}, bf16[4,64,256]{2,1,0:T(8,128)(2,1)S(1)}, u32[]{:S(2)}, u32[]{:S(2)}) %collective-permute-start.2) | collective-permute-done | bytes 131104 | tf_op jit(solution)/shard_map/ppermute | solution.py:240
  13.8 2.3 %step.2 = (f32[8,64,256]{2,1,0:T(8,128)S(1)}, bf16[8,64,256]{2,1,0:T(8,128)(2,1)S(1)}, bf16[4,64,256]{2,1,0:T(8,128)(2,1)S(1)}, bf16[4,64,256]{2,1,0:T(8,128)(2,...) custom-call(s32[8,8]{1,0:T(8,128)S(1)} %get-tuple-element.28.refs_0_.cols, ...), custom_call_target="tpu_custom_call" | custom-call | flops 536870912 | bytes 8388608 | tf_op jit(solution)/shard_map/step/pallas_call | solution.py:314
  16.2 2.9 %collective-permute-start.4 = (bf16[4,64,256]{2,1,0:T(8,128)(2,1)S(1)}, bf16[4,64,256]{2,1,0:T(8,128)(2,1)S(1)}, u32[]{:S(2)}, u32[]{:S(2)}) collective-permute-start(bf16[4,64,256]{2,1,0:T(8,128)(2,1)S(1)} %get-tuple-element.39), channel_id=1, source_target_pairs={{1,2},{2,1},{3,4},{4,3},{5,6},{6,5},{7,8},{8,7},{9,10},{10,9},{11,... | collective-permute-start | bytes 393224 | tf_op jit(solution)/shard_map/ppermute | solution.py:242
  19.0 2.0 %collective-permute-start.5 = (bf16[4,64,256]{2,1,0:T(8,128)(2,1)S(1)}, bf16[4,64,256]{2,1,0:T(8,128)(2,1)S(1)}, u32[]{:S(2)}, u32[]{:S(2)}) collective-permute-start(bf16[4,64,256]{2,1,0:T(8,128)(2,1)S(1)} %get-tuple-element.40), channel_id=1, source_target_pairs={{32,64},{64,32},{96,128},{128,96},{160,192},{192,160},{224,0},{0,2... | collective-permute-start | bytes 393224 | tf_op jit(solution)/shard_map/ppermute | solution.py:239
  21.1 1.0 %collective-permute-start.6 = (bf16[4,64,256]{2,1,0:T(8,128)(2,1)S(1)}, bf16[4,64,256]{2,1,0:T(8,128)(2,1)S(1)}, u32[]{:S(2)}, u32[]{:S(2)}) collective-permute-start(bf16[4,64,256]{2,1,0:T(8,128)(2,1)S(1)} %get-tuple-element.41), channel_id=1, source_target_pairs={{0,32},{32,0},{64,96},{96,64},{128,160},{160,128},{192,224},{224,1... | collective-permute-start | bytes 393224 | tf_op jit(solution)/shard_map/ppermute | solution.py:240
  22.1 2.0 %spread.1.refs_9_.refs_4_ = f32[25,64,256]{2,1,0:T(8,128)S(1)} custom-call(s32[8,8]{1,0:T(8,128)S(1)} %get-tuple-element.28.refs_0_.cols, s32[8]{0:T(128)S(1)} %get-tuple-element.29.refs_1_.live, bf16[8,64,256]{2,1,0:T(8,128)(2,1)S(1)} %get-tuple-element.43.refs_2_.high, bf16[8,8,256,256]{3,2,1,0:T(8,128)(2,1)S(1)} %get-tuple-element.36.refs_8_.refs_3_.blocks), custom_call_target="tpu_custom_call" | custom-call | flops 536870912 | bytes 4194304 | tf_op jit(solution)/shard_map/spread/pallas_call | solution.py:341
  24.4 0.8 %collective-permute-done.5.refs_5_ = bf16[4,64,256]{2,1,0:T(8,128)(2,1)S(1)} collective-permute-done((bf16[4,64,256]{2,1,0:T(8,128)(2,1)S(1)}, bf16[4,64,256]{2,1,0:T(8,128)(2,1)S(1)}, u32[]{:S(2)}, u32[]{:S(2)}) %collective-permute-start.5) | collective-permute-done | bytes 131104 | tf_op jit(solution)/shard_map/ppermute | solution.py:239
  25.2 0.8 %collective-permute-done.6.refs_6_ = bf16[4,64,256]{2,1,0:T(8,128)(2,1)S(1)} collective-permute-done((bf16[4,64,256]{2,1,0:T(8,128)(2,1)S(1)}, bf16[4,64,256]{2,1,0:T(8,128)(2,1)S(1)}, u32[]{:S(2)}, u32[]{:S(2)}) %collective-permute-start.6) | collective-permute-done | bytes 131104 | tf_op jit(solution)/shard_map/ppermute | solution.py:240
  26.0 2.3 %step.3 = (f32[8,64,256]{2,1,0:T(8,128)S(1)}, bf16[8,64,256]{2,1,0:T(8,128)(2,1)S(1)}, bf16[4,64,256]{2,1,0:T(8,128)(2,1)S(1)}, bf16[4,64,256]{2,1,0:T(8,128)(2,...) custom-call(s32[8,8]{1,0:T(8,128)S(1)} %get-tuple-element.28.refs_0_.cols, ...), custom_call_target="tpu_custom_call" | custom-call | flops 536870912 | bytes 8388608 | tf_op jit(solution)/shard_map/step/pallas_call | solution.py:314
  28.4 1.5 %collective-permute-start.9 = (bf16[4,64,256]{2,1,0:T(8,128)(2,1)S(1)}, bf16[4,64,256]{2,1,0:T(8,128)(2,1)S(1)}, u32[]{:S(2)}, u32[]{:S(2)}) collective-permute-start(bf16[4,64,256]{2,1,0:T(8,128)(2,1)S(1)} %get-tuple-element.48), channel_id=1, source_target_pairs={{32,64},{64,32},{96,128},{128,96},{160,192},{192,160},{224,0},{0,2... | collective-permute-start | bytes 393224 | tf_op jit(solution)/shard_map/ppermute | solution.py:239
  29.9 1.0 %collective-permute-start.10 = (bf16[4,64,256]{2,1,0:T(8,128)(2,1)S(1)}, bf16[4,64,256]{2,1,0:T(8,128)(2,1)S(1)}, u32[]{:S(2)}, u32[]{:S(2)}) collective-permute-start(bf16[4,64,256]{2,1,0:T(8,128)(2,1)S(1)} %get-tuple-element.49), channel_id=1, source_target_pairs={{0,32},{32,0},{64,96},{96,64},{128,160},{160,128},{192,224},{224,1... | collective-permute-start | bytes 393224 | tf_op jit(solution)/shard_map/ppermute | solution.py:240
  30.9 2.0 %respread.1.z = f32[25,64,256]{2,1,0:T(8,128)S(1)} custom-call(s32[8,8]{1,0:T(8,128)S(1)} %get-tuple-element.28.refs_0_.cols, s32[8]{0:T(128)S(1)} %get-tuple-element.29.refs_1_.live, bf16[8,64,256]{2,1,0:T(8,128)(2,1)S(1)} %get-tuple-element.43.refs_2_.high, bf16[8,8,256,256]{3,2,1,0:T(8,128)(2,1)S(1)} %get-tuple-element.36.refs_8_.refs_3_.blocks, ...), custom_call_target="tpu_custom_call" | custom-call | flops 536870912 | bytes 4194304 | tf_op jit(solution)/shard_map/respread/pallas_call | solution.py:345
  33.6 1.1 %collective-permute-done.9.rd = bf16[4,64,256]{2,1,0:T(8,128)(2,1)S(1)} collective-permute-done((bf16[4,64,256]{2,1,0:T(8,128)(2,1)S(1)}, bf16[4,64,256]{2,1,0:T(8,128)(2,1)S(1)}, u32[]{:S(2)}, u32[]{:S(2)}) %collective-permute-start.9) | collective-permute-done | bytes 131104 | tf_op jit(solution)/shard_map/ppermute | solution.py:239
  36.7 1.5 %collective-permute-start.12 = (bf16[2,64,128]{2,1,0:T(8,128)(2,1)S(1)}, bf16[2,64,128]{2,1,0:T(8,128)(2,1)S(1)}, u32[]{:S(2)}, u32[]{:S(2)}) collective-permute-start(bf16[2,64,128]{2,1,0:T(8,128)(2,1)S(1)} %reduce-precision_convert_fusion), channel_id=1, source_target_pairs={{0,1},{1,0},{32,33},{33,32},{64,65},{65,64},{96,97},{97,96},{128,1... | collective-permute-start | bytes 98312 | tf_op jit(solution)/shard_map/ppermute | solution.py:255
  38.2 2.0 %collective-permute-done.14 = bf16[2,64,128]{2,1,0:T(8,128)(2,1)S(1)} collective-permute-done((bf16[2,64,128]{2,1,0:T(8,128)(2,1)S(1)}, bf16[2,64,128]{2,1,0:T(8,128)(2,1)S(1)}, u32[]{:S(2)}, u32[]{:S(2)}) %collective-permute-start.14) | collective-permute-done | bytes 32800 | tf_op jit(solution)/shard_map/ppermute | solution.py:255
  40.2 1.8 %collective-permute-start.17 = (bf16[2,64,128]{2,1,0:T(8,128)(2,1)S(1)}, bf16[2,64,128]{2,1,0:T(8,128)(2,1)S(1)}, u32[]{:S(2)}, u32[]{:S(2)}) collective-permute-start(bf16[2,64,128]{2,1,0:T(8,128)(2,1)S(1)} %get-tuple-element.54), channel_id=1, source_target_pairs={{0,4},{2,6},{4,0},{6,2},{1,5},{3,7},{5,1},{7,3},{8,12},{10,14},{12... | collective-permute-start | bytes 98312 | tf_op jit(solution)/shard_map/ppermute | solution.py:255
  42.0 3.5 %collective-permute-start.16 = (bf16[2,64,128]{2,1,0:T(8,128)(2,1)S(1)}, bf16[2,64,128]{2,1,0:T(8,128)(2,1)S(1)}, u32[]{:S(2)}, u32[]{:S(2)}) collective-permute-start(bf16[2,64,128]{2,1,0:T(8,128)(2,1)S(1)} %get-tuple-element.54), channel_id=1, source_target_pairs={{0,6},{2,4},{4,2},{6,0},{1,7},{3,5},{5,3},{7,1},{8,14},{10,12},{12... | collective-permute-start | bytes 98312 | tf_op jit(solution)/shard_map/ppermute | solution.py:255
  45.7 1.7 %collective-permute-done.16 = bf16[2,64,128]{2,1,0:T(8,128)(2,1)S(1)} collective-permute-done((bf16[2,64,128]{2,1,0:T(8,128)(2,1)S(1)}, bf16[2,64,128]{2,1,0:T(8,128)(2,1)S(1)}, u32[]{:S(2)}, u32[]{:S(2)}) %collective-permute-start.16) | collective-permute-done | bytes 32800 | tf_op jit(solution)/shard_map/ppermute | solution.py:255
  47.4 2.0 %collective-permute-done.15 = bf16[2,64,128]{2,1,0:T(8,128)(2,1)S(1)} collective-permute-done((bf16[2,64,128]{2,1,0:T(8,128)(2,1)S(1)}, bf16[2,64,128]{2,1,0:T(8,128)(2,1)S(1)}, u32[]{:S(2)}, u32[]{:S(2)}) %collective-permute-start.15) | collective-permute-done | bytes 32800 | tf_op jit(solution)/shard_map/ppermute | solution.py:255
  50.0 1.1 %collective-permute-start.19 = (bf16[2,64,128]{2,1,0:T(8,128)(2,1)S(1)}, bf16[2,64,128]{2,1,0:T(8,128)(2,1)S(1)}, u32[]{:S(2)}, u32[]{:S(2)}) collective-permute-start(bf16[2,64,128]{2,1,0:T(8,128)(2,1)S(1)} %fusion), channel_id=1, source_target_pairs={{0,24},{8,16},{16,8},{24,0},{1,25},{9,17},{17,9},{25,1},{2,26},{10... | collective-permute-start | bytes 98312 | tf_op jit(solution)/shard_map/ppermute | solution.py:255
  51.1 1.9 %collective-permute-start.18 = (bf16[2,64,128]{2,1,0:T(8,128)(2,1)S(1)}, bf16[2,64,128]{2,1,0:T(8,128)(2,1)S(1)}, u32[]{:S(2)}, u32[]{:S(2)}) collective-permute-start(bf16[2,64,128]{2,1,0:T(8,128)(2,1)S(1)} %fusion), channel_id=1, source_target_pairs={{0,8},{8,0},{16,24},{24,16},{1,9},{9,1},{17,25},{25,17},{2,10},{10... | collective-permute-start | bytes 98312 | tf_op jit(solution)/shard_map/ppermute | solution.py:255
  53.0 1.9 %collective-permute-done.20 = bf16[2,64,128]{2,1,0:T(8,128)(2,1)S(1)} collective-permute-done((bf16[2,64,128]{2,1,0:T(8,128)(2,1)S(1)}, bf16[2,64,128]{2,1,0:T(8,128)(2,1)S(1)}, u32[]{:S(2)}, u32[]{:S(2)}) %collective-permute-start.20) | collective-permute-done | bytes 32800 | tf_op jit(solution)/shard_map/ppermute | solution.py:255
  55.3 2.8 %collective-permute-start.23 = (bf16[2,64,128]{2,1,0:T(8,128)(2,1)S(1)}, bf16[2,64,128]{2,1,0:T(8,128)(2,1)S(1)}, u32[]{:S(2)}, u32[]{:S(2)}) collective-permute-start(bf16[2,64,128]{2,1,0:T(8,128)(2,1)S(1)} %get-tuple-element.52), channel_id=1, source_target_pairs={{0,128},{32,160},{64,192},{96,224},{128,0},{160,32},{192,64},{224,... | collective-permute-start | bytes 98312 | tf_op jit(solution)/shard_map/ppermute | solution.py:255
  58.2 2.7 %collective-permute-start.22 = (bf16[2,64,128]{2,1,0:T(8,128)(2,1)S(1)}, bf16[2,64,128]{2,1,0:T(8,128)(2,1)S(1)}, u32[]{:S(2)}, u32[]{:S(2)}) collective-permute-start(bf16[2,64,128]{2,1,0:T(8,128)(2,1)S(1)} %get-tuple-element.52), channel_id=1, source_target_pairs={{0,192},{32,224},{64,128},{96,160},{128,64},{160,96},{192,0},{224,... | collective-permute-start | bytes 98312 | tf_op jit(solution)/shard_map/ppermute | solution.py:255
  60.9 1.0 %collective-permute-start.21 = (bf16[2,64,128]{2,1,0:T(8,128)(2,1)S(1)}, bf16[2,64,128]{2,1,0:T(8,128)(2,1)S(1)}, u32[]{:S(2)}, u32[]{:S(2)}) collective-permute-start(bf16[2,64,128]{2,1,0:T(8,128)(2,1)S(1)} %get-tuple-element.52), channel_id=1, source_target_pairs={{0,64},{32,96},{64,0},{96,32},{128,192},{160,224},{192,128},{224,1... | collective-permute-start | bytes 98312 | tf_op jit(solution)/shard_map/ppermute | solution.py:255
  61.9 2.2 %last.1.v3 = f32[8,64,256]{2,1,0:T(8,128)S(1)} custom-call(s32[8,8]{1,0:T(8,128)S(1)} %get-tuple-element.28.refs_0_.cols, s32[8]{0:T(128)S(1)} %get-tuple-element.29.refs_1_.live, bf16[8,64,256]{2,1,0:T(8,128)(2,1)S(1)} %get-tuple-element.46.x, bf16[4,64,256]{2,1,0:T(8,128)(2,1)S(1)} %collective-permute-done.8.rb, ...), custom_call_target="tpu_custom_call" | custom-call | flops 536870912 | bytes 8388608 | tf_op jit(solution)/shard_map/last/pallas_call | solution.py:355
  64.3 1.8 %collective-permute-done.21 = bf16[2,64,128]{2,1,0:T(8,128)(2,1)S(1)} collective-permute-done((bf16[2,64,128]{2,1,0:T(8,128)(2,1)S(1)}, bf16[2,64,128]{2,1,0:T(8,128)(2,1)S(1)}, u32[]{:S(2)}, u32[]{:S(2)}) %collective-permute-start.21) | collective-permute-done | bytes 32800 | tf_op jit(solution)/shard_map/ppermute | solution.py:255
  66.1 2.6 %final.1 = (f32[4,8,64,256]{3,2,1,0:T(8,128)}, f32[4,4,64]{2,1,0:T(4,128)}) custom-call(f32[8,64,256]{2,1,0:T(8,128)S(1)} %get-tuple-element.27.start.v0, f32[8,64,256]{2,1,0:T(8,128)S(1)} %get-tuple-element.37.v.v1, f32[8,64,256]{2,1,0:T(8,128)S(1)} %get-tuple-element.45.v.v2, f32[8,64,256]{2,1,0:T(8,128)S(1)} %last.1.v3, f32[2,64,128]{2,1,0:T(8,128)S(1)} %add_add_fusion.w), custom_call_target="tpu_custom_call" | custom-call | flops 4194304 | bytes 4194304 | tf_op jit(solution)/shard_map/final/pallas_call | solution.py:365
  (33 shorter events, 4.5 us)
Async XLA Ops:
  1.8 11.0 %collective-permute-start = (bf16[4,64,256]{2,1,0:T(8,128)(2,1)S(1)}, bf16[4,64,256]{2,1,0:T(8,128)(2,1)S(1)}, u32[]{:S(2)}, u32[]{:S(2)}) collective-permute-start(bf16[4,64,256]{2,1,0:T(8,128)(2,1)S(1)} %get-tuple-element.32), channel_id=1, source_target_pairs={{1,2},{2,1},{3,4},{4,3},{5,6},{6,5},{7,8},{8,7},{9,10},{10,9},{11,... | collective-permute-start | bytes 393224 | tf_op jit(solution)/shard_map/ppermute | solution.py:242
  1.9 10.9 %collective-permute-start.1 = (bf16[4,64,256]{2,1,0:T(8,128)(2,1)S(1)}, bf16[4,64,256]{2,1,0:T(8,128)(2,1)S(1)}, u32[]{:S(2)}, u32[]{:S(2)}) collective-permute-start(bf16[4,64,256]{2,1,0:T(8,128)(2,1)S(1)} %get-tuple-element.33), channel_id=1, source_target_pairs={{32,64},{64,32},{96,128},{128,96},{160,192},{192,160},{224,0},{0,2... | collective-permute-start | bytes 393224 | tf_op jit(solution)/shard_map/ppermute | solution.py:239
  7.8 6.0 %collective-permute-start.2 = (bf16[4,64,256]{2,1,0:T(8,128)(2,1)S(1)}, bf16[4,64,256]{2,1,0:T(8,128)(2,1)S(1)}, u32[]{:S(2)}, u32[]{:S(2)}) collective-permute-start(bf16[4,64,256]{2,1,0:T(8,128)(2,1)S(1)} %get-tuple-element.34), channel_id=1, source_target_pairs={{0,32},{32,0},{64,96},{96,64},{128,160},{160,128},{192,224},{224,1... | collective-permute-start | bytes 393224 | tf_op jit(solution)/shard_map/ppermute | solution.py:240
  7.8 6.0 %collective-permute-start.3 = (bf16[4,64,256]{2,1,0:T(8,128)(2,1)S(1)}, bf16[4,64,256]{2,1,0:T(8,128)(2,1)S(1)}, u32[]{:S(2)}, u32[]{:S(2)}) collective-permute-start(bf16[4,64,256]{2,1,0:T(8,128)(2,1)S(1)} %get-tuple-element.35), channel_id=1, source_target_pairs={{0,1},{1,0},{2,3},{3,2},{4,5},{5,4},{6,7},{7,6},{8,9},{9,8},{10,11... | collective-permute-start | bytes 393224 | tf_op jit(solution)/shard_map/ppermute | solution.py:241
  16.2 8.3 %collective-permute-start.4 = (bf16[4,64,256]{2,1,0:T(8,128)(2,1)S(1)}, bf16[4,64,256]{2,1,0:T(8,128)(2,1)S(1)}, u32[]{:S(2)}, u32[]{:S(2)}) collective-permute-start(bf16[4,64,256]{2,1,0:T(8,128)(2,1)S(1)} %get-tuple-element.39), channel_id=1, source_target_pairs={{1,2},{2,1},{3,4},{4,3},{5,6},{6,5},{7,8},{8,7},{9,10},{10,9},{11,... | collective-permute-start | bytes 393224 | tf_op jit(solution)/shard_map/ppermute | solution.py:242
  19.0 6.2 %collective-permute-start.5 = (bf16[4,64,256]{2,1,0:T(8,128)(2,1)S(1)}, bf16[4,64,256]{2,1,0:T(8,128)(2,1)S(1)}, u32[]{:S(2)}, u32[]{:S(2)}) collective-permute-start(bf16[4,64,256]{2,1,0:T(8,128)(2,1)S(1)} %get-tuple-element.40), channel_id=1, source_target_pairs={{32,64},{64,32},{96,128},{128,96},{160,192},{192,160},{224,0},{0,2... | collective-permute-start | bytes 393224 | tf_op jit(solution)/shard_map/ppermute | solution.py:239
  21.1 5.0 %collective-permute-start.6 = (bf16[4,64,256]{2,1,0:T(8,128)(2,1)S(1)}, bf16[4,64,256]{2,1,0:T(8,128)(2,1)S(1)}, u32[]{:S(2)}, u32[]{:S(2)}) collective-permute-start(bf16[4,64,256]{2,1,0:T(8,128)(2,1)S(1)} %get-tuple-element.41), channel_id=1, source_target_pairs={{0,32},{32,0},{64,96},{96,64},{128,160},{160,128},{192,224},{224,1... | collective-permute-start | bytes 393224 | tf_op jit(solution)/shard_map/ppermute | solution.py:240
  22.1 4.0 %collective-permute-start.7 = (bf16[4,64,256]{2,1,0:T(8,128)(2,1)S(1)}, bf16[4,64,256]{2,1,0:T(8,128)(2,1)S(1)}, u32[]{:S(2)}, u32[]{:S(2)}) collective-permute-start(bf16[4,64,256]{2,1,0:T(8,128)(2,1)S(1)} %get-tuple-element.42), channel_id=1, source_target_pairs={{0,1},{1,0},{2,3},{3,2},{4,5},{5,4},{6,7},{7,6},{8,9},{9,8},{10,11... | collective-permute-start | bytes 393224 | tf_op jit(solution)/shard_map/ppermute | solution.py:241
  28.3 5.2 %collective-permute-start.8 = (bf16[4,64,256]{2,1,0:T(8,128)(2,1)S(1)}, bf16[4,64,256]{2,1,0:T(8,128)(2,1)S(1)}, u32[]{:S(2)}, u32[]{:S(2)}) collective-permute-start(bf16[4,64,256]{2,1,0:T(8,128)(2,1)S(1)} %get-tuple-element.47), channel_id=1, source_target_pairs={{1,2},{2,1},{3,4},{4,3},{5,6},{6,5},{7,8},{8,7},{9,10},{10,9},{11,... | collective-permute-start | bytes 393224 | tf_op jit(solution)/shard_map/ppermute | solution.py:242
  28.4 6.3 %collective-permute-start.9 = (bf16[4,64,256]{2,1,0:T(8,128)(2,1)S(1)}, bf16[4,64,256]{2,1,0:T(8,128)(2,1)S(1)}, u32[]{:S(2)}, u32[]{:S(2)}) collective-permute-start(bf16[4,64,256]{2,1,0:T(8,128)(2,1)S(1)} %get-tuple-element.48), channel_id=1, source_target_pairs={{32,64},{64,32},{96,128},{128,96},{160,192},{192,160},{224,0},{0,2... | collective-permute-start | bytes 393224 | tf_op jit(solution)/shard_map/ppermute | solution.py:239
  29.9 5.6 %collective-permute-start.10 = (bf16[4,64,256]{2,1,0:T(8,128)(2,1)S(1)}, bf16[4,64,256]{2,1,0:T(8,128)(2,1)S(1)}, u32[]{:S(2)}, u32[]{:S(2)}) collective-permute-start(bf16[4,64,256]{2,1,0:T(8,128)(2,1)S(1)} %get-tuple-element.49), channel_id=1, source_target_pairs={{0,32},{32,0},{64,96},{96,64},{128,160},{160,128},{192,224},{224,1... | collective-permute-start | bytes 393224 | tf_op jit(solution)/shard_map/ppermute | solution.py:240
  30.9 4.5 %collective-permute-start.11 = (bf16[4,64,256]{2,1,0:T(8,128)(2,1)S(1)}, bf16[4,64,256]{2,1,0:T(8,128)(2,1)S(1)}, u32[]{:S(2)}, u32[]{:S(2)}) collective-permute-start(bf16[4,64,256]{2,1,0:T(8,128)(2,1)S(1)} %get-tuple-element.50), channel_id=1, source_target_pairs={{0,1},{1,0},{2,3},{3,2},{4,5},{5,4},{6,7},{7,6},{8,9},{9,8},{10,11... | collective-permute-start | bytes 393224 | tf_op jit(solution)/shard_map/ppermute | solution.py:241
  36.0 4.2 %collective-permute-start.14 = (bf16[2,64,128]{2,1,0:T(8,128)(2,1)S(1)}, bf16[2,64,128]{2,1,0:T(8,128)(2,1)S(1)}, u32[]{:S(2)}, u32[]{:S(2)}) collective-permute-start(bf16[2,64,128]{2,1,0:T(8,128)(2,1)S(1)} %reduce-precision_convert_fusion), channel_id=1, source_target_pairs={{0,32},{1,33},{32,0},{33,1},{64,96},{65,97},{96,64},{97,65},{128,1... | collective-permute-start | bytes 98312 | tf_op jit(solution)/shard_map/ppermute | solution.py:255
  36.5 3.7 %collective-permute-start.13 = (bf16[2,64,128]{2,1,0:T(8,128)(2,1)S(1)}, bf16[2,64,128]{2,1,0:T(8,128)(2,1)S(1)}, u32[]{:S(2)}, u32[]{:S(2)}) collective-permute-start(bf16[2,64,128]{2,1,0:T(8,128)(2,1)S(1)} %reduce-precision_convert_fusion), channel_id=1, source_target_pairs={{0,33},{1,32},{32,1},{33,0},{64,97},{65,96},{96,65},{97,64},{128,1... | collective-permute-start | bytes 98312 | tf_op jit(solution)/shard_map/ppermute | solution.py:255
  36.7 3.5 %collective-permute-start.12 = (bf16[2,64,128]{2,1,0:T(8,128)(2,1)S(1)}, bf16[2,64,128]{2,1,0:T(8,128)(2,1)S(1)}, u32[]{:S(2)}, u32[]{:S(2)}) collective-permute-start(bf16[2,64,128]{2,1,0:T(8,128)(2,1)S(1)} %reduce-precision_convert_fusion), channel_id=1, source_target_pairs={{0,1},{1,0},{32,33},{33,32},{64,65},{65,64},{96,97},{97,96},{128,1... | collective-permute-start | bytes 98312 | tf_op jit(solution)/shard_map/ppermute | solution.py:255
  40.2 5.5 %collective-permute-start.17 = (bf16[2,64,128]{2,1,0:T(8,128)(2,1)S(1)}, bf16[2,64,128]{2,1,0:T(8,128)(2,1)S(1)}, u32[]{:S(2)}, u32[]{:S(2)}) collective-permute-start(bf16[2,64,128]{2,1,0:T(8,128)(2,1)S(1)} %get-tuple-element.54), channel_id=1, source_target_pairs={{0,4},{2,6},{4,0},{6,2},{1,5},{3,7},{5,1},{7,3},{8,12},{10,14},{12... | collective-permute-start | bytes 98312 | tf_op jit(solution)/shard_map/ppermute | solution.py:255
  42.0 5.4 %collective-permute-start.16 = (bf16[2,64,128]{2,1,0:T(8,128)(2,1)S(1)}, bf16[2,64,128]{2,1,0:T(8,128)(2,1)S(1)}, u32[]{:S(2)}, u32[]{:S(2)}) collective-permute-start(bf16[2,64,128]{2,1,0:T(8,128)(2,1)S(1)} %get-tuple-element.54), channel_id=1, source_target_pairs={{0,6},{2,4},{4,2},{6,0},{1,7},{3,5},{5,3},{7,1},{8,14},{10,12},{12... | collective-permute-start | bytes 98312 | tf_op jit(solution)/shard_map/ppermute | solution.py:255
  45.5 3.9 %collective-permute-start.15 = (bf16[2,64,128]{2,1,0:T(8,128)(2,1)S(1)}, bf16[2,64,128]{2,1,0:T(8,128)(2,1)S(1)}, u32[]{:S(2)}, u32[]{:S(2)}) collective-permute-start(bf16[2,64,128]{2,1,0:T(8,128)(2,1)S(1)} %get-tuple-element.54), channel_id=1, source_target_pairs={{0,2},{2,0},{4,6},{6,4},{1,3},{3,1},{5,7},{7,5},{8,10},{10,8},{12,... | collective-permute-start | bytes 98312 | tf_op jit(solution)/shard_map/ppermute | solution.py:255
  49.4 5.5 %collective-permute-start.20 = (bf16[2,64,128]{2,1,0:T(8,128)(2,1)S(1)}, bf16[2,64,128]{2,1,0:T(8,128)(2,1)S(1)}, u32[]{:S(2)}, u32[]{:S(2)}) collective-permute-start(bf16[2,64,128]{2,1,0:T(8,128)(2,1)S(1)} %fusion), channel_id=1, source_target_pairs={{0,16},{8,24},{16,0},{24,8},{1,17},{9,25},{17,1},{25,9},{2,18},{10... | collective-permute-start | bytes 98312 | tf_op jit(solution)/shard_map/ppermute | solution.py:255
  50.0 5.3 %collective-permute-start.19 = (bf16[2,64,128]{2,1,0:T(8,128)(2,1)S(1)}, bf16[2,64,128]{2,1,0:T(8,128)(2,1)S(1)}, u32[]{:S(2)}, u32[]{:S(2)}) collective-permute-start(bf16[2,64,128]{2,1,0:T(8,128)(2,1)S(1)} %fusion), channel_id=1, source_target_pairs={{0,24},{8,16},{16,8},{24,0},{1,25},{9,17},{17,9},{25,1},{2,26},{10... | collective-permute-start | bytes 98312 | tf_op jit(solution)/shard_map/ppermute | solution.py:255
  51.1 4.2 %collective-permute-start.18 = (bf16[2,64,128]{2,1,0:T(8,128)(2,1)S(1)}, bf16[2,64,128]{2,1,0:T(8,128)(2,1)S(1)}, u32[]{:S(2)}, u32[]{:S(2)}) collective-permute-start(bf16[2,64,128]{2,1,0:T(8,128)(2,1)S(1)} %fusion), channel_id=1, source_target_pairs={{0,8},{8,0},{16,24},{24,16},{1,9},{9,1},{17,25},{25,17},{2,10},{10... | collective-permute-start | bytes 98312 | tf_op jit(solution)/shard_map/ppermute | solution.py:255
  55.3 8.8 %collective-permute-start.23 = (bf16[2,64,128]{2,1,0:T(8,128)(2,1)S(1)}, bf16[2,64,128]{2,1,0:T(8,128)(2,1)S(1)}, u32[]{:S(2)}, u32[]{:S(2)}) collective-permute-start(bf16[2,64,128]{2,1,0:T(8,128)(2,1)S(1)} %get-tuple-element.52), channel_id=1, source_target_pairs={{0,128},{32,160},{64,192},{96,224},{128,0},{160,32},{192,64},{224,... | collective-permute-start | bytes 98312 | tf_op jit(solution)/shard_map/ppermute | solution.py:255
  58.2 6.1 %collective-permute-start.22 = (bf16[2,64,128]{2,1,0:T(8,128)(2,1)S(1)}, bf16[2,64,128]{2,1,0:T(8,128)(2,1)S(1)}, u32[]{:S(2)}, u32[]{:S(2)}) collective-permute-start(bf16[2,64,128]{2,1,0:T(8,128)(2,1)S(1)} %get-tuple-element.52), channel_id=1, source_target_pairs={{0,192},{32,224},{64,128},{96,160},{128,64},{160,96},{192,0},{224,... | collective-permute-start | bytes 98312 | tf_op jit(solution)/shard_map/ppermute | solution.py:255
  60.9 5.2 %collective-permute-start.21 = (bf16[2,64,128]{2,1,0:T(8,128)(2,1)S(1)}, bf16[2,64,128]{2,1,0:T(8,128)(2,1)S(1)}, u32[]{:S(2)}, u32[]{:S(2)}) collective-permute-start(bf16[2,64,128]{2,1,0:T(8,128)(2,1)S(1)} %get-tuple-element.52), channel_id=1, source_target_pairs={{0,64},{32,96},{64,0},{96,32},{128,192},{160,224},{192,128},{224,1... | collective-permute-start | bytes 98312 | tf_op jit(solution)/shard_map/ppermute | solution.py:255

commit v4 on v3

--- a/solution.py
+++ b/solution.py
@@ -82,7 +82,7 @@
     return jnp.dot(jnp.concatenate(picked, axis=1), tall, preferred_element_type=F32)
 
 
-def step_kernel(cols, live, send, x, rb, rd, rc, ra, blocks, v_out, x_out, oa, ob, oc, od, src):
+def step_kernel(cols, live, send, x, rb, rc, rd, ra, blocks, v_out, x_out, oa, ob, oc, od, src):
     side, layer = parities()
     place_rows(x, (ra, rb, rc, rd), src, side, layer)
     for i in range(x.shape[0]):
@@ -164,7 +164,7 @@
     w_out[...] = against([x[e] for e in own], [z[e] for e in own])
 
 
-def gather_kernel(rb, rd, rc, ra, z, w0, w1, w2, own, w_out):
+def gather_kernel(rb, rc, rd, ra, z, w0, w1, w2, own, w_out):
     side, layer = parities()
     numbers, _ = directions(side, layer)
     width = ra.shape[0]
@@ -177,14 +177,14 @@
     w_out[1] = jnp.concatenate([w2[...], own[...] + against(rows, z_rows)], axis=1)
 
 
-def last_kernel(cols, live, x, rb, rd, rc, ra, blocks, v_out, src):
+def last_kernel(cols, live, x, rb, rc, rd, ra, blocks, v_out, src):
     side, layer = parities()
     place_rows(x, (ra, rb, rc, rd), src, side, layer)
     for i in range(x.shape[0]):
         v_out[i] = product_of_row(i, cols, live, src, blocks)
 
 
-def final_kernel(v0, v1, v2, v3, w, basis, factor_out, out, sems):
+def final_kernel(v0, v1, v2, v3, w, basis, factor_hbm, out, factor_out, sems):
     count = 4
     size = w.shape[2] // 2
     sums = [w[s // 2][:, (s % 2) * size : (s % 2 + 1) * size] for s in range(count)]
@@ -213,7 +213,6 @@
     for s in range(1, count):
         add_column(s)
         write_basis(s - 1)
-    write_basis(count - 1)
     lane = lax.broadcasted_iota(jnp.int32, (w.shape[1], 128), 1)
     table = jnp.zeros((w.shape[1], 128), F32)
     for (m, s), value in factor.items():
@@ -221,6 +220,9 @@
     table = table.T
     for m in range(count):
         factor_out[m] = table[m * count : (m + 1) * count]
+    copies.append(pltpu.make_async_copy(factor_out, factor_hbm, sems.at[count]))
+    copies[-1].start()
+    write_basis(count - 1)
     for copy in copies:
         copy.wait()
 
@@ -240,7 +242,7 @@
     rc = lax.ppermute(oc, "gx", swaps(gx, 0))
     ra = lax.ppermute(oa, GY, swaps(gy, 0))
     rb = lax.ppermute(ob, GY, swaps(gy, 1))
-    return rb, rd, rc, ra
+    return rb, rc, rd, ra
 
 
 def rounded_to(x):
@@ -370,10 +372,14 @@
             jax.ShapeDtypeStruct((STEPS + 1, *start.shape), F32),
             jax.ShapeDtypeStruct((STEPS + 1, STEPS + 1, rhs), F32),
         ],
-        [pltpu.VMEM((STEPS + 1, *start.shape), F32), pltpu.SemaphoreType.DMA((STEPS + 1,))],
+        [
+            pltpu.VMEM((STEPS + 1, *start.shape), F32),
+            pltpu.VMEM((STEPS + 1, STEPS + 1, rhs), F32),
+            pltpu.SemaphoreType.DMA((STEPS + 2,)),
+        ],
         flops=1 << 22,
         nbytes=1 << 22,
-        out_specs=[pl.BlockSpec(memory_space=pl.ANY), VMEM],
+        out_specs=[pl.BlockSpec(memory_space=pl.ANY)] * 2,
     )(v0, v1, v2, v3, w)
     return basis, factor
 

time: 69.2 us -> 68.3 us (0.987)
  waiting for transfers between devices: 14.5 us -> 13.6 us
    ppermute x3, waiting for transfers between devices: 2.57 us -> 0.84 us  [exchange(): rc = lax.ppermute(oc, 'gx', swaps(gx, 0))]
    ppermute x3, starting transfers between devices: 3.08 us -> 4.6 us  [exchange(): rb = lax.ppermute(ob, GY, swaps(gy, 1))]
    ppermute x3, waiting for transfers between devices: 1.89 us -> 3.09 us  [exchange(): rd = lax.ppermute(od, 'gx', swaps(gx, 1))]
    ppermute x3, starting transfers between devices: 9.4 us -> 8.31 us  [exchange(): rd = lax.ppermute(od, 'gx', swaps(gx, 1))]
  transfers between devices with their start and end apart: 24 -> 24, of which waited for: 13 -> 12; matrix products, arithmetic and copies ran while one was open for 0% -> 0% of each run, Pallas kernels for 16% -> 16%
where the time goes in v4:
time: 68.3 us; the launch traced here: 67.9 us
  starting transfers between devices  34 us (50%)
  Pallas kernels  19.2 us (28%)
  waiting for transfers between devices  13.6 us (20%)
  between operations  0.98 us (1%)
    ppermute x12, starting transfers between devices, four_sum(): lax.ppermute(sent, axes, [(i, i ^ bits) for i in range(count)]).astype(F32)  17.4 us
    ppermute x12, waiting for transfers between devices, four_sum(): lax.ppermute(sent, axes, [(i, i ^ bits) for i in range(count)]).astype(F32)  9.61 us
    ppermute x3, starting transfers between devices, exchange(): rd = lax.ppermute(od, 'gx', swaps(gx, 1))  8.31 us
    pallas_call x2, Pallas kernels, step(): call(kernel, 'step', [SMEM] * 3 + [VMEM] * (6 + len(earlier)), [vector, r...  4.61 us
    ppermute x3, starting transfers between devices, exchange(): rb = lax.ppermute(ob, GY, swaps(gy, 1))  4.6 us
    pallas_call x1, Pallas kernels, on_device(): call(prepare_kernel, 'prepare', [HBM] * 4 + [VMEM], [jax.ShapeDtypeStruct...  3.66 us
    ppermute x3, waiting for transfers between devices, exchange(): rd = lax.ppermute(od, 'gx', swaps(gx, 1))  3.09 us
    ppermute x3, starting transfers between devices, exchange(): rc = lax.ppermute(oc, 'gx', swaps(gx, 0))  2.67 us
  transfers between devices with their start and end apart: 24, of which 12 were waited for; matrix products, arithmetic and copies ran while one was open for 0% of the time, Pallas kernels for 16%

profile of v4, /device:TPU:8, one launch (start us, length us, event | category | flops | bytes accessed | tf_op | source)
XLA Modules:
  0.0 67.9 jit_solution(6085086082486293977)
XLA Ops:
  0.6 1.1 %first.1 = (f32[8,64,256]{2,1,0:T(8,128)S(1)}, s32[1,4,4]{2,1,0:T(4,128)S(1)}, bf16[8,64,256]{2,1,0:T(8,128)(2,1)S(1)}, bf16[4,64,256]{2,1,0:T(8,128)(2,1)S(1)},...) custom-call(s32[1,4,4]{2,1,0:T(4,128)} %send_hbm.1, ...), custom_call_target="tpu_custom_call" | custom-call | flops 1048576 | bytes 1048576 | tf_op jit(solution)/shard_map/first/pallas_call | solution.py:283
  1.9 2.0 %collective-permute-start.1 = (bf16[4,64,256]{2,1,0:T(8,128)(2,1)S(1)}, bf16[4,64,256]{2,1,0:T(8,128)(2,1)S(1)}, u32[]{:S(2)}, u32[]{:S(2)}) collective-permute-start(bf16[4,64,256]{2,1,0:T(8,128)(2,1)S(1)} %get-tuple-element.33), channel_id=1, source_target_pairs={{0,32},{32,0},{64,96},{96,64},{128,160},{160,128},{192,224},{224,1... | collective-permute-start | bytes 393224 | tf_op jit(solution)/shard_map/ppermute | solution.py:242
  3.9 4.9 %collective-permute-start.2 = (bf16[4,64,256]{2,1,0:T(8,128)(2,1)S(1)}, bf16[4,64,256]{2,1,0:T(8,128)(2,1)S(1)}, u32[]{:S(2)}, u32[]{:S(2)}) collective-permute-start(bf16[4,64,256]{2,1,0:T(8,128)(2,1)S(1)} %get-tuple-element.34), channel_id=1, source_target_pairs={{32,64},{64,32},{96,128},{128,96},{160,192},{192,160},{224,0},{0,2... | collective-permute-start | bytes 393224 | tf_op jit(solution)/shard_map/ppermute | solution.py:241
  8.8 1.0 %collective-permute-start.3 = (bf16[4,64,256]{2,1,0:T(8,128)(2,1)S(1)}, bf16[4,64,256]{2,1,0:T(8,128)(2,1)S(1)}, u32[]{:S(2)}, u32[]{:S(2)}) collective-permute-start(bf16[4,64,256]{2,1,0:T(8,128)(2,1)S(1)} %get-tuple-element.35), channel_id=1, source_target_pairs={{0,1},{1,0},{2,3},{3,2},{4,5},{5,4},{6,7},{7,6},{8,9},{9,8},{10,11... | collective-permute-start | bytes 393224 | tf_op jit(solution)/shard_map/ppermute | solution.py:243
  9.9 3.7 %prepare.1 = (bf16[8,8,256,256]{3,2,1,0:T(8,128)(2,1)S(1)}, s32[8,8]{1,0:T(8,128)S(1)}, s32[8]{0:T(128)S(1)}, bf16[8,64,256]{2,1,0:T(8,128)(2,1)S(1)}, bf16[8,64...) custom-call(bf16[8,8,256,256]{3,2,1,0:T(8,128)(2,1)} %blocks_hbm.1, f32[64,8,256]{2,1,0:T(8,128)} %sketch_hbm.1, ...), custom_call_target="tpu_custom_call" | custom-call | flops 50331648 | bytes 8388608 | tf_op jit(solution)/shard_map/prepare/pallas_call | solution.py:293
  13.6 2.3 %step.2 = (f32[8,64,256]{2,1,0:T(8,128)S(1)}, bf16[8,64,256]{2,1,0:T(8,128)(2,1)S(1)}, bf16[4,64,256]{2,1,0:T(8,128)(2,1)S(1)}, bf16[4,64,256]{2,1,0:T(8,128)(2,...) custom-call(s32[8,8]{1,0:T(8,128)S(1)} %get-tuple-element.28.refs_0_.cols, ...), custom_call_target="tpu_custom_call" | custom-call | flops 536870912 | bytes 8388608 | tf_op jit(solution)/shard_map/step/pallas_call | solution.py:316
  15.9 4.2 %collective-permute-start.4 = (bf16[4,64,256]{2,1,0:T(8,128)(2,1)S(1)}, bf16[4,64,256]{2,1,0:T(8,128)(2,1)S(1)}, u32[]{:S(2)}, u32[]{:S(2)}) collective-permute-start(bf16[4,64,256]{2,1,0:T(8,128)(2,1)S(1)} %get-tuple-element.39), channel_id=1, source_target_pairs={{1,2},{2,1},{3,4},{4,3},{5,6},{6,5},{7,8},{8,7},{9,10},{10,9},{11,... | collective-permute-start | bytes 393224 | tf_op jit(solution)/shard_map/ppermute | solution.py:244
  20.1 2.0 %collective-permute-start.6 = (bf16[4,64,256]{2,1,0:T(8,128)(2,1)S(1)}, bf16[4,64,256]{2,1,0:T(8,128)(2,1)S(1)}, u32[]{:S(2)}, u32[]{:S(2)}) collective-permute-start(bf16[4,64,256]{2,1,0:T(8,128)(2,1)S(1)} %get-tuple-element.41), channel_id=1, source_target_pairs={{32,64},{64,32},{96,128},{128,96},{160,192},{192,160},{224,0},{0,2... | collective-permute-start | bytes 393224 | tf_op jit(solution)/shard_map/ppermute | solution.py:241
  22.1 2.0 %spread.1.refs_9_.refs_4_ = f32[25,64,256]{2,1,0:T(8,128)S(1)} custom-call(s32[8,8]{1,0:T(8,128)S(1)} %get-tuple-element.28.refs_0_.cols, s32[8]{0:T(128)S(1)} %get-tuple-element.29.refs_1_.live, bf16[8,64,256]{2,1,0:T(8,128)(2,1)S(1)} %get-tuple-element.43.refs_2_.high, bf16[8,8,256,256]{3,2,1,0:T(8,128)(2,1)S(1)} %get-tuple-element.36.refs_8_.refs_3_.blocks), custom_call_target="tpu_custom_call" | custom-call | flops 536870912 | bytes 4194304 | tf_op jit(solution)/shard_map/spread/pallas_call | solution.py:343
  24.5 0.6 collective-permute-done.5.refs_5_
  25.0 1.2 %collective-permute-done.6.refs_6_ = bf16[4,64,256]{2,1,0:T(8,128)(2,1)S(1)} collective-permute-done((bf16[4,64,256]{2,1,0:T(8,128)(2,1)S(1)}, bf16[4,64,256]{2,1,0:T(8,128)(2,1)S(1)}, u32[]{:S(2)}, u32[]{:S(2)}) %collective-permute-start.6) | collective-permute-done | bytes 131104 | tf_op jit(solution)/shard_map/ppermute | solution.py:241
  26.2 2.3 %step.3 = (f32[8,64,256]{2,1,0:T(8,128)S(1)}, bf16[8,64,256]{2,1,0:T(8,128)(2,1)S(1)}, bf16[4,64,256]{2,1,0:T(8,128)(2,1)S(1)}, bf16[4,64,256]{2,1,0:T(8,128)(2,...) custom-call(s32[8,8]{1,0:T(8,128)S(1)} %get-tuple-element.28.refs_0_.cols, ...), custom_call_target="tpu_custom_call" | custom-call | flops 536870912 | bytes 8388608 | tf_op jit(solution)/shard_map/step/pallas_call | solution.py:316
  28.9 0.7 collective-permute-start.9
  29.5 1.4 %collective-permute-start.10 = (bf16[4,64,256]{2,1,0:T(8,128)(2,1)S(1)}, bf16[4,64,256]{2,1,0:T(8,128)(2,1)S(1)}, u32[]{:S(2)}, u32[]{:S(2)}) collective-permute-start(bf16[4,64,256]{2,1,0:T(8,128)(2,1)S(1)} %get-tuple-element.49), channel_id=1, source_target_pairs={{32,64},{64,32},{96,128},{128,96},{160,192},{192,160},{224,0},{0,2... | collective-permute-start | bytes 393224 | tf_op jit(solution)/shard_map/ppermute | solution.py:241
  30.9 2.0 %respread.1.z = f32[25,64,256]{2,1,0:T(8,128)S(1)} custom-call(s32[8,8]{1,0:T(8,128)S(1)} %get-tuple-element.28.refs_0_.cols, s32[8]{0:T(128)S(1)} %get-tuple-element.29.refs_1_.live, bf16[8,64,256]{2,1,0:T(8,128)(2,1)S(1)} %get-tuple-element.43.refs_2_.high, bf16[8,8,256,256]{3,2,1,0:T(8,128)(2,1)S(1)} %get-tuple-element.36.refs_8_.refs_3_.blocks, ...), custom_call_target="tpu_custom_call" | custom-call | flops 536870912 | bytes 4194304 | tf_op jit(solution)/shard_map/respread/pallas_call | solution.py:347
  33.9 1.9 %collective-permute-done.10.rd = bf16[4,64,256]{2,1,0:T(8,128)(2,1)S(1)} collective-permute-done((bf16[4,64,256]{2,1,0:T(8,128)(2,1)S(1)}, bf16[4,64,256]{2,1,0:T(8,128)(2,1)S(1)}, u32[]{:S(2)}, u32[]{:S(2)}) %collective-permute-start.10) | collective-permute-done | bytes 131104 | tf_op jit(solution)/shard_map/ppermute | solution.py:241
  35.7 0.5 gather.1
  36.5 2.0 %collective-permute-start.12 = (bf16[2,64,128]{2,1,0:T(8,128)(2,1)S(1)}, bf16[2,64,128]{2,1,0:T(8,128)(2,1)S(1)}, u32[]{:S(2)}, u32[]{:S(2)}) collective-permute-start(bf16[2,64,128]{2,1,0:T(8,128)(2,1)S(1)} %reduce-precision_convert_fusion), channel_id=1, source_target_pairs={{0,1},{1,0},{32,33},{33,32},{64,65},{65,64},{96,97},{97,96},{128,1... | collective-permute-start | bytes 98312 | tf_op jit(solution)/shard_map/ppermute | solution.py:257
  38.5 1.8 %collective-permute-done.14 = bf16[2,64,128]{2,1,0:T(8,128)(2,1)S(1)} collective-permute-done((bf16[2,64,128]{2,1,0:T(8,128)(2,1)S(1)}, bf16[2,64,128]{2,1,0:T(8,128)(2,1)S(1)}, u32[]{:S(2)}, u32[]{:S(2)}) %collective-permute-start.14) | collective-permute-done | bytes 32800 | tf_op jit(solution)/shard_map/ppermute | solution.py:257
  40.3 0.7 %collective-permute-start.17 = (bf16[2,64,128]{2,1,0:T(8,128)(2,1)S(1)}, bf16[2,64,128]{2,1,0:T(8,128)(2,1)S(1)}, u32[]{:S(2)}, u32[]{:S(2)}) collective-permute-start(bf16[2,64,128]{2,1,0:T(8,128)(2,1)S(1)} %get-tuple-element.54), channel_id=1, source_target_pairs={{0,4},{2,6},{4,0},{6,2},{1,5},{3,7},{5,1},{7,3},{8,12},{10,14},{12... | collective-permute-start | bytes 98312 | tf_op jit(solution)/shard_map/ppermute | solution.py:257
  41.0 4.3 %collective-permute-start.16 = (bf16[2,64,128]{2,1,0:T(8,128)(2,1)S(1)}, bf16[2,64,128]{2,1,0:T(8,128)(2,1)S(1)}, u32[]{:S(2)}, u32[]{:S(2)}) collective-permute-start(bf16[2,64,128]{2,1,0:T(8,128)(2,1)S(1)} %get-tuple-element.54), channel_id=1, source_target_pairs={{0,6},{2,4},{4,2},{6,0},{1,7},{3,5},{5,3},{7,1},{8,14},{10,12},{12... | collective-permute-start | bytes 98312 | tf_op jit(solution)/shard_map/ppermute | solution.py:257
  45.8 1.4 %collective-permute-done.16 = bf16[2,64,128]{2,1,0:T(8,128)(2,1)S(1)} collective-permute-done((bf16[2,64,128]{2,1,0:T(8,128)(2,1)S(1)}, bf16[2,64,128]{2,1,0:T(8,128)(2,1)S(1)}, u32[]{:S(2)}, u32[]{:S(2)}) %collective-permute-start.16) | collective-permute-done | bytes 32800 | tf_op jit(solution)/shard_map/ppermute | solution.py:257
  47.2 2.0 %collective-permute-done.15 = bf16[2,64,128]{2,1,0:T(8,128)(2,1)S(1)} collective-permute-done((bf16[2,64,128]{2,1,0:T(8,128)(2,1)S(1)}, bf16[2,64,128]{2,1,0:T(8,128)(2,1)S(1)}, u32[]{:S(2)}, u32[]{:S(2)}) %collective-permute-start.15) | collective-permute-done | bytes 32800 | tf_op jit(solution)/shard_map/ppermute | solution.py:257
  49.4 0.9 %collective-permute-start.19 = (bf16[2,64,128]{2,1,0:T(8,128)(2,1)S(1)}, bf16[2,64,128]{2,1,0:T(8,128)(2,1)S(1)}, u32[]{:S(2)}, u32[]{:S(2)}) collective-permute-start(bf16[2,64,128]{2,1,0:T(8,128)(2,1)S(1)} %fusion), channel_id=1, source_target_pairs={{0,24},{8,16},{16,8},{24,0},{1,25},{9,17},{17,9},{25,1},{2,26},{10... | collective-permute-start | bytes 98312 | tf_op jit(solution)/shard_map/ppermute | solution.py:257
  50.2 2.6 %collective-permute-start.18 = (bf16[2,64,128]{2,1,0:T(8,128)(2,1)S(1)}, bf16[2,64,128]{2,1,0:T(8,128)(2,1)S(1)}, u32[]{:S(2)}, u32[]{:S(2)}) collective-permute-start(bf16[2,64,128]{2,1,0:T(8,128)(2,1)S(1)} %fusion), channel_id=1, source_target_pairs={{0,8},{8,0},{16,24},{24,16},{1,9},{9,1},{17,25},{25,17},{2,10},{10... | collective-permute-start | bytes 98312 | tf_op jit(solution)/shard_map/ppermute | solution.py:257
  52.8 2.0 %collective-permute-done.20 = bf16[2,64,128]{2,1,0:T(8,128)(2,1)S(1)} collective-permute-done((bf16[2,64,128]{2,1,0:T(8,128)(2,1)S(1)}, bf16[2,64,128]{2,1,0:T(8,128)(2,1)S(1)}, u32[]{:S(2)}, u32[]{:S(2)}) %collective-permute-start.20) | collective-permute-done | bytes 32800 | tf_op jit(solution)/shard_map/ppermute | solution.py:257
  55.0 4.1 %collective-permute-start.23 = (bf16[2,64,128]{2,1,0:T(8,128)(2,1)S(1)}, bf16[2,64,128]{2,1,0:T(8,128)(2,1)S(1)}, u32[]{:S(2)}, u32[]{:S(2)}) collective-permute-start(bf16[2,64,128]{2,1,0:T(8,128)(2,1)S(1)} %get-tuple-element.52), channel_id=1, source_target_pairs={{0,128},{32,160},{64,192},{96,224},{128,0},{160,32},{192,64},{224,... | collective-permute-start | bytes 98312 | tf_op jit(solution)/shard_map/ppermute | solution.py:257
  59.1 1.4 %collective-permute-start.22 = (bf16[2,64,128]{2,1,0:T(8,128)(2,1)S(1)}, bf16[2,64,128]{2,1,0:T(8,128)(2,1)S(1)}, u32[]{:S(2)}, u32[]{:S(2)}) collective-permute-start(bf16[2,64,128]{2,1,0:T(8,128)(2,1)S(1)} %get-tuple-element.52), channel_id=1, source_target_pairs={{0,192},{32,224},{64,128},{96,160},{128,64},{160,96},{192,0},{224,... | collective-permute-start | bytes 98312 | tf_op jit(solution)/shard_map/ppermute | solution.py:257
  60.5 1.1 %collective-permute-start.21 = (bf16[2,64,128]{2,1,0:T(8,128)(2,1)S(1)}, bf16[2,64,128]{2,1,0:T(8,128)(2,1)S(1)}, u32[]{:S(2)}, u32[]{:S(2)}) collective-permute-start(bf16[2,64,128]{2,1,0:T(8,128)(2,1)S(1)} %get-tuple-element.52), channel_id=1, source_target_pairs={{0,64},{32,96},{64,0},{96,32},{128,192},{160,224},{192,128},{224,1... | collective-permute-start | bytes 98312 | tf_op jit(solution)/shard_map/ppermute | solution.py:257
  61.6 2.2 %last.1.v3 = f32[8,64,256]{2,1,0:T(8,128)S(1)} custom-call(s32[8,8]{1,0:T(8,128)S(1)} %get-tuple-element.28.refs_0_.cols, s32[8]{0:T(128)S(1)} %get-tuple-element.29.refs_1_.live, bf16[8,64,256]{2,1,0:T(8,128)(2,1)S(1)} %get-tuple-element.46.x, bf16[4,64,256]{2,1,0:T(8,128)(2,1)S(1)} %collective-permute-done.8.rb, ...), custom_call_target="tpu_custom_call" | custom-call | flops 536870912 | bytes 8388608 | tf_op jit(solution)/shard_map/last/pallas_call | solution.py:357
  63.8 1.4 %collective-permute-done.22 = bf16[2,64,128]{2,1,0:T(8,128)(2,1)S(1)} collective-permute-done((bf16[2,64,128]{2,1,0:T(8,128)(2,1)S(1)}, bf16[2,64,128]{2,1,0:T(8,128)(2,1)S(1)}, u32[]{:S(2)}, u32[]{:S(2)}) %collective-permute-start.22) | collective-permute-done | bytes 32800 | tf_op jit(solution)/shard_map/ppermute | solution.py:257
  65.7 2.1 %final.1 = (f32[4,8,64,256]{3,2,1,0:T(8,128)}, f32[4,4,64]{2,1,0:T(4,128)}) custom-call(f32[8,64,256]{2,1,0:T(8,128)S(1)} %get-tuple-element.27.start.v0, f32[8,64,256]{2,1,0:T(8,128)S(1)} %get-tuple-element.37.v.v1, f32[8,64,256]{2,1,0:T(8,128)S(1)} %get-tuple-element.45.v.v2, f32[8,64,256]{2,1,0:T(8,128)S(1)} %last.1.v3, f32[2,64,128]{2,1,0:T(8,128)S(1)} %add_add_fusion.w), custom_call_target="tpu_custom_call" | custom-call | flops 4194304 | bytes 4194304 | tf_op jit(solution)/shard_map/final/pallas_call | solution.py:367
  (33 shorter events, 3.1 us)
Async XLA Ops:
  1.8 11.8 %collective-permute-start = (bf16[4,64,256]{2,1,0:T(8,128)(2,1)S(1)}, bf16[4,64,256]{2,1,0:T(8,128)(2,1)S(1)}, u32[]{:S(2)}, u32[]{:S(2)}) collective-permute-start(bf16[4,64,256]{2,1,0:T(8,128)(2,1)S(1)} %get-tuple-element.32), channel_id=1, source_target_pairs={{1,2},{2,1},{3,4},{4,3},{5,6},{6,5},{7,8},{8,7},{9,10},{10,9},{11,... | collective-permute-start | bytes 393224 | tf_op jit(solution)/shard_map/ppermute | solution.py:244
  1.9 11.7 %collective-permute-start.1 = (bf16[4,64,256]{2,1,0:T(8,128)(2,1)S(1)}, bf16[4,64,256]{2,1,0:T(8,128)(2,1)S(1)}, u32[]{:S(2)}, u32[]{:S(2)}) collective-permute-start(bf16[4,64,256]{2,1,0:T(8,128)(2,1)S(1)} %get-tuple-element.33), channel_id=1, source_target_pairs={{0,32},{32,0},{64,96},{96,64},{128,160},{160,128},{192,224},{224,1... | collective-permute-start | bytes 393224 | tf_op jit(solution)/shard_map/ppermute | solution.py:242
  3.9 9.7 %collective-permute-start.2 = (bf16[4,64,256]{2,1,0:T(8,128)(2,1)S(1)}, bf16[4,64,256]{2,1,0:T(8,128)(2,1)S(1)}, u32[]{:S(2)}, u32[]{:S(2)}) collective-permute-start(bf16[4,64,256]{2,1,0:T(8,128)(2,1)S(1)} %get-tuple-element.34), channel_id=1, source_target_pairs={{32,64},{64,32},{96,128},{128,96},{160,192},{192,160},{224,0},{0,2... | collective-permute-start | bytes 393224 | tf_op jit(solution)/shard_map/ppermute | solution.py:241
  8.8 4.7 %collective-permute-start.3 = (bf16[4,64,256]{2,1,0:T(8,128)(2,1)S(1)}, bf16[4,64,256]{2,1,0:T(8,128)(2,1)S(1)}, u32[]{:S(2)}, u32[]{:S(2)}) collective-permute-start(bf16[4,64,256]{2,1,0:T(8,128)(2,1)S(1)} %get-tuple-element.35), channel_id=1, source_target_pairs={{0,1},{1,0},{2,3},{3,2},{4,5},{5,4},{6,7},{7,6},{8,9},{9,8},{10,11... | collective-permute-start | bytes 393224 | tf_op jit(solution)/shard_map/ppermute | solution.py:243
  15.9 8.6 %collective-permute-start.4 = (bf16[4,64,256]{2,1,0:T(8,128)(2,1)S(1)}, bf16[4,64,256]{2,1,0:T(8,128)(2,1)S(1)}, u32[]{:S(2)}, u32[]{:S(2)}) collective-permute-start(bf16[4,64,256]{2,1,0:T(8,128)(2,1)S(1)} %get-tuple-element.39), channel_id=1, source_target_pairs={{1,2},{2,1},{3,4},{4,3},{5,6},{6,5},{7,8},{8,7},{9,10},{10,9},{11,... | collective-permute-start | bytes 393224 | tf_op jit(solution)/shard_map/ppermute | solution.py:244
  20.0 5.0 %collective-permute-start.5 = (bf16[4,64,256]{2,1,0:T(8,128)(2,1)S(1)}, bf16[4,64,256]{2,1,0:T(8,128)(2,1)S(1)}, u32[]{:S(2)}, u32[]{:S(2)}) collective-permute-start(bf16[4,64,256]{2,1,0:T(8,128)(2,1)S(1)} %get-tuple-element.40), channel_id=1, source_target_pairs={{0,32},{32,0},{64,96},{96,64},{128,160},{160,128},{192,224},{224,1... | collective-permute-start | bytes 393224 | tf_op jit(solution)/shard_map/ppermute | solution.py:242
  20.1 6.2 %collective-permute-start.6 = (bf16[4,64,256]{2,1,0:T(8,128)(2,1)S(1)}, bf16[4,64,256]{2,1,0:T(8,128)(2,1)S(1)}, u32[]{:S(2)}, u32[]{:S(2)}) collective-permute-start(bf16[4,64,256]{2,1,0:T(8,128)(2,1)S(1)} %get-tuple-element.41), channel_id=1, source_target_pairs={{32,64},{64,32},{96,128},{128,96},{160,192},{192,160},{224,0},{0,2... | collective-permute-start | bytes 393224 | tf_op jit(solution)/shard_map/ppermute | solution.py:241
  22.1 4.2 %collective-permute-start.7 = (bf16[4,64,256]{2,1,0:T(8,128)(2,1)S(1)}, bf16[4,64,256]{2,1,0:T(8,128)(2,1)S(1)}, u32[]{:S(2)}, u32[]{:S(2)}) collective-permute-start(bf16[4,64,256]{2,1,0:T(8,128)(2,1)S(1)} %get-tuple-element.42), channel_id=1, source_target_pairs={{0,1},{1,0},{2,3},{3,2},{4,5},{5,4},{6,7},{7,6},{8,9},{9,8},{10,11... | collective-permute-start | bytes 393224 | tf_op jit(solution)/shard_map/ppermute | solution.py:243
  28.5 5.0 %collective-permute-start.8 = (bf16[4,64,256]{2,1,0:T(8,128)(2,1)S(1)}, bf16[4,64,256]{2,1,0:T(8,128)(2,1)S(1)}, u32[]{:S(2)}, u32[]{:S(2)}) collective-permute-start(bf16[4,64,256]{2,1,0:T(8,128)(2,1)S(1)} %get-tuple-element.47), channel_id=1, source_target_pairs={{1,2},{2,1},{3,4},{4,3},{5,6},{6,5},{7,8},{8,7},{9,10},{10,9},{11,... | collective-permute-start | bytes 393224 | tf_op jit(solution)/shard_map/ppermute | solution.py:244
  28.9 5.0 %collective-permute-start.9 = (bf16[4,64,256]{2,1,0:T(8,128)(2,1)S(1)}, bf16[4,64,256]{2,1,0:T(8,128)(2,1)S(1)}, u32[]{:S(2)}, u32[]{:S(2)}) collective-permute-start(bf16[4,64,256]{2,1,0:T(8,128)(2,1)S(1)} %get-tuple-element.48), channel_id=1, source_target_pairs={{0,32},{32,0},{64,96},{96,64},{128,160},{160,128},{192,224},{224,1... | collective-permute-start | bytes 393224 | tf_op jit(solution)/shard_map/ppermute | solution.py:242
  29.5 6.2 %collective-permute-start.10 = (bf16[4,64,256]{2,1,0:T(8,128)(2,1)S(1)}, bf16[4,64,256]{2,1,0:T(8,128)(2,1)S(1)}, u32[]{:S(2)}, u32[]{:S(2)}) collective-permute-start(bf16[4,64,256]{2,1,0:T(8,128)(2,1)S(1)} %get-tuple-element.49), channel_id=1, source_target_pairs={{32,64},{64,32},{96,128},{128,96},{160,192},{192,160},{224,0},{0,2... | collective-permute-start | bytes 393224 | tf_op jit(solution)/shard_map/ppermute | solution.py:241
  30.9 4.8 %collective-permute-start.11 = (bf16[4,64,256]{2,1,0:T(8,128)(2,1)S(1)}, bf16[4,64,256]{2,1,0:T(8,128)(2,1)S(1)}, u32[]{:S(2)}, u32[]{:S(2)}) collective-permute-start(bf16[4,64,256]{2,1,0:T(8,128)(2,1)S(1)} %get-tuple-element.50), channel_id=1, source_target_pairs={{0,1},{1,0},{2,3},{3,2},{4,5},{5,4},{6,7},{7,6},{8,9},{9,8},{10,11... | collective-permute-start | bytes 393224 | tf_op jit(solution)/shard_map/ppermute | solution.py:243
  36.2 4.0 %collective-permute-start.14 = (bf16[2,64,128]{2,1,0:T(8,128)(2,1)S(1)}, bf16[2,64,128]{2,1,0:T(8,128)(2,1)S(1)}, u32[]{:S(2)}, u32[]{:S(2)}) collective-permute-start(bf16[2,64,128]{2,1,0:T(8,128)(2,1)S(1)} %reduce-precision_convert_fusion), channel_id=1, source_target_pairs={{0,32},{1,33},{32,0},{33,1},{64,96},{65,97},{96,64},{97,65},{128,1... | collective-permute-start | bytes 98312 | tf_op jit(solution)/shard_map/ppermute | solution.py:257
  36.5 3.8 %collective-permute-start.13 = (bf16[2,64,128]{2,1,0:T(8,128)(2,1)S(1)}, bf16[2,64,128]{2,1,0:T(8,128)(2,1)S(1)}, u32[]{:S(2)}, u32[]{:S(2)}) collective-permute-start(bf16[2,64,128]{2,1,0:T(8,128)(2,1)S(1)} %reduce-precision_convert_fusion), channel_id=1, source_target_pairs={{0,33},{1,32},{32,1},{33,0},{64,97},{65,96},{96,65},{97,64},{128,1... | collective-permute-start | bytes 98312 | tf_op jit(solution)/shard_map/ppermute | solution.py:257
  36.5 3.8 %collective-permute-start.12 = (bf16[2,64,128]{2,1,0:T(8,128)(2,1)S(1)}, bf16[2,64,128]{2,1,0:T(8,128)(2,1)S(1)}, u32[]{:S(2)}, u32[]{:S(2)}) collective-permute-start(bf16[2,64,128]{2,1,0:T(8,128)(2,1)S(1)} %reduce-precision_convert_fusion), channel_id=1, source_target_pairs={{0,1},{1,0},{32,33},{33,32},{64,65},{65,64},{96,97},{97,96},{128,1... | collective-permute-start | bytes 98312 | tf_op jit(solution)/shard_map/ppermute | solution.py:257
  40.3 5.5 %collective-permute-start.17 = (bf16[2,64,128]{2,1,0:T(8,128)(2,1)S(1)}, bf16[2,64,128]{2,1,0:T(8,128)(2,1)S(1)}, u32[]{:S(2)}, u32[]{:S(2)}) collective-permute-start(bf16[2,64,128]{2,1,0:T(8,128)(2,1)S(1)} %get-tuple-element.54), channel_id=1, source_target_pairs={{0,4},{2,6},{4,0},{6,2},{1,5},{3,7},{5,1},{7,3},{8,12},{10,14},{12... | collective-permute-start | bytes 98312 | tf_op jit(solution)/shard_map/ppermute | solution.py:257
  41.0 6.2 %collective-permute-start.16 = (bf16[2,64,128]{2,1,0:T(8,128)(2,1)S(1)}, bf16[2,64,128]{2,1,0:T(8,128)(2,1)S(1)}, u32[]{:S(2)}, u32[]{:S(2)}) collective-permute-start(bf16[2,64,128]{2,1,0:T(8,128)(2,1)S(1)} %get-tuple-element.54), channel_id=1, source_target_pairs={{0,6},{2,4},{4,2},{6,0},{1,7},{3,5},{5,3},{7,1},{8,14},{10,12},{12... | collective-permute-start | bytes 98312 | tf_op jit(solution)/shard_map/ppermute | solution.py:257
  45.3 3.9 %collective-permute-start.15 = (bf16[2,64,128]{2,1,0:T(8,128)(2,1)S(1)}, bf16[2,64,128]{2,1,0:T(8,128)(2,1)S(1)}, u32[]{:S(2)}, u32[]{:S(2)}) collective-permute-start(bf16[2,64,128]{2,1,0:T(8,128)(2,1)S(1)} %get-tuple-element.54), channel_id=1, source_target_pairs={{0,2},{2,0},{4,6},{6,4},{1,3},{3,1},{5,7},{7,5},{8,10},{10,8},{12,... | collective-permute-start | bytes 98312 | tf_op jit(solution)/shard_map/ppermute | solution.py:257
  49.3 5.6 %collective-permute-start.20 = (bf16[2,64,128]{2,1,0:T(8,128)(2,1)S(1)}, bf16[2,64,128]{2,1,0:T(8,128)(2,1)S(1)}, u32[]{:S(2)}, u32[]{:S(2)}) collective-permute-start(bf16[2,64,128]{2,1,0:T(8,128)(2,1)S(1)} %fusion), channel_id=1, source_target_pairs={{0,16},{8,24},{16,0},{24,8},{1,17},{9,25},{17,1},{25,9},{2,18},{10... | collective-permute-start | bytes 98312 | tf_op jit(solution)/shard_map/ppermute | solution.py:257
  49.4 5.6 %collective-permute-start.19 = (bf16[2,64,128]{2,1,0:T(8,128)(2,1)S(1)}, bf16[2,64,128]{2,1,0:T(8,128)(2,1)S(1)}, u32[]{:S(2)}, u32[]{:S(2)}) collective-permute-start(bf16[2,64,128]{2,1,0:T(8,128)(2,1)S(1)} %fusion), channel_id=1, source_target_pairs={{0,24},{8,16},{16,8},{24,0},{1,25},{9,17},{17,9},{25,1},{2,26},{10... | collective-permute-start | bytes 98312 | tf_op jit(solution)/shard_map/ppermute | solution.py:257
  50.2 4.7 %collective-permute-start.18 = (bf16[2,64,128]{2,1,0:T(8,128)(2,1)S(1)}, bf16[2,64,128]{2,1,0:T(8,128)(2,1)S(1)}, u32[]{:S(2)}, u32[]{:S(2)}) collective-permute-start(bf16[2,64,128]{2,1,0:T(8,128)(2,1)S(1)} %fusion), channel_id=1, source_target_pairs={{0,8},{8,0},{16,24},{24,16},{1,9},{9,1},{17,25},{25,17},{2,10},{10... | collective-permute-start | bytes 98312 | tf_op jit(solution)/shard_map/ppermute | solution.py:257
  55.0 8.8 %collective-permute-start.23 = (bf16[2,64,128]{2,1,0:T(8,128)(2,1)S(1)}, bf16[2,64,128]{2,1,0:T(8,128)(2,1)S(1)}, u32[]{:S(2)}, u32[]{:S(2)}) collective-permute-start(bf16[2,64,128]{2,1,0:T(8,128)(2,1)S(1)} %get-tuple-element.52), channel_id=1, source_target_pairs={{0,128},{32,160},{64,192},{96,224},{128,0},{160,32},{192,64},{224,... | collective-permute-start | bytes 98312 | tf_op jit(solution)/shard_map/ppermute | solution.py:257
  59.1 6.1 %collective-permute-start.22 = (bf16[2,64,128]{2,1,0:T(8,128)(2,1)S(1)}, bf16[2,64,128]{2,1,0:T(8,128)(2,1)S(1)}, u32[]{:S(2)}, u32[]{:S(2)}) collective-permute-start(bf16[2,64,128]{2,1,0:T(8,128)(2,1)S(1)} %get-tuple-element.52), channel_id=1, source_target_pairs={{0,192},{32,224},{64,128},{96,160},{128,64},{160,96},{192,0},{224,... | collective-permute-start | bytes 98312 | tf_op jit(solution)/shard_map/ppermute | solution.py:257
  60.5 5.2 %collective-permute-start.21 = (bf16[2,64,128]{2,1,0:T(8,128)(2,1)S(1)}, bf16[2,64,128]{2,1,0:T(8,128)(2,1)S(1)}, u32[]{:S(2)}, u32[]{:S(2)}) collective-permute-start(bf16[2,64,128]{2,1,0:T(8,128)(2,1)S(1)} %get-tuple-element.52), channel_id=1, source_target_pairs={{0,64},{32,96},{64,0},{96,32},{128,192},{160,224},{192,128},{224,1... | collective-permute-start | bytes 98312 | tf_op jit(solution)/shard_map/ppermute | solution.py:257

commit v5 on v4

--- a/solution.py
+++ b/solution.py
@@ -146,11 +146,11 @@
             )
 
 
-def against(rows, z_rows):
+def against(rows, z_halves):
     left, right = [], []
-    for row, z_row in zip(rows, z_rows, strict=True):
+    for row, pair in zip(rows, z_halves, strict=True):
         left += [row, row]
-        right += list(halves(z_row))
+        right += list(pair)
     return lax.dot_general(
         jnp.concatenate(left, axis=1),
         jnp.concatenate(right, axis=1),
@@ -159,22 +159,24 @@
     )
 
 
-def own_kernel(x, z, w_out):
-    own = range(x.shape[0])
-    w_out[...] = against([x[e] for e in own], [z[e] for e in own])
-
-
-def gather_kernel(rb, rc, rd, ra, z, w0, w1, w2, own, w_out):
+def own_kernel(x, z, w_out, z_high, z_low):
+    count = x.shape[0]
+    w_out[...] = against([x[e] for e in range(count)], [halves(z[e]) for e in range(count)])
+    for e in range(z_high.shape[0]):
+        z_high[e], z_low[e] = halves(z[count + e])
+
+
+def gather_kernel(rb, rc, rd, ra, z_high, z_low, w0, w1, w2, own, w_out):
     side, layer = parities()
     numbers, _ = directions(side, layer)
     width = ra.shape[0]
-    count = z.shape[0] - 1 - 4 * width
-    rows, z_rows = [], []
+    rows, z_halves = [], []
     for ref, direction in zip((ra, rb, rc, rd), numbers, strict=True):
         rows += [ref[j] for j in range(width)]
-        z_rows += [z[count + direction * width + j] for j in range(width)]
+        places = [direction * width + j for j in range(width)]
+        z_halves += [(z_high[place], z_low[place]) for place in places]
     w_out[0] = jnp.concatenate([w0[...], w1[...]], axis=1)
-    w_out[1] = jnp.concatenate([w2[...], own[...] + against(rows, z_rows)], axis=1)
+    w_out[1] = jnp.concatenate([w2[...], own[...] + against(rows, z_halves)], axis=1)
 
 
 def last_kernel(cols, live, x, rb, rc, rd, ra, blocks, v_out, src):
@@ -345,15 +347,18 @@
     received = exchange(messages)
     (w2,) = sketch_of(v2, high, low)
     (z,) = spread("respread", half, rows, 1)(cols, live, high, here, z)
-    (own,) = call(own_kernel, "own", [VMEM] * 2, [part], flops=sketch_flops, nbytes=1 << 20)(x, z)
+    half_table = jax.ShapeDtypeStruct((4 * width, count, size), BF16)
+    own, z_high, z_low = call(
+        own_kernel, "own", [VMEM] * 2, [part] + [half_table] * 2, flops=sketch_flops, nbytes=1 << 20
+    )(x, z)
     (w,) = call(
         gather_kernel,
         "gather",
-        [VMEM] * 9,
+        [VMEM] * 10,
         [jax.ShapeDtypeStruct((2, rhs, 2 * count), F32)],
         flops=sketch_flops,
         nbytes=1 << 20,
-    )(*received, z, w0, w1, w2, own)
+    )(*received, z_high, z_low, w0, w1, w2, own)
     (v3,) = call(
         last_kernel,
         "last",

time: 68.3 us -> 68.3 us (level)
  no operation moved by 1% of the time
where the time goes in v5:
time: 68.3 us; the launch traced here: 67.9 us
  starting transfers between devices  34 us (50%)
  Pallas kernels  19.3 us (28%)
  waiting for transfers between devices  13.5 us (20%)
  between operations  0.98 us (1%)
    ppermute x12, starting transfers between devices, four_sum(): lax.ppermute(sent, axes, [(i, i ^ bits) for i in range(count)]).astype(F32)  17.4 us
    ppermute x12, waiting for transfers between devices, four_sum(): lax.ppermute(sent, axes, [(i, i ^ bits) for i in range(count)]).astype(F32)  9.62 us
    ppermute x3, starting transfers between devices, exchange(): rd = lax.ppermute(od, 'gx', swaps(gx, 1))  8.32 us
    pallas_call x2, Pallas kernels, step(): call(kernel, 'step', [SMEM] * 3 + [VMEM] * (6 + len(earlier)), [vector, r...  4.61 us
    ppermute x3, starting transfers between devices, exchange(): rb = lax.ppermute(ob, GY, swaps(gy, 1))  4.6 us
    pallas_call x1, Pallas kernels, on_device(): call(prepare_kernel, 'prepare', [HBM] * 4 + [VMEM], [jax.ShapeDtypeStruct...  3.66 us
    ppermute x3, waiting for transfers between devices, exchange(): rd = lax.ppermute(od, 'gx', swaps(gx, 1))  3.09 us
    ppermute x3, starting transfers between devices, exchange(): rc = lax.ppermute(oc, 'gx', swaps(gx, 0))  2.67 us
  transfers between devices with their start and end apart: 24, of which 12 were waited for; matrix products, arithmetic and copies ran while one was open for 0% of the time, Pallas kernels for 16%

profile of v5, /device:TPU:8, one launch (start us, length us, event | category | flops | bytes accessed | tf_op | source)
XLA Modules:
  0.0 67.9 jit_solution(11542748932191528784)
XLA Ops:
  0.6 1.1 %first.1 = (f32[8,64,256]{2,1,0:T(8,128)S(1)}, s32[1,4,4]{2,1,0:T(4,128)S(1)}, bf16[8,64,256]{2,1,0:T(8,128)(2,1)S(1)}, bf16[4,64,256]{2,1,0:T(8,128)(2,1)S(1)},...) custom-call(s32[1,4,4]{2,1,0:T(4,128)} %send_hbm.1, ...), custom_call_target="tpu_custom_call" | custom-call | flops 1048576 | bytes 1048576 | tf_op jit(solution)/shard_map/first/pallas_call | solution.py:285
  1.9 2.0 %collective-permute-start.1 = (bf16[4,64,256]{2,1,0:T(8,128)(2,1)S(1)}, bf16[4,64,256]{2,1,0:T(8,128)(2,1)S(1)}, u32[]{:S(2)}, u32[]{:S(2)}) collective-permute-start(bf16[4,64,256]{2,1,0:T(8,128)(2,1)S(1)} %get-tuple-element.36), channel_id=1, source_target_pairs={{0,32},{32,0},{64,96},{96,64},{128,160},{160,128},{192,224},{224,1... | collective-permute-start | bytes 393224 | tf_op jit(solution)/shard_map/ppermute | solution.py:244
  3.9 4.9 %collective-permute-start.2 = (bf16[4,64,256]{2,1,0:T(8,128)(2,1)S(1)}, bf16[4,64,256]{2,1,0:T(8,128)(2,1)S(1)}, u32[]{:S(2)}, u32[]{:S(2)}) collective-permute-start(bf16[4,64,256]{2,1,0:T(8,128)(2,1)S(1)} %get-tuple-element.37), channel_id=1, source_target_pairs={{32,64},{64,32},{96,128},{128,96},{160,192},{192,160},{224,0},{0,2... | collective-permute-start | bytes 393224 | tf_op jit(solution)/shard_map/ppermute | solution.py:243
  8.8 1.0 %collective-permute-start.3 = (bf16[4,64,256]{2,1,0:T(8,128)(2,1)S(1)}, bf16[4,64,256]{2,1,0:T(8,128)(2,1)S(1)}, u32[]{:S(2)}, u32[]{:S(2)}) collective-permute-start(bf16[4,64,256]{2,1,0:T(8,128)(2,1)S(1)} %get-tuple-element.38), channel_id=1, source_target_pairs={{0,1},{1,0},{2,3},{3,2},{4,5},{5,4},{6,7},{7,6},{8,9},{9,8},{10,11... | collective-permute-start | bytes 393224 | tf_op jit(solution)/shard_map/ppermute | solution.py:245
  9.9 3.7 %prepare.1 = (bf16[8,8,256,256]{3,2,1,0:T(8,128)(2,1)S(1)}, s32[8,8]{1,0:T(8,128)S(1)}, s32[8]{0:T(128)S(1)}, bf16[8,64,256]{2,1,0:T(8,128)(2,1)S(1)}, bf16[8,64...) custom-call(bf16[8,8,256,256]{3,2,1,0:T(8,128)(2,1)} %blocks_hbm.1, f32[64,8,256]{2,1,0:T(8,128)} %sketch_hbm.1, ...), custom_call_target="tpu_custom_call" | custom-call | flops 50331648 | bytes 8388608 | tf_op jit(solution)/shard_map/prepare/pallas_call | solution.py:295
  13.6 2.3 %step.2 = (f32[8,64,256]{2,1,0:T(8,128)S(1)}, bf16[8,64,256]{2,1,0:T(8,128)(2,1)S(1)}, bf16[4,64,256]{2,1,0:T(8,128)(2,1)S(1)}, bf16[4,64,256]{2,1,0:T(8,128)(2,...) custom-call(s32[8,8]{1,0:T(8,128)S(1)} %get-tuple-element.31.refs_0_.cols, ...), custom_call_target="tpu_custom_call" | custom-call | flops 536870912 | bytes 8388608 | tf_op jit(solution)/shard_map/step/pallas_call | solution.py:318
  15.9 4.2 %collective-permute-start.4 = (bf16[4,64,256]{2,1,0:T(8,128)(2,1)S(1)}, bf16[4,64,256]{2,1,0:T(8,128)(2,1)S(1)}, u32[]{:S(2)}, u32[]{:S(2)}) collective-permute-start(bf16[4,64,256]{2,1,0:T(8,128)(2,1)S(1)} %get-tuple-element.42), channel_id=1, source_target_pairs={{1,2},{2,1},{3,4},{4,3},{5,6},{6,5},{7,8},{8,7},{9,10},{10,9},{11,... | collective-permute-start | bytes 393224 | tf_op jit(solution)/shard_map/ppermute | solution.py:246
  20.1 2.0 %collective-permute-start.6 = (bf16[4,64,256]{2,1,0:T(8,128)(2,1)S(1)}, bf16[4,64,256]{2,1,0:T(8,128)(2,1)S(1)}, u32[]{:S(2)}, u32[]{:S(2)}) collective-permute-start(bf16[4,64,256]{2,1,0:T(8,128)(2,1)S(1)} %get-tuple-element.44), channel_id=1, source_target_pairs={{32,64},{64,32},{96,128},{128,96},{160,192},{192,160},{224,0},{0,2... | collective-permute-start | bytes 393224 | tf_op jit(solution)/shard_map/ppermute | solution.py:243
  22.1 2.0 %spread.1.refs_9_.refs_4_ = f32[25,64,256]{2,1,0:T(8,128)S(1)} custom-call(s32[8,8]{1,0:T(8,128)S(1)} %get-tuple-element.31.refs_0_.cols, s32[8]{0:T(128)S(1)} %get-tuple-element.32.refs_1_.live, bf16[8,64,256]{2,1,0:T(8,128)(2,1)S(1)} %get-tuple-element.46.refs_2_.high, bf16[8,8,256,256]{3,2,1,0:T(8,128)(2,1)S(1)} %get-tuple-element.39.refs_8_.refs_3_.blocks), custom_call_target="tpu_custom_call" | custom-call | flops 536870912 | bytes 4194304 | tf_op jit(solution)/shard_map/spread/pallas_call | solution.py:345
  24.5 0.6 collective-permute-done.5.refs_5_
  25.0 1.2 %collective-permute-done.6.refs_6_ = bf16[4,64,256]{2,1,0:T(8,128)(2,1)S(1)} collective-permute-done((bf16[4,64,256]{2,1,0:T(8,128)(2,1)S(1)}, bf16[4,64,256]{2,1,0:T(8,128)(2,1)S(1)}, u32[]{:S(2)}, u32[]{:S(2)}) %collective-permute-start.6) | collective-permute-done | bytes 131104 | tf_op jit(solution)/shard_map/ppermute | solution.py:243
  26.2 2.3 %step.3 = (f32[8,64,256]{2,1,0:T(8,128)S(1)}, bf16[8,64,256]{2,1,0:T(8,128)(2,1)S(1)}, bf16[4,64,256]{2,1,0:T(8,128)(2,1)S(1)}, bf16[4,64,256]{2,1,0:T(8,128)(2,...) custom-call(s32[8,8]{1,0:T(8,128)S(1)} %get-tuple-element.31.refs_0_.cols, ...), custom_call_target="tpu_custom_call" | custom-call | flops 536870912 | bytes 8388608 | tf_op jit(solution)/shard_map/step/pallas_call | solution.py:318
  28.9 0.7 collective-permute-start.9
  29.5 1.4 %collective-permute-start.10 = (bf16[4,64,256]{2,1,0:T(8,128)(2,1)S(1)}, bf16[4,64,256]{2,1,0:T(8,128)(2,1)S(1)}, u32[]{:S(2)}, u32[]{:S(2)}) collective-permute-start(bf16[4,64,256]{2,1,0:T(8,128)(2,1)S(1)} %get-tuple-element.52), channel_id=1, source_target_pairs={{32,64},{64,32},{96,128},{128,96},{160,192},{192,160},{224,0},{0,2... | collective-permute-start | bytes 393224 | tf_op jit(solution)/shard_map/ppermute | solution.py:243
  30.9 2.0 %respread.1.z = f32[25,64,256]{2,1,0:T(8,128)S(1)} custom-call(s32[8,8]{1,0:T(8,128)S(1)} %get-tuple-element.31.refs_0_.cols, s32[8]{0:T(128)S(1)} %get-tuple-element.32.refs_1_.live, bf16[8,64,256]{2,1,0:T(8,128)(2,1)S(1)} %get-tuple-element.46.refs_2_.high, bf16[8,8,256,256]{3,2,1,0:T(8,128)(2,1)S(1)} %get-tuple-element.39.refs_8_.refs_3_.blocks, ...), custom_call_target="tpu_custom_call" | custom-call | flops 536870912 | bytes 4194304 | tf_op jit(solution)/shard_map/respread/pallas_call | solution.py:349
  33.8 1.9 %collective-permute-done.10.rd = bf16[4,64,256]{2,1,0:T(8,128)(2,1)S(1)} collective-permute-done((bf16[4,64,256]{2,1,0:T(8,128)(2,1)S(1)}, bf16[4,64,256]{2,1,0:T(8,128)(2,1)S(1)}, u32[]{:S(2)}, u32[]{:S(2)}) %collective-permute-start.10) | collective-permute-done | bytes 131104 | tf_op jit(solution)/shard_map/ppermute | solution.py:243
  35.7 0.5 gather.1
  36.5 2.0 %collective-permute-start.12 = (bf16[2,64,128]{2,1,0:T(8,128)(2,1)S(1)}, bf16[2,64,128]{2,1,0:T(8,128)(2,1)S(1)}, u32[]{:S(2)}, u32[]{:S(2)}) collective-permute-start(bf16[2,64,128]{2,1,0:T(8,128)(2,1)S(1)} %reduce-precision_convert_fusion), channel_id=1, source_target_pairs={{0,1},{1,0},{32,33},{33,32},{64,65},{65,64},{96,97},{97,96},{128,1... | collective-permute-start | bytes 98312 | tf_op jit(solution)/shard_map/ppermute | solution.py:259
  38.5 1.8 %collective-permute-done.14 = bf16[2,64,128]{2,1,0:T(8,128)(2,1)S(1)} collective-permute-done((bf16[2,64,128]{2,1,0:T(8,128)(2,1)S(1)}, bf16[2,64,128]{2,1,0:T(8,128)(2,1)S(1)}, u32[]{:S(2)}, u32[]{:S(2)}) %collective-permute-start.14) | collective-permute-done | bytes 32800 | tf_op jit(solution)/shard_map/ppermute | solution.py:259
  40.3 0.8 %collective-permute-start.17 = (bf16[2,64,128]{2,1,0:T(8,128)(2,1)S(1)}, bf16[2,64,128]{2,1,0:T(8,128)(2,1)S(1)}, u32[]{:S(2)}, u32[]{:S(2)}) collective-permute-start(bf16[2,64,128]{2,1,0:T(8,128)(2,1)S(1)} %get-tuple-element.60), channel_id=1, source_target_pairs={{0,4},{2,6},{4,0},{6,2},{1,5},{3,7},{5,1},{7,3},{8,12},{10,14},{12... | collective-permute-start | bytes 98312 | tf_op jit(solution)/shard_map/ppermute | solution.py:259
  41.1 4.3 %collective-permute-start.16 = (bf16[2,64,128]{2,1,0:T(8,128)(2,1)S(1)}, bf16[2,64,128]{2,1,0:T(8,128)(2,1)S(1)}, u32[]{:S(2)}, u32[]{:S(2)}) collective-permute-start(bf16[2,64,128]{2,1,0:T(8,128)(2,1)S(1)} %get-tuple-element.60), channel_id=1, source_target_pairs={{0,6},{2,4},{4,2},{6,0},{1,7},{3,5},{5,3},{7,1},{8,14},{10,12},{12... | collective-permute-start | bytes 98312 | tf_op jit(solution)/shard_map/ppermute | solution.py:259
  45.8 1.4 %collective-permute-done.16 = bf16[2,64,128]{2,1,0:T(8,128)(2,1)S(1)} collective-permute-done((bf16[2,64,128]{2,1,0:T(8,128)(2,1)S(1)}, bf16[2,64,128]{2,1,0:T(8,128)(2,1)S(1)}, u32[]{:S(2)}, u32[]{:S(2)}) %collective-permute-start.16) | collective-permute-done | bytes 32800 | tf_op jit(solution)/shard_map/ppermute | solution.py:259
  47.2 2.0 %collective-permute-done.15 = bf16[2,64,128]{2,1,0:T(8,128)(2,1)S(1)} collective-permute-done((bf16[2,64,128]{2,1,0:T(8,128)(2,1)S(1)}, bf16[2,64,128]{2,1,0:T(8,128)(2,1)S(1)}, u32[]{:S(2)}, u32[]{:S(2)}) %collective-permute-start.15) | collective-permute-done | bytes 32800 | tf_op jit(solution)/shard_map/ppermute | solution.py:259
  49.3 0.9 %collective-permute-start.19 = (bf16[2,64,128]{2,1,0:T(8,128)(2,1)S(1)}, bf16[2,64,128]{2,1,0:T(8,128)(2,1)S(1)}, u32[]{:S(2)}, u32[]{:S(2)}) collective-permute-start(bf16[2,64,128]{2,1,0:T(8,128)(2,1)S(1)} %fusion), channel_id=1, source_target_pairs={{0,24},{8,16},{16,8},{24,0},{1,25},{9,17},{17,9},{25,1},{2,26},{10... | collective-permute-start | bytes 98312 | tf_op jit(solution)/shard_map/ppermute | solution.py:259
  50.2 2.6 %collective-permute-start.18 = (bf16[2,64,128]{2,1,0:T(8,128)(2,1)S(1)}, bf16[2,64,128]{2,1,0:T(8,128)(2,1)S(1)}, u32[]{:S(2)}, u32[]{:S(2)}) collective-permute-start(bf16[2,64,128]{2,1,0:T(8,128)(2,1)S(1)} %fusion), channel_id=1, source_target_pairs={{0,8},{8,0},{16,24},{24,16},{1,9},{9,1},{17,25},{25,17},{2,10},{10... | collective-permute-start | bytes 98312 | tf_op jit(solution)/shard_map/ppermute | solution.py:259
  52.8 2.0 %collective-permute-done.20 = bf16[2,64,128]{2,1,0:T(8,128)(2,1)S(1)} collective-permute-done((bf16[2,64,128]{2,1,0:T(8,128)(2,1)S(1)}, bf16[2,64,128]{2,1,0:T(8,128)(2,1)S(1)}, u32[]{:S(2)}, u32[]{:S(2)}) %collective-permute-start.20) | collective-permute-done | bytes 32800 | tf_op jit(solution)/shard_map/ppermute | solution.py:259
  55.0 4.1 %collective-permute-start.23 = (bf16[2,64,128]{2,1,0:T(8,128)(2,1)S(1)}, bf16[2,64,128]{2,1,0:T(8,128)(2,1)S(1)}, u32[]{:S(2)}, u32[]{:S(2)}) collective-permute-start(bf16[2,64,128]{2,1,0:T(8,128)(2,1)S(1)} %get-tuple-element.58), channel_id=1, source_target_pairs={{0,128},{32,160},{64,192},{96,224},{128,0},{160,32},{192,64},{224,... | collective-permute-start | bytes 98312 | tf_op jit(solution)/shard_map/ppermute | solution.py:259
  59.0 1.4 %collective-permute-start.22 = (bf16[2,64,128]{2,1,0:T(8,128)(2,1)S(1)}, bf16[2,64,128]{2,1,0:T(8,128)(2,1)S(1)}, u32[]{:S(2)}, u32[]{:S(2)}) collective-permute-start(bf16[2,64,128]{2,1,0:T(8,128)(2,1)S(1)} %get-tuple-element.58), channel_id=1, source_target_pairs={{0,192},{32,224},{64,128},{96,160},{128,64},{160,96},{192,0},{224,... | collective-permute-start | bytes 98312 | tf_op jit(solution)/shard_map/ppermute | solution.py:259
  60.4 1.1 %collective-permute-start.21 = (bf16[2,64,128]{2,1,0:T(8,128)(2,1)S(1)}, bf16[2,64,128]{2,1,0:T(8,128)(2,1)S(1)}, u32[]{:S(2)}, u32[]{:S(2)}) collective-permute-start(bf16[2,64,128]{2,1,0:T(8,128)(2,1)S(1)} %get-tuple-element.58), channel_id=1, source_target_pairs={{0,64},{32,96},{64,0},{96,32},{128,192},{160,224},{192,128},{224,1... | collective-permute-start | bytes 98312 | tf_op jit(solution)/shard_map/ppermute | solution.py:259
  61.5 2.2 %last.1.v3 = f32[8,64,256]{2,1,0:T(8,128)S(1)} custom-call(s32[8,8]{1,0:T(8,128)S(1)} %get-tuple-element.31.refs_0_.cols, s32[8]{0:T(128)S(1)} %get-tuple-element.32.refs_1_.live, bf16[8,64,256]{2,1,0:T(8,128)(2,1)S(1)} %get-tuple-element.49.x, bf16[4,64,256]{2,1,0:T(8,128)(2,1)S(1)} %collective-permute-done.8.rb, ...), custom_call_target="tpu_custom_call" | custom-call | flops 536870912 | bytes 8388608 | tf_op jit(solution)/shard_map/last/pallas_call | solution.py:362
  63.8 1.4 %collective-permute-done.22 = bf16[2,64,128]{2,1,0:T(8,128)(2,1)S(1)} collective-permute-done((bf16[2,64,128]{2,1,0:T(8,128)(2,1)S(1)}, bf16[2,64,128]{2,1,0:T(8,128)(2,1)S(1)}, u32[]{:S(2)}, u32[]{:S(2)}) %collective-permute-start.22) | collective-permute-done | bytes 32800 | tf_op jit(solution)/shard_map/ppermute | solution.py:259
  65.6 2.1 %final.1 = (f32[4,8,64,256]{3,2,1,0:T(8,128)}, f32[4,4,64]{2,1,0:T(4,128)}) custom-call(f32[8,64,256]{2,1,0:T(8,128)S(1)} %get-tuple-element.30.start.v0, f32[8,64,256]{2,1,0:T(8,128)S(1)} %get-tuple-element.40.v.v1, f32[8,64,256]{2,1,0:T(8,128)S(1)} %get-tuple-element.48.v.v2, f32[8,64,256]{2,1,0:T(8,128)S(1)} %last.1.v3, f32[2,64,128]{2,1,0:T(8,128)S(1)} %add_add_fusion.w), custom_call_target="tpu_custom_call" | custom-call | flops 4194304 | bytes 4194304 | tf_op jit(solution)/shard_map/final/pallas_call | solution.py:372
  (33 shorter events, 3.1 us)
Async XLA Ops:
  1.8 11.8 %collective-permute-start = (bf16[4,64,256]{2,1,0:T(8,128)(2,1)S(1)}, bf16[4,64,256]{2,1,0:T(8,128)(2,1)S(1)}, u32[]{:S(2)}, u32[]{:S(2)}) collective-permute-start(bf16[4,64,256]{2,1,0:T(8,128)(2,1)S(1)} %get-tuple-element.35), channel_id=1, source_target_pairs={{1,2},{2,1},{3,4},{4,3},{5,6},{6,5},{7,8},{8,7},{9,10},{10,9},{11,... | collective-permute-start | bytes 393224 | tf_op jit(solution)/shard_map/ppermute | solution.py:246
  1.9 11.7 %collective-permute-start.1 = (bf16[4,64,256]{2,1,0:T(8,128)(2,1)S(1)}, bf16[4,64,256]{2,1,0:T(8,128)(2,1)S(1)}, u32[]{:S(2)}, u32[]{:S(2)}) collective-permute-start(bf16[4,64,256]{2,1,0:T(8,128)(2,1)S(1)} %get-tuple-element.36), channel_id=1, source_target_pairs={{0,32},{32,0},{64,96},{96,64},{128,160},{160,128},{192,224},{224,1... | collective-permute-start | bytes 393224 | tf_op jit(solution)/shard_map/ppermute | solution.py:244
  3.9 9.7 %collective-permute-start.2 = (bf16[4,64,256]{2,1,0:T(8,128)(2,1)S(1)}, bf16[4,64,256]{2,1,0:T(8,128)(2,1)S(1)}, u32[]{:S(2)}, u32[]{:S(2)}) collective-permute-start(bf16[4,64,256]{2,1,0:T(8,128)(2,1)S(1)} %get-tuple-element.37), channel_id=1, source_target_pairs={{32,64},{64,32},{96,128},{128,96},{160,192},{192,160},{224,0},{0,2... | collective-permute-start | bytes 393224 | tf_op jit(solution)/shard_map/ppermute | solution.py:243
  8.8 4.7 %collective-permute-start.3 = (bf16[4,64,256]{2,1,0:T(8,128)(2,1)S(1)}, bf16[4,64,256]{2,1,0:T(8,128)(2,1)S(1)}, u32[]{:S(2)}, u32[]{:S(2)}) collective-permute-start(bf16[4,64,256]{2,1,0:T(8,128)(2,1)S(1)} %get-tuple-element.38), channel_id=1, source_target_pairs={{0,1},{1,0},{2,3},{3,2},{4,5},{5,4},{6,7},{7,6},{8,9},{9,8},{10,11... | collective-permute-start | bytes 393224 | tf_op jit(solution)/shard_map/ppermute | solution.py:245
  15.9 8.6 %collective-permute-start.4 = (bf16[4,64,256]{2,1,0:T(8,128)(2,1)S(1)}, bf16[4,64,256]{2,1,0:T(8,128)(2,1)S(1)}, u32[]{:S(2)}, u32[]{:S(2)}) collective-permute-start(bf16[4,64,256]{2,1,0:T(8,128)(2,1)S(1)} %get-tuple-element.42), channel_id=1, source_target_pairs={{1,2},{2,1},{3,4},{4,3},{5,6},{6,5},{7,8},{8,7},{9,10},{10,9},{11,... | collective-permute-start | bytes 393224 | tf_op jit(solution)/shard_map/ppermute | solution.py:246
  20.0 5.0 %collective-permute-start.5 = (bf16[4,64,256]{2,1,0:T(8,128)(2,1)S(1)}, bf16[4,64,256]{2,1,0:T(8,128)(2,1)S(1)}, u32[]{:S(2)}, u32[]{:S(2)}) collective-permute-start(bf16[4,64,256]{2,1,0:T(8,128)(2,1)S(1)} %get-tuple-element.43), channel_id=1, source_target_pairs={{0,32},{32,0},{64,96},{96,64},{128,160},{160,128},{192,224},{224,1... | collective-permute-start | bytes 393224 | tf_op jit(solution)/shard_map/ppermute | solution.py:244
  20.1 6.2 %collective-permute-start.6 = (bf16[4,64,256]{2,1,0:T(8,128)(2,1)S(1)}, bf16[4,64,256]{2,1,0:T(8,128)(2,1)S(1)}, u32[]{:S(2)}, u32[]{:S(2)}) collective-permute-start(bf16[4,64,256]{2,1,0:T(8,128)(2,1)S(1)} %get-tuple-element.44), channel_id=1, source_target_pairs={{32,64},{64,32},{96,128},{128,96},{160,192},{192,160},{224,0},{0,2... | collective-permute-start | bytes 393224 | tf_op jit(solution)/shard_map/ppermute | solution.py:243
  22.1 4.2 %collective-permute-start.7 = (bf16[4,64,256]{2,1,0:T(8,128)(2,1)S(1)}, bf16[4,64,256]{2,1,0:T(8,128)(2,1)S(1)}, u32[]{:S(2)}, u32[]{:S(2)}) collective-permute-start(bf16[4,64,256]{2,1,0:T(8,128)(2,1)S(1)} %get-tuple-element.45), channel_id=1, source_target_pairs={{0,1},{1,0},{2,3},{3,2},{4,5},{5,4},{6,7},{7,6},{8,9},{9,8},{10,11... | collective-permute-start | bytes 393224 | tf_op jit(solution)/shard_map/ppermute | solution.py:245
  28.5 5.1 %collective-permute-start.8 = (bf16[4,64,256]{2,1,0:T(8,128)(2,1)S(1)}, bf16[4,64,256]{2,1,0:T(8,128)(2,1)S(1)}, u32[]{:S(2)}, u32[]{:S(2)}) collective-permute-start(bf16[4,64,256]{2,1,0:T(8,128)(2,1)S(1)} %get-tuple-element.50), channel_id=1, source_target_pairs={{1,2},{2,1},{3,4},{4,3},{5,6},{6,5},{7,8},{8,7},{9,10},{10,9},{11,... | collective-permute-start | bytes 393224 | tf_op jit(solution)/shard_map/ppermute | solution.py:246
  28.9 5.0 %collective-permute-start.9 = (bf16[4,64,256]{2,1,0:T(8,128)(2,1)S(1)}, bf16[4,64,256]{2,1,0:T(8,128)(2,1)S(1)}, u32[]{:S(2)}, u32[]{:S(2)}) collective-permute-start(bf16[4,64,256]{2,1,0:T(8,128)(2,1)S(1)} %get-tuple-element.51), channel_id=1, source_target_pairs={{0,32},{32,0},{64,96},{96,64},{128,160},{160,128},{192,224},{224,1... | collective-permute-start | bytes 393224 | tf_op jit(solution)/shard_map/ppermute | solution.py:244
  29.5 6.2 %collective-permute-start.10 = (bf16[4,64,256]{2,1,0:T(8,128)(2,1)S(1)}, bf16[4,64,256]{2,1,0:T(8,128)(2,1)S(1)}, u32[]{:S(2)}, u32[]{:S(2)}) collective-permute-start(bf16[4,64,256]{2,1,0:T(8,128)(2,1)S(1)} %get-tuple-element.52), channel_id=1, source_target_pairs={{32,64},{64,32},{96,128},{128,96},{160,192},{192,160},{224,0},{0,2... | collective-permute-start | bytes 393224 | tf_op jit(solution)/shard_map/ppermute | solution.py:243
  30.9 4.8 %collective-permute-start.11 = (bf16[4,64,256]{2,1,0:T(8,128)(2,1)S(1)}, bf16[4,64,256]{2,1,0:T(8,128)(2,1)S(1)}, u32[]{:S(2)}, u32[]{:S(2)}) collective-permute-start(bf16[4,64,256]{2,1,0:T(8,128)(2,1)S(1)} %get-tuple-element.53), channel_id=1, source_target_pairs={{0,1},{1,0},{2,3},{3,2},{4,5},{5,4},{6,7},{7,6},{8,9},{9,8},{10,11... | collective-permute-start | bytes 393224 | tf_op jit(solution)/shard_map/ppermute | solution.py:245
  36.2 4.0 %collective-permute-start.14 = (bf16[2,64,128]{2,1,0:T(8,128)(2,1)S(1)}, bf16[2,64,128]{2,1,0:T(8,128)(2,1)S(1)}, u32[]{:S(2)}, u32[]{:S(2)}) collective-permute-start(bf16[2,64,128]{2,1,0:T(8,128)(2,1)S(1)} %reduce-precision_convert_fusion), channel_id=1, source_target_pairs={{0,32},{1,33},{32,0},{33,1},{64,96},{65,97},{96,64},{97,65},{128,1... | collective-permute-start | bytes 98312 | tf_op jit(solution)/shard_map/ppermute | solution.py:259
  36.5 3.8 %collective-permute-start.13 = (bf16[2,64,128]{2,1,0:T(8,128)(2,1)S(1)}, bf16[2,64,128]{2,1,0:T(8,128)(2,1)S(1)}, u32[]{:S(2)}, u32[]{:S(2)}) collective-permute-start(bf16[2,64,128]{2,1,0:T(8,128)(2,1)S(1)} %reduce-precision_convert_fusion), channel_id=1, source_target_pairs={{0,33},{1,32},{32,1},{33,0},{64,97},{65,96},{96,65},{97,64},{128,1... | collective-permute-start | bytes 98312 | tf_op jit(solution)/shard_map/ppermute | solution.py:259
  36.5 3.8 %collective-permute-start.12 = (bf16[2,64,128]{2,1,0:T(8,128)(2,1)S(1)}, bf16[2,64,128]{2,1,0:T(8,128)(2,1)S(1)}, u32[]{:S(2)}, u32[]{:S(2)}) collective-permute-start(bf16[2,64,128]{2,1,0:T(8,128)(2,1)S(1)} %reduce-precision_convert_fusion), channel_id=1, source_target_pairs={{0,1},{1,0},{32,33},{33,32},{64,65},{65,64},{96,97},{97,96},{128,1... | collective-permute-start | bytes 98312 | tf_op jit(solution)/shard_map/ppermute | solution.py:259
  40.3 5.5 %collective-permute-start.17 = (bf16[2,64,128]{2,1,0:T(8,128)(2,1)S(1)}, bf16[2,64,128]{2,1,0:T(8,128)(2,1)S(1)}, u32[]{:S(2)}, u32[]{:S(2)}) collective-permute-start(bf16[2,64,128]{2,1,0:T(8,128)(2,1)S(1)} %get-tuple-element.60), channel_id=1, source_target_pairs={{0,4},{2,6},{4,0},{6,2},{1,5},{3,7},{5,1},{7,3},{8,12},{10,14},{12... | collective-permute-start | bytes 98312 | tf_op jit(solution)/shard_map/ppermute | solution.py:259
  41.1 6.1 %collective-permute-start.16 = (bf16[2,64,128]{2,1,0:T(8,128)(2,1)S(1)}, bf16[2,64,128]{2,1,0:T(8,128)(2,1)S(1)}, u32[]{:S(2)}, u32[]{:S(2)}) collective-permute-start(bf16[2,64,128]{2,1,0:T(8,128)(2,1)S(1)} %get-tuple-element.60), channel_id=1, source_target_pairs={{0,6},{2,4},{4,2},{6,0},{1,7},{3,5},{5,3},{7,1},{8,14},{10,12},{12... | collective-permute-start | bytes 98312 | tf_op jit(solution)/shard_map/ppermute | solution.py:259
  45.3 3.9 %collective-permute-start.15 = (bf16[2,64,128]{2,1,0:T(8,128)(2,1)S(1)}, bf16[2,64,128]{2,1,0:T(8,128)(2,1)S(1)}, u32[]{:S(2)}, u32[]{:S(2)}) collective-permute-start(bf16[2,64,128]{2,1,0:T(8,128)(2,1)S(1)} %get-tuple-element.60), channel_id=1, source_target_pairs={{0,2},{2,0},{4,6},{6,4},{1,3},{3,1},{5,7},{7,5},{8,10},{10,8},{12,... | collective-permute-start | bytes 98312 | tf_op jit(solution)/shard_map/ppermute | solution.py:259
  49.2 5.6 %collective-permute-start.20 = (bf16[2,64,128]{2,1,0:T(8,128)(2,1)S(1)}, bf16[2,64,128]{2,1,0:T(8,128)(2,1)S(1)}, u32[]{:S(2)}, u32[]{:S(2)}) collective-permute-start(bf16[2,64,128]{2,1,0:T(8,128)(2,1)S(1)} %fusion), channel_id=1, source_target_pairs={{0,16},{8,24},{16,0},{24,8},{1,17},{9,25},{17,1},{25,9},{2,18},{10... | collective-permute-start | bytes 98312 | tf_op jit(solution)/shard_map/ppermute | solution.py:259
  49.3 5.6 %collective-permute-start.19 = (bf16[2,64,128]{2,1,0:T(8,128)(2,1)S(1)}, bf16[2,64,128]{2,1,0:T(8,128)(2,1)S(1)}, u32[]{:S(2)}, u32[]{:S(2)}) collective-permute-start(bf16[2,64,128]{2,1,0:T(8,128)(2,1)S(1)} %fusion), channel_id=1, source_target_pairs={{0,24},{8,16},{16,8},{24,0},{1,25},{9,17},{17,9},{25,1},{2,26},{10... | collective-permute-start | bytes 98312 | tf_op jit(solution)/shard_map/ppermute | solution.py:259
  50.2 4.7 %collective-permute-start.18 = (bf16[2,64,128]{2,1,0:T(8,128)(2,1)S(1)}, bf16[2,64,128]{2,1,0:T(8,128)(2,1)S(1)}, u32[]{:S(2)}, u32[]{:S(2)}) collective-permute-start(bf16[2,64,128]{2,1,0:T(8,128)(2,1)S(1)} %fusion), channel_id=1, source_target_pairs={{0,8},{8,0},{16,24},{24,16},{1,9},{9,1},{17,25},{25,17},{2,10},{10... | collective-permute-start | bytes 98312 | tf_op jit(solution)/shard_map/ppermute | solution.py:259
  55.0 8.8 %collective-permute-start.23 = (bf16[2,64,128]{2,1,0:T(8,128)(2,1)S(1)}, bf16[2,64,128]{2,1,0:T(8,128)(2,1)S(1)}, u32[]{:S(2)}, u32[]{:S(2)}) collective-permute-start(bf16[2,64,128]{2,1,0:T(8,128)(2,1)S(1)} %get-tuple-element.58), channel_id=1, source_target_pairs={{0,128},{32,160},{64,192},{96,224},{128,0},{160,32},{192,64},{224,... | collective-permute-start | bytes 98312 | tf_op jit(solution)/shard_map/ppermute | solution.py:259
  59.0 6.1 %collective-permute-start.22 = (bf16[2,64,128]{2,1,0:T(8,128)(2,1)S(1)}, bf16[2,64,128]{2,1,0:T(8,128)(2,1)S(1)}, u32[]{:S(2)}, u32[]{:S(2)}) collective-permute-start(bf16[2,64,128]{2,1,0:T(8,128)(2,1)S(1)} %get-tuple-element.58), channel_id=1, source_target_pairs={{0,192},{32,224},{64,128},{96,160},{128,64},{160,96},{192,0},{224,... | collective-permute-start | bytes 98312 | tf_op jit(solution)/shard_map/ppermute | solution.py:259
  60.4 5.2 %collective-permute-start.21 = (bf16[2,64,128]{2,1,0:T(8,128)(2,1)S(1)}, bf16[2,64,128]{2,1,0:T(8,128)(2,1)S(1)}, u32[]{:S(2)}, u32[]{:S(2)}) collective-permute-start(bf16[2,64,128]{2,1,0:T(8,128)(2,1)S(1)} %get-tuple-element.58), channel_id=1, source_target_pairs={{0,64},{32,96},{64,0},{96,32},{128,192},{160,224},{192,128},{224,1... | collective-permute-start | bytes 98312 | tf_op jit(solution)/shard_map/ppermute | solution.py:259
